TPU v7x, 16 devices: a 4x2x1 block of a 4x4x8 slice. The times are simulated.
16 devices in a mesh: dp: 2 (over y, z), tp: 8 (over x, core).
Axes of the slice: x: 4, y: 2, z: 1, core: 2. Of those that a mesh axis runs over, the one named last changes fastest.
The devices are a block of a 4x4x8 slice.
Arguments:
- ids: int32 [4, 256], P('dp'), parts along dimension 0
- emb: bfloat16 [65536, 2048], P('tp')
- g: bfloat16 [2048], replicated
- w: bfloat16 [2048, 3072], P(None, 'tp')
- du: bfloat16 [4, 256, 3072], P('dp', None, 'tp'), parts along dimension 0
- dres: bfloat16 [4, 256, 2048], P('dp', 'tp'), parts along dimension 0
Outputs:
- output 1: bfloat16 [4, 256, 3072], P('dp', None, 'tp'), parts along dimension 0
- output 2: bfloat16 [4, 256, 2048], P('dp', 'tp'), parts along dimension 0
- output 3: float32 [131072, 2048], P(('dp', 'tp')), parts along dimension 0
- output 4: float32 [2048, 6144], P(None, ('dp', 'tp')), parts along dimension 1
- output 5: float32 [4096], P('dp'), parts along dimension 0
There are 2 independent parts. A program takes and returns all parts, laid end to end along the dimension named above; an argument that names none is the same for every part.
All inputs are finite; a program needn't handle non-finite values.
Results may differ from a plain program's by a relative error of at most 0.001.
Values are sent between devices in bfloat16 or wider.
A program may use at most 768 MiB of HBM per device.

v0:
```python
import jax
import jax.numpy as jnp
from jax import lax
from jax.sharding import PartitionSpec as P

EPS = 1e-6


def solution(mesh):
    groups = mesh.shape["tp"]

    def local(ids, emb, g, w, du, dres):
        r = lax.axis_index("tp")
        t = ids.shape[1]
        vl, d = emb.shape
        tl = t // groups
        lo = r * vl
        start = r * tl
        gf = g.astype(jnp.float32)
        cols = lax.broadcasted_iota(jnp.int32, (1, vl), 1)

        def micro(dg, inp):
            idm, dum, drm = inp
            oh = ((idm - lo)[:, None] == cols).astype(jnp.bfloat16)
            xp = jnp.dot(oh, emb, preferred_element_type=jnp.float32).astype(jnp.bfloat16)
            x = lax.psum(xp, "tp")
            xf = x.astype(jnp.float32)
            rs = lax.rsqrt(jnp.mean(xf * xf, axis=-1, keepdims=True) + EPS)
            nh = xf * rs
            n = (nh * gf).astype(jnp.bfloat16)
            u = jnp.dot(n, w, preferred_element_type=jnp.float32).astype(jnp.bfloat16)
            pdn = jnp.einsum("tf,df->td", dum, w, preferred_element_type=jnp.float32).astype(jnp.bfloat16)
            recv = lax.all_to_all(pdn, "tp", 0, 0, tiled=True).reshape(groups, tl, d)
            dn = jnp.sum(recv.astype(jnp.float32), axis=0)
            nhs = lax.dynamic_slice_in_dim(nh, start, tl, 0)
            rss = lax.dynamic_slice_in_dim(rs, start, tl, 0)
            gdn = gf * dn
            dxn = rss * (gdn - nhs * jnp.mean(nhs * gdn, axis=-1, keepdims=True))
            dx = (drm.astype(jnp.float32) + dxn).astype(jnp.bfloat16)
            dxa = lax.all_gather(dx, "tp", axis=0, tiled=True)
            dg = dg + jnp.sum(dn * nhs, axis=0)
            return dg, (u, lax.dynamic_slice_in_dim(x, start, tl, 0), n, dxa)

        dg, (u, xo, ns, dxs) = lax.scan(micro, jnp.zeros((d,), jnp.float32), (ids, du, dres))
        loc = (ids - lo).reshape(-1)
        oh = (lax.broadcasted_iota(jnp.int32, (vl, loc.shape[0]), 0) == loc[None, :]).astype(jnp.bfloat16)
        de = jnp.dot(oh, dxs.reshape(-1, d), preferred_element_type=jnp.float32)
        dw = jnp.einsum("ktd,ktf->df", ns, du, preferred_element_type=jnp.float32)
        dg = lax.psum(dg, "tp")
        return u, xo, de, dw, dg

    return jax.shard_map(
        local,
        mesh=mesh,
        in_specs=(P("dp", None), P("tp", None), P(None), P(None, "tp"), P("dp", None, "tp"), P("dp", "tp", None)),
        out_specs=(P("dp", None, "tp"), P("dp", "tp", None), P(("dp", "tp"), None), P(None, ("dp", "tp")), P("dp")),
        check_vma=False,
    )
```

profile of v0, /device:TPU:112, one launch (start us, length us, event | category | flops | bytes accessed | tf_op | source)
XLA Modules:
  0.0 270.6 jit_solution(13328641487316624226)
XLA Ops:
  7.2 0.7 convert_element_type.48
  7.9 209.6 %while.21 = (s32[]{:T(128)}, f32[2048]{0:T(1024)S(1)}, bf16[2,256,384]{2,1,0:T(8,128)(2,1)}, bf16[2,32,2048]{2,1,0:T(8,128)(2,1)S(1)}, bf16[2,256,2048]{2,1,0:T(...) while((s32[]{:T(128)}, f32[2048]{0:T(1024)S(1)}, ...), condition=%wide.region_6.7_spmd.clone, body=%wide.region_0.6_spmd.clone.sunk | while | flops 9407596544 | bytes 94447992 | solution.py:44
  7.9 0.7 fusion.34
  8.6 15.4 %fusion.35 = bf16[256,2048]{1,0:T(8,128)(2,1)} fusion(bf16[8192,2048]{1,0:T(8,128)(2,1)} %get-tuple-element.395, s32[256]{0:T(256)S(1)} %bitcast.52), kind=kOutput, calls=%fused_computation.6.clone.1 | convolution fusion | flops 8592556032 | bytes 34604032 | tf_op jit(solution)/shard_map/while/body/eval_jaxpr/dot_general | solution.py:25
  24.1 1.7 convolution_convert_fusion.3
  25.9 5.3 %all-to-all-start = ((bf16[8,32,2048]{2,1,0:T(8,128)(2,1)}), bf16[8,32,2048]{2,1,0:T(8,128)(2,1)S(1)}, u32[]{:S(2)}, u32[]{:S(2)}) async-start(bf16[8,32,2048]{2,1,0:T(8,128)(2,1)} %bitcast.50), calls=%async_computation | async-start | bytes 2097152 | tf_op jit(solution)/shard_map/while/body/eval_jaxpr/all_to_all | solution.py:33
  31.2 54.2 %all-reduce.2.cloned.1.call-done = bf16[256,2048]{1,0:T(8,128)(2,1)} async-done(((bf16[256,2048]{1,0:T(8,128)(2,1)}), bf16[256,2048]{1,0:T(8,128)(2,1)}) %all-reduce.2.cloned.1.call-update) | async-done | bytes 1048592 | tf_op jit(solution)/shard_map/while/body/eval_jaxpr/psum | solution.py:26
  85.4 1.5 fusion.36
  87.0 2.8 %convert_multiply_fusion.4 = f32[256,2048]{1,0:T(8,128)} fusion(bf16[256,2048]{1,0:T(8,128)(2,1)} %all-reduce.2.cloned.1.call-done, f32[256]{0:T(256)S(1)} %add_rsqrt_fusion.2), kind=kLoop, calls=%fused_computation.4.clone.3 | loop fusion | flops 1048576 | bytes 3146752 | tf_op jit(solution)/shard_map/while/body/eval_jaxpr/mul | solution.py:29
  90.0 1.2 multiply_reduce_fusion.3
  91.2 1.7 fusion.38
  93.1 3.0 %fusion.37 = bf16[2,256,384]{2,1,0:T(8,128)(2,1)} fusion(bf16[2,256,384]{2,1,0:T(8,128)(2,1)} %get-tuple-element.371, s32[]{:T(128)S(6)} %copy.25, bf16[2048,384]{1,0:T(8,128)(2,1)} %get-tuple-element.392, f32[2048]{0:T(1024)S(1)} %get-tuple-element.397, bf16[256,2048]{1,0:T(8,128)(2,1)S(1)} %copy-done, f32[256]{0:T(256)S(1)} %add_rsqrt_fusion.2), kind=kOutput, calls=%fused_computation.13.clone.1 | convolution fusion | flops 404848640 | bytes 2827268 | tf_op jit(solution)/shard_map/while/body/eval_jaxpr/dot_general | solution.py:31
  96.1 0.3 bitcast_dynamic-update-slice_fusion.7
  96.4 14.9 %all-gather.2.cloned.1.call-done = bf16[256,2048]{1,0:T(8,128)(2,1)} async-done(((bf16[32,2048]{1,0:T(8,128)(2,1)}), bf16[256,2048]{1,0:T(8,128)(2,1)}) %all-gather.2.cloned.1.call-update) | async-done | bytes 1048592 | tf_op jit(solution)/shard_map/while/body/eval_jaxpr/all_gather | solution.py:40
  111.3 2.3 bitcast_dynamic-update-slice_fusion.8
  113.7 0.7 fusion.34
  114.4 15.4 %fusion.35 = bf16[256,2048]{1,0:T(8,128)(2,1)} fusion(bf16[8192,2048]{1,0:T(8,128)(2,1)} %get-tuple-element.395, s32[256]{0:T(256)S(1)} %bitcast.52), kind=kOutput, calls=%fused_computation.6.clone.1 | convolution fusion | flops 8592556032 | bytes 34604032 | tf_op jit(solution)/shard_map/while/body/eval_jaxpr/dot_general | solution.py:25
  129.9 1.7 convolution_convert_fusion.3
  131.6 3.8 %all-to-all-start = ((bf16[8,32,2048]{2,1,0:T(8,128)(2,1)}), bf16[8,32,2048]{2,1,0:T(8,128)(2,1)S(1)}, u32[]{:S(2)}, u32[]{:S(2)}) async-start(bf16[8,32,2048]{2,1,0:T(8,128)(2,1)} %bitcast.50), calls=%async_computation | async-start | bytes 2097152 | tf_op jit(solution)/shard_map/while/body/eval_jaxpr/all_to_all | solution.py:33
  135.5 53.8 %all-reduce.2.cloned.1.call-done = bf16[256,2048]{1,0:T(8,128)(2,1)} async-done(((bf16[256,2048]{1,0:T(8,128)(2,1)}), bf16[256,2048]{1,0:T(8,128)(2,1)}) %all-reduce.2.cloned.1.call-update) | async-done | bytes 1048592 | tf_op jit(solution)/shard_map/while/body/eval_jaxpr/psum | solution.py:26
  189.3 1.5 fusion.36
  190.9 2.8 %convert_multiply_fusion.4 = f32[256,2048]{1,0:T(8,128)} fusion(bf16[256,2048]{1,0:T(8,128)(2,1)} %all-reduce.2.cloned.1.call-done, f32[256]{0:T(256)S(1)} %add_rsqrt_fusion.2), kind=kLoop, calls=%fused_computation.4.clone.3 | loop fusion | flops 1048576 | bytes 3146752 | tf_op jit(solution)/shard_map/while/body/eval_jaxpr/mul | solution.py:29
  193.8 1.2 multiply_reduce_fusion.3
  195.1 1.7 fusion.38
  196.9 3.0 %fusion.37 = bf16[2,256,384]{2,1,0:T(8,128)(2,1)} fusion(bf16[2,256,384]{2,1,0:T(8,128)(2,1)} %get-tuple-element.371, s32[]{:T(128)S(6)} %copy.25, bf16[2048,384]{1,0:T(8,128)(2,1)} %get-tuple-element.392, f32[2048]{0:T(1024)S(1)} %get-tuple-element.397, bf16[256,2048]{1,0:T(8,128)(2,1)S(1)} %copy-done, f32[256]{0:T(256)S(1)} %add_rsqrt_fusion.2), kind=kOutput, calls=%fused_computation.13.clone.1 | convolution fusion | flops 404848640 | bytes 2827268 | tf_op jit(solution)/shard_map/while/body/eval_jaxpr/dot_general | solution.py:31
  199.9 0.3 bitcast_dynamic-update-slice_fusion.7
  200.3 14.9 %all-gather.2.cloned.1.call-done = bf16[256,2048]{1,0:T(8,128)(2,1)} async-done(((bf16[32,2048]{1,0:T(8,128)(2,1)}), bf16[256,2048]{1,0:T(8,128)(2,1)}) %all-gather.2.cloned.1.call-update) | async-done | bytes 1048592 | tf_op jit(solution)/shard_map/while/body/eval_jaxpr/all_gather | solution.py:40
  215.2 2.4 bitcast_dynamic-update-slice_fusion.8
  217.6 0.7 subtract_bitcast_fusion
  218.3 28.6 %fusion.13 = f32[8192,2048]{1,0:T(8,128)} fusion(bf16[512,2048]{1,0:T(8,128)(2,1)} %bitcast.54, s32[512]{0:T(512)S(1)} %bitcast.53), kind=kOutput, calls=%fused_computation.30 | convolution fusion | flops 17184063488 | bytes 69208064 | tf_op jit(solution)/shard_map/dot_general | solution.py:47
  246.9 3.0 %convolution_bitcast_fusion = f32[2048,384]{1,0:T(8,128)} fusion(bf16[2,256,2048]{2,1,0:T(8,128)(2,1)S(1)} %copy-done.7, bf16[2,256,384]{2,1,0:T(8,128)(2,1)S(1)} %copy-done.3), kind=kOutput, calls=%fused_computation.32 | convolution fusion | flops 805306368 | bytes 5636096 | tf_op jit(solution)/shard_map/ktd,ktf->df/dot_general | solution.py:48
  249.9 14.2 %psum.16 = f32[2048]{0:T(1024)} all-reduce(f32[2048]{0:T(1024)S(1)} %get-tuple-element.186), channel_id=1, replica_groups=mesh['dp'=2,'tp'=8] {'tp'}, use_global_device_ids=true, to_apply=%region_7.8 | all-reduce | flops 2048 | bytes 16384 | tf_op jit(solution)/shard_map/psum | solution.py:49
  (58 shorter events, 0.9 us)
Async XLA Ops:
  7.9 77.5 %all-reduce.2.cloned.1.call-start = ((), (), s32[]{:S(2)}) async-start(), calls=%async_computation.1 | async-start | bytes 2097152 | tf_op jit(solution)/shard_map/while/body/eval_jaxpr/psum | solution.py:26
  8.6 15.5 %copy-start.1 = (bf16[2048,384]{1,0:T(8,128)(2,1)S(1)}, bf16[2048,384]{1,0:T(8,128)(2,1)}, u32[]{:S(2)}) copy-start(bf16[2048,384]{1,0:T(8,128)(2,1)} %get-tuple-element.392) | copy-start | bytes 4718596 | tf_op jit(solution)/shard_map/while
  8.6 15.5 %copy-start.2 = (bf16[2,256,384]{2,1,0:T(8,128)(2,1)S(1)}, bf16[2,256,384]{2,1,0:T(8,128)(2,1)}, u32[]{:S(2)}) copy-start(bf16[2,256,384]{2,1,0:T(8,128)(2,1)} %get-tuple-element.391) | copy-start | bytes 1179652 | tf_op jit(solution)/shard_map/while
  25.9 64.0 %all-to-all-start = ((bf16[8,32,2048]{2,1,0:T(8,128)(2,1)}), bf16[8,32,2048]{2,1,0:T(8,128)(2,1)S(1)}, u32[]{:S(2)}, u32[]{:S(2)}) async-start(bf16[8,32,2048]{2,1,0:T(8,128)(2,1)} %bitcast.50), calls=%async_computation | async-start | bytes 2097152 | tf_op jit(solution)/shard_map/while/body/eval_jaxpr/all_to_all | solution.py:33
  31.2 80.2 %all-gather.2.cloned.1.call-start = ((), (), s32[]{:S(2)}) async-start(), calls=%async_computation.2 | async-start | bytes 1179648 | tf_op jit(solution)/shard_map/while/body/eval_jaxpr/all_gather | solution.py:40
  87.0 4.2 %copy-start.4 = (bf16[2,32,2048]{2,1,0:T(8,128)(2,1)S(1)}, bf16[2,32,2048]{2,1,0:T(8,128)(2,1)}, u32[]{:S(2)}) copy-start(bf16[2,32,2048]{2,1,0:T(8,128)(2,1)} %get-tuple-element.398) | copy-start | bytes 786436 | tf_op jit(solution)/shard_map/while
  89.8 3.2 %copy-start = (bf16[256,2048]{1,0:T(8,128)(2,1)S(1)}, bf16[256,2048]{1,0:T(8,128)(2,1)}, u32[]{:S(2)}) copy-start(bf16[256,2048]{1,0:T(8,128)(2,1)} %all-reduce.2.cloned.1.call-done) | copy-start | bytes 3145732 | tf_op jit(solution)/shard_map/while
  93.0 3.0 %copy-start.5 = (bf16[2,256,2048]{2,1,0:T(8,128)(2,1)S(1)}, bf16[2,256,2048]{2,1,0:T(8,128)(2,1)}, u32[]{:S(2)}) copy-start(bf16[2,256,2048]{2,1,0:T(8,128)(2,1)} %get-tuple-element.373) | copy-start | bytes 6291460 | tf_op jit(solution)/shard_map/while
  96.4 17.3 %copy-start.6 = (bf16[2,256,2048]{2,1,0:T(8,128)(2,1)}, bf16[2,256,2048]{2,1,0:T(8,128)(2,1)S(1)}, u32[]{:S(2)}) copy-start(bf16[2,256,2048]{2,1,0:T(8,128)(2,1)S(1)} %bitcast_dynamic-update-slice_fusion.7) | copy-start | bytes 6291460 | tf_op jit(solution)/shard_map/while
  113.7 75.6 %all-reduce.2.cloned.1.call-start = ((), (), s32[]{:S(2)}) async-start(), calls=%async_computation.1 | async-start | bytes 2097152 | tf_op jit(solution)/shard_map/while/body/eval_jaxpr/psum | solution.py:26
  114.4 15.5 %copy-start.1 = (bf16[2048,384]{1,0:T(8,128)(2,1)S(1)}, bf16[2048,384]{1,0:T(8,128)(2,1)}, u32[]{:S(2)}) copy-start(bf16[2048,384]{1,0:T(8,128)(2,1)} %get-tuple-element.392) | copy-start | bytes 4718596 | tf_op jit(solution)/shard_map/while
  114.4 15.5 %copy-start.2 = (bf16[2,256,384]{2,1,0:T(8,128)(2,1)S(1)}, bf16[2,256,384]{2,1,0:T(8,128)(2,1)}, u32[]{:S(2)}) copy-start(bf16[2,256,384]{2,1,0:T(8,128)(2,1)} %get-tuple-element.391) | copy-start | bytes 1179652 | tf_op jit(solution)/shard_map/while
  131.6 62.1 %all-to-all-start = ((bf16[8,32,2048]{2,1,0:T(8,128)(2,1)}), bf16[8,32,2048]{2,1,0:T(8,128)(2,1)S(1)}, u32[]{:S(2)}, u32[]{:S(2)}) async-start(bf16[8,32,2048]{2,1,0:T(8,128)(2,1)} %bitcast.50), calls=%async_computation | async-start | bytes 2097152 | tf_op jit(solution)/shard_map/while/body/eval_jaxpr/all_to_all | solution.py:33
  135.4 79.8 %all-gather.2.cloned.1.call-start = ((), (), s32[]{:S(2)}) async-start(), calls=%async_computation.2 | async-start | bytes 1179648 | tf_op jit(solution)/shard_map/while/body/eval_jaxpr/all_gather | solution.py:40
  190.9 4.2 %copy-start.4 = (bf16[2,32,2048]{2,1,0:T(8,128)(2,1)S(1)}, bf16[2,32,2048]{2,1,0:T(8,128)(2,1)}, u32[]{:S(2)}) copy-start(bf16[2,32,2048]{2,1,0:T(8,128)(2,1)} %get-tuple-element.398) | copy-start | bytes 786436 | tf_op jit(solution)/shard_map/while
  193.7 3.2 %copy-start = (bf16[256,2048]{1,0:T(8,128)(2,1)S(1)}, bf16[256,2048]{1,0:T(8,128)(2,1)}, u32[]{:S(2)}) copy-start(bf16[256,2048]{1,0:T(8,128)(2,1)} %all-reduce.2.cloned.1.call-done) | copy-start | bytes 3145732 | tf_op jit(solution)/shard_map/while
  196.9 3.1 %copy-start.5 = (bf16[2,256,2048]{2,1,0:T(8,128)(2,1)S(1)}, bf16[2,256,2048]{2,1,0:T(8,128)(2,1)}, u32[]{:S(2)}) copy-start(bf16[2,256,2048]{2,1,0:T(8,128)(2,1)} %get-tuple-element.373) | copy-start | bytes 6291460 | tf_op jit(solution)/shard_map/while
  200.2 17.3 %copy-start.6 = (bf16[2,256,2048]{2,1,0:T(8,128)(2,1)}, bf16[2,256,2048]{2,1,0:T(8,128)(2,1)S(1)}, u32[]{:S(2)}) copy-start(bf16[2,256,2048]{2,1,0:T(8,128)(2,1)S(1)} %bitcast_dynamic-update-slice_fusion.7) | copy-start | bytes 6291460 | tf_op jit(solution)/shard_map/while
  217.6 29.3 %copy-start.8 = (bf16[2,32,2048]{2,1,0:T(8,128)(2,1)}, bf16[2,32,2048]{2,1,0:T(8,128)(2,1)S(1)}, u32[]{:S(2)}) copy-start(bf16[2,32,2048]{2,1,0:T(8,128)(2,1)S(1)} %get-tuple-element.178) | copy-start | bytes 786436
  218.2 28.6 %copy-start.3 = (bf16[2,256,384]{2,1,0:T(8,128)(2,1)S(1)}, bf16[2,256,384]{2,1,0:T(8,128)(2,1)}, u32[]{:S(2)}) copy-start(bf16[2,256,384]{2,1,0:T(8,128)(2,1)} %get-tuple-element.410) | copy-start | bytes 1179652
  218.2 28.6 %copy-start.7 = (bf16[2,256,2048]{2,1,0:T(8,128)(2,1)S(1)}, bf16[2,256,2048]{2,1,0:T(8,128)(2,1)}, u32[]{:S(2)}) copy-start(bf16[2,256,2048]{2,1,0:T(8,128)(2,1)} %get-tuple-element.185) | copy-start | bytes 6291460
Sparse Core Ops, SparseCore 0:
  24.2 61.1 all-reduce.1
  93.1 18.1 all-gather.1
  130.0 59.2 all-reduce.1
  197.0 18.1 all-gather.1
where the time goes:
time: 271 us
  waiting for transfers between devices  138 us (51%)
  matrix products  72 us (27%)
  other arithmetic  18.2 us (7%)
  blocking collectives  14.2 us (5%)
  between operations  13.8 us (5%)
  starting transfers between devices  9.2 us (3%)
  local copies, waits for them, and re-layouts  4.93 us (2%)
    psum x2, waiting for transfers between devices, micro(): x = lax.psum(xp, 'tp')  108 us
    dot_general x2, matrix products, micro(): jnp.dot(oh, emb, preferred_element_type=jnp.float32).astype(jnp.bfloat16)  30.9 us
    all_gather x2, waiting for transfers between devices, micro(): dxa = lax.all_gather(dx, 'tp', axis=0, tiled=True)  29.9 us
    dot_general x1, matrix products, local(): de = jnp.dot(oh, dxs.reshape(-1, d), preferred_element_type=jnp.float32)  28.6 us
    psum x1, blocking collectives, local(): dg = lax.psum(dg, 'tp')  14.2 us
    all_to_all x2, starting transfers between devices, micro(): recv = lax.all_to_all(pdn, 'tp', 0, 0, tiled=True).reshape(groups, tl, d)  9.07 us
    dot_general x2, matrix products, micro(): u = jnp.dot(n, w, preferred_element_type=jnp.float32).astype(jnp.bfloat16)  6.02 us
    mul x2, other arithmetic, micro(): nh = xf * rs  5.59 us
  transfers between devices with their start and end apart: 6, of which 4 were waited for; matrix products, arithmetic and copies ran while one was open for 7% of the time, Pallas kernels for 0%

commit v1 on v0

v1 whole, which is shorter than its diff:
```python
import functools

import jax
import jax.numpy as jnp
from jax import lax
from jax.experimental import pallas as pl
from jax.experimental.pallas import tpu as pltpu
from jax.sharding import PartitionSpec as P

EPS = 1e-6
MESH = pl.DeviceIdType.MESH
VMEM = pl.BlockSpec(memory_space=pltpu.VMEM)
SMEM = pl.BlockSpec(memory_space=pltpu.SMEM)
ANY = pl.BlockSpec(memory_space=pl.ANY)
F32 = jnp.float32
BF16 = jnp.bfloat16


def exchange(n, p_ref, du_ref, w_ref, g_ref, dres_ref, y_ref, dg_ref,
             d_s, prx, prd, sx, sd, rx, rd, nh_s, rs_s, dgs,
             pxs, pxr, pds, pdr, xs_sem, xr_sem, ds_sem, dr_sem, gs_sem, gr_sem):
    me = lax.axis_index("tp")
    chips = n // 2
    chip, core = me // 2, me % 2
    partner = chip * 2 + 1 - core
    right = ((chip + 1) % chips) * 2 + core
    left = ((chip + chips - 1) % chips) * 2 + core
    k, h, d = dres_ref.shape
    t = du_ref.shape[1]

    def dev(j, same):
        return ((chip + j) % chips) * 2 + (core if same else 1 - core)

    barrier = pltpu.get_barrier_semaphore()
    for o in range(1, n):
        pl.semaphore_signal(barrier, inc=1, device_id={"tp": (me + o) % n}, device_id_type=MESH)
    pl.semaphore_wait(barrier, n - 1)

    copies = []

    def send(src, dst, ss, rs, to):
        c = pltpu.make_async_remote_copy(src_ref=src, dst_ref=dst, send_sem=ss, recv_sem=rs,
                                         device_id={"tp": to}, device_id_type=MESH)
        c.start()
        copies.append(c)

    def arrived(dst, ss, rs):
        pltpu.make_async_remote_copy(src_ref=dst, dst_ref=dst, send_sem=ss, recv_sem=rs,
                                     device_id={"tp": partner}, device_id_type=MESH).wait_recv()

    order = (2, 1, 3, 0)
    for j in order:
        send(p_ref.at[dev(j, False)], prx.at[j], pxs.at[j], pxr.at[j], partner)

    def partial_dn(m):
        cw = 512

        def cols(i, _):
            c0 = pl.multiple_of(i * cw, cw)
            v = lax.dot_general(du_ref[m], w_ref[pl.ds(c0, cw), :], (((1,), (1,)), ((), ())),
                                preferred_element_type=F32)
            d_s[:, m * h:(m + 1) * h, pl.ds(c0, cw)] = v.astype(BF16).reshape(n, h, cw)
            return 0

        lax.fori_loop(0, d // cw, cols, 0)

    def half(ref, j, m):
        return ref.at[j, pl.ds(m * h, h)]

    def ring(s, r, ss, rs, direction, chunk, src):
        send(src, r.at[direction, chunk], ss.at[direction, chunk], rs.at[direction, chunk],
             right if direction == 0 else left)

    def first_hops(j, s, r, ss, rs):
        if j == 2:
            ring(s, r, ss, rs, 0, 0, half(s, 2, 0))
            ring(s, r, ss, rs, 1, 0, half(s, 2, 1))
        if j == 1:
            ring(s, r, ss, rs, 0, 1, half(s, 1, 1))
        if j == 3:
            ring(s, r, ss, rs, 1, 1, half(s, 3, 0))

    partial_dn(0)
    for j in order:
        arrived(prx.at[j], pxs.at[j], pxr.at[j])
        sx[j] = p_ref[dev(j, True)] + prx[j]
        first_hops(j, sx, rx, xs_sem, xr_sem)
    partial_dn(1)
    for j in order:
        send(d_s.at[dev(j, False)], prd.at[j], pds.at[j], pdr.at[j], partner)
    for j in order:
        arrived(prd.at[j], pds.at[j], pdr.at[j])
        sd[j] = d_s[dev(j, True)].astype(F32) + prd[j].astype(F32)
        first_hops(j, sd, rd, ds_sem, dr_sem)

    def second_hops(s, r, ss, rs):
        arrived(r.at[0, 0], ss.at[0, 0], rs.at[0, 0])
        s[1, :h] = s[1, :h] + r[0, 0]
        ring(s, r, ss, rs, 0, 2, half(s, 1, 0))
        arrived(r.at[1, 0], ss.at[1, 0], rs.at[1, 0])
        s[3, h:] = s[3, h:] + r[1, 0]
        ring(s, r, ss, rs, 1, 2, half(s, 3, 1))

    second_hops(sx, rx, xs_sem, xr_sem)
    second_hops(sd, rd, ds_sem, dr_sem)

    q = 16
    steps = h // q
    for dr, c in ((0, 1), (1, 1), (0, 2), (1, 2)):
        arrived(rx.at[dr, c], xs_sem.at[dr, c], xr_sem.at[dr, c])
    for m in range(k):
        ca, cb = (2, 1) if m == 0 else (1, 2)

        def norm(i, _):
            r0 = pl.multiple_of(i * q, q)
            rows = pl.ds(r0, q)
            x = sx[0, pl.ds(m * h + r0, q)] + rx[0, ca, rows] + rx[1, cb, rows]
            y_ref[0, m, rows] = x
            xf = x.astype(F32)
            rs = lax.rsqrt(jnp.mean(xf * xf, axis=-1, keepdims=True) + EPS)
            nh_s[m, rows] = xf * rs
            rs_s[m, rows] = jnp.broadcast_to(rs, (q, rs_s.shape[-1]))
            return 0

        lax.fori_loop(0, steps, norm, 0)

    for dr, c in ((0, 1), (1, 1), (0, 2), (1, 2)):
        arrived(rd.at[dr, c], ds_sem.at[dr, c], dr_sem.at[dr, c])
    dg = jnp.zeros((1, d), F32)
    for m in range(k):
        ca, cb = (2, 1) if m == 0 else (1, 2)

        def total(i, acc):
            r0 = pl.multiple_of(i * q, q)
            rows = pl.ds(r0, q)
            dn = sd[0, pl.ds(m * h + r0, q)] + rd[0, ca, rows] + rd[1, cb, rows]
            sd[0, pl.ds(m * h + r0, q)] = dn
            return acc + jnp.sum(dn * nh_s[m, rows], axis=0, keepdims=True)

        dg = lax.fori_loop(0, steps, total, dg)
    dgs[me] = dg
    for o in range(1, n):
        send(dgs.at[me], dgs.at[me], gs_sem.at[o], gr_sem.at[me], (me + o) % n)

    gf = g_ref[...].astype(F32)
    for m in range(k):
        def grad(i, _):
            r0 = pl.multiple_of(i * q, q)
            rows = pl.ds(r0, q)
            nh = nh_s[m, rows]
            gdn = gf * sd[0, pl.ds(m * h + r0, q)]
            dxn = rs_s[m, rows, :1] * (gdn - nh * jnp.mean(nh * gdn, axis=-1, keepdims=True))
            y_ref[1, m, rows] = (dres_ref[m, rows].astype(F32) + dxn).astype(BF16)
            return 0

        lax.fori_loop(0, steps, grad, 0)

    for o in range(1, n):
        src = (me + o) % n
        arrived(dgs.at[src], gs_sem.at[o], gr_sem.at[src])
    total_dg = dgs[0]
    for i in range(1, n):
        total_dg = total_dg + dgs[i]
    dg_ref[...] = total_dg
    for c in copies:
        c.wait_send()


def clear(first, rows, prev, tie_ref, z_in, de_ref, z, sem):
    del prev, tie_ref, z_in
    z[...] = jnp.zeros_like(z)
    zr = z.shape[0]
    cs = [pltpu.make_async_copy(z, de_ref.at[pl.ds(first + i * zr, zr)], sem) for i in range(rows // zr)]
    for c in cs:
        c.start()
    for c in cs:
        c.wait()


def clear_first(first, rows, tie_ref, de_ref, z, sem):
    clear(first, rows, None, tie_ref, None, de_ref, z, sem)


def clear_next(first, rows, tie_ref, z_in, de_ref, z, sem):
    clear(first, rows, None, tie_ref, z_in, de_ref, z, sem)


def finish(n, ids_ref, *refs):
    np_ = 2 * n
    xs, dxs = refs[:n], refs[n:np_]
    w_ref, du_ref, g_ref, de_in, u_ref, dw_ref, de_ref = refs[np_:np_ + 7]
    n_s, dxb, dxf, acc, table, blocks, sem = refs[np_ + 7:]
    del de_in
    me = lax.axis_index("tp")
    chips = n // 2
    chip, core = me // 2, me % 2
    k, h, d = xs[0].shape
    t = h * n
    vl = de_ref.shape[0] * de_ref.shape[1]
    lo = me * vl
    gf = g_ref[...].astype(F32)
    offs = (0, chips - 1, 1, 2)
    devs = [((chip + offs[i % 4]) % chips) * 2 + (core if i < 4 else 1 - core) for i in range(n)]
    q = 16
    for i in range(n):
        for m in range(k):
            def one(s, _):
                r0 = pl.multiple_of(s * q, q)
                rows = pl.ds(r0, q)
                xf = xs[i][m, rows].astype(F32)
                rs = lax.rsqrt(jnp.mean(xf * xf, axis=-1, keepdims=True) + EPS)
                n_s[pl.ds(pl.multiple_of(m * t + devs[i] * h + r0, q), q)] = ((xf * rs) * gf).astype(BF16)
                dxf[pl.ds(pl.multiple_of(devs[i] * (k * h) + m * h + r0, q), q)] = dxs[i][m, rows].astype(F32)
                return 0

            lax.fori_loop(0, h // q, one, 0)

    nb = table.shape[0]

    def reset(i, _):
        table[i] = -1
        return 0

    lax.fori_loop(0, nb, reset, 0, unroll=8)
    sub = lax.broadcasted_iota(jnp.int32, (8, d), 0)

    def scatter(i, cnt):
        v = ids_ref[i] - lo
        owned = (v >= 0) & (v < vl)

        def hit(cnt):
            b = v // 8
            slot0 = table[b]
            fresh = slot0 < 0
            slot = jnp.where(fresh, cnt, slot0)
            table[b] = slot
            blocks[slot] = b
            row = jnp.where(sub == v % 8, jnp.broadcast_to(dxf[pl.ds(i, 1)], (8, d)), 0.0)
            acc[slot] = row + jnp.where(fresh, jnp.zeros((8, d), F32), acc[slot])
            return jnp.where(fresh, cnt + 1, cnt)

        return lax.cond(owned, hit, lambda c: c, cnt)

    cnt = lax.fori_loop(0, k * t, scatter, 0)

    def put(i, _):
        pltpu.make_async_copy(acc.at[i], de_ref.at[blocks[i]], sem).start()
        return 0

    lax.fori_loop(0, cnt, put, 0)

    w = w_ref[...]
    for m in range(k):
        u_ref[m] = jnp.dot(n_s[m * t:(m + 1) * t], w, preferred_element_type=F32).astype(BF16)
    cw = 256

    def wgrad(i, _):
        c0 = pl.multiple_of(i * cw, cw)
        v = jnp.zeros((cw, w_ref.shape[1]), F32)
        for m in range(k):
            v = v + lax.dot_general(n_s[m * t:(m + 1) * t, pl.ds(c0, cw)], du_ref[m], (((0,), (0,)), ((), ())),
                                    preferred_element_type=F32)
        dw_ref[pl.ds(c0, cw)] = v
        return 0

    lax.fori_loop(0, d // cw, wgrad, 0)

    def drain(i, _):
        pltpu.make_async_copy(acc.at[i], de_ref.at[blocks[i]], sem).wait()
        return 0

    lax.fori_loop(0, cnt, drain, 0)


def solution(mesh):
    n = mesh.shape["tp"]
    chips = n // 2
    to_right = [(r, (r + 2) % n) for r in range(n)]
    to_left = [(r, (r + n - 2) % n) for r in range(n)]
    to_partner = [(r, r ^ 1) for r in range(n)]

    def local(ids, emb, g, w, du, dres):
        r = lax.axis_index("tp")
        k, t = ids.shape
        vl, d = emb.shape
        f = w.shape[1]
        h = t // n
        g2 = g.reshape(1, d)
        slab_ids = ids.reshape(k, n, h).transpose(1, 0, 2).reshape(-1)
        loc = slab_ids - r * vl
        own = (loc >= 0) & (loc < vl)
        rows = jnp.where(own[:, None], emb[jnp.clip(loc, 0, vl - 1)], jnp.zeros((), BF16))

        dma = pltpu.SemaphoreType.DMA
        y, dg = pl.pallas_call(
            functools.partial(exchange, n),
            out_shape=(jax.ShapeDtypeStruct((2, k, h, d), BF16), jax.ShapeDtypeStruct((1, d), F32)),
            in_specs=[VMEM] * 5,
            out_specs=(VMEM, VMEM),
            scratch_shapes=[
                pltpu.VMEM((n, k * h, d), BF16),
                pltpu.VMEM((chips, k * h, d), BF16),
                pltpu.VMEM((chips, k * h, d), BF16),
                pltpu.VMEM((chips, k * h, d), BF16),
                pltpu.VMEM((chips, k * h, d), F32),
                pltpu.VMEM((2, 3, h, d), BF16),
                pltpu.VMEM((2, 3, h, d), F32),
                pltpu.VMEM((k, h, d), F32),
                pltpu.VMEM((k, h, 128), F32),
                pltpu.VMEM((n, 1, d), F32),
                dma((chips,)), dma((chips,)), dma((chips,)), dma((chips,)),
                dma((2, 3)), dma((2, 3)), dma((2, 3)), dma((2, 3)),
                dma((n,)), dma((n,)),
            ],
            compiler_params=pltpu.CompilerParams(collective_id=0, has_side_effects=True, vmem_limit_bytes=40 << 20),
            name="exchange",
        )(rows.reshape(n, k * h, d), du, w, g2, dres)

        yl = lax.ppermute(y, "tp", to_right)
        yr = lax.ppermute(y, "tp", to_left)
        py = lax.ppermute(y, "tp", to_partner)
        xo = lax.ppermute(yl[0], "tp", to_right)
        do = lax.ppermute(yr[1], "tp", to_left)
        pyl = lax.ppermute(yl, "tp", to_partner)
        pyr = lax.ppermute(yr, "tp", to_partner)
        pxo = lax.ppermute(xo, "tp", to_partner)
        pdo = lax.ppermute(do, "tp", to_partner)

        zr = 512
        split = (vl * 5 // 8) // zr * zr
        zcost = lambda b: pl.CostEstimate(flops=0, bytes_accessed=b, transcendentals=0)
        de = pl.pallas_call(
            functools.partial(clear_first, 0, split),
            out_shape=jax.ShapeDtypeStruct((vl, d), F32),
            in_specs=[ANY], out_specs=ANY,
            scratch_shapes=[pltpu.VMEM((zr, d), F32), dma],
            cost_estimate=zcost(split * d * 4),
            name="clear0",
        )(dg)
        de = pl.pallas_call(
            functools.partial(clear_next, split, vl - split),
            out_shape=jax.ShapeDtypeStruct((vl, d), F32),
            in_specs=[ANY, ANY], out_specs=ANY,
            input_output_aliases={1: 0},
            scratch_shapes=[pltpu.VMEM((zr, d), F32), dma],
            cost_estimate=zcost((vl - split) * d * 4),
            name="clear1",
        )(yl, de)

        xs = [y[0], yl[0], yr[0], xo, py[0], pyl[0], pyr[0], pxo]
        dxs = [y[1], yl[1], yr[1], do, py[1], pyl[1], pyr[1], pdo]
        u, dw, de = pl.pallas_call(
            functools.partial(finish, n),
            out_shape=(jax.ShapeDtypeStruct((k, t, f), BF16), jax.ShapeDtypeStruct((d, f), F32),
                       jax.ShapeDtypeStruct((vl // 8, 8, d), F32)),
            in_specs=[SMEM] + [VMEM] * (2 * n + 3) + [ANY],
            out_specs=(VMEM, VMEM, ANY),
            input_output_aliases={2 * n + 4: 2},
            scratch_shapes=[
                pltpu.VMEM((k * t, d), BF16),
                pltpu.VMEM((8, d), BF16),
                pltpu.VMEM((k * t, d), F32),
                pltpu.VMEM((k * t, 8, d), F32),
                pltpu.SMEM((vl // 8,), jnp.int32),
                pltpu.SMEM((k * t,), jnp.int32),
                dma,
            ],
            compiler_params=pltpu.CompilerParams(vmem_limit_bytes=60 << 20),
            name="finish",
        )(slab_ids, *xs, *dxs, w, du, g2, de.reshape(vl // 8, 8, d))
        return u, y[0], de.reshape(vl, d), dw, dg.reshape(d)

    return jax.shard_map(
        local,
        mesh=mesh,
        in_specs=(P("dp", None), P("tp", None), P(None), P(None, "tp"), P("dp", None, "tp"), P("dp", "tp", None)),
        out_specs=(P("dp", None, "tp"), P("dp", "tp", None), P(("dp", "tp"), None), P(None, ("dp", "tp")), P("dp")),
        check_vma=False,
    )
```

time: 271 us -> 122 us (0.45)
  waiting for transfers between devices: 138 us -> 0.02 us
  Pallas kernels: 0 us -> 86 us
  matrix products: 72 us -> 0 us
  local copies, waits for them, and re-layouts: 4.93 us -> 29.1 us
  other arithmetic: 18.2 us -> 0.25 us
  blocking collectives: 14.2 us -> 0 us
  between operations: 13.8 us -> 0.83 us
  starting transfers between devices: 9.2 us -> 5.88 us
    psum x2 -> x0, waiting for transfers between devices: 108 us -> none  [micro(): x = lax.psum(xp, 'tp')]
    pallas_call x0 -> x4, Pallas kernels: none -> 86 us  [the longest x1 39 us: local(): pl.pallas_call(functools.partial(exchange, n), out_shape=(jax.ShapeDtypeS...]
    dot_general x8 -> x0, matrix products: 72 us -> none  [the longest x2 30.9 us: micro(): jnp.dot(oh, emb, preferred_element_type=jnp.float32).astype(jnp.bfloat16)]
    all_gather x2 -> x0, waiting for transfers between devices: 29.9 us -> none  [micro(): dxa = lax.all_gather(dx, 'tp', axis=0, tiled=True)]
    gather x0 -> x1, local copies, waits for them, and re-layouts: none -> 18.1 us  [local(): emb[jnp.clip(loc, 0, vl - 1)]]
    psum x1 -> x0, blocking collectives: 14.2 us -> none  [local(): dg = lax.psum(dg, 'tp')]
    all_to_all x2 -> x0, starting transfers between devices: 9.07 us -> none  [micro(): recv = lax.all_to_all(pdn, 'tp', 0, 0, tiled=True).reshape(groups, tl, d)]
    squeeze x0 -> x6, local copies, waits for them, and re-layouts: none -> 5.96 us  [local(): dxs = [y[1], yl[1], yr[1], do, py[1], pyl[1], pyr[1], pdo]]
  transfers between devices with their start and end apart: 6 -> 9, of which waited for: 4 -> 0; matrix products, arithmetic and copies ran while one was open for 7% -> 5% of each run, Pallas kernels for 0% -> 18%
where the time goes in v1:
time: 122 us
  Pallas kernels  86 us (70%)
  local copies, waits for them, and re-layouts  29.1 us (24%)
  starting transfers between devices  5.88 us (5%)
    pallas_call x1, Pallas kernels, local(): pl.pallas_call(functools.partial(exchange, n), out_shape=(jax.ShapeDtypeS...  39 us
    pallas_call x1, Pallas kernels, local(): pl.pallas_call(functools.partial(finish, n), out_shape=(jax.ShapeDtypeStr...  24.4 us
    gather x1, local copies, waits for them, and re-layouts, local(): emb[jnp.clip(loc, 0, vl - 1)]  18.1 us
    pallas_call x1, Pallas kernels, local(): pl.pallas_call(functools.partial(clear_first, 0, split), out_shape=jax.Sh...  13.8 us
    pallas_call x1, Pallas kernels, local(): pl.pallas_call(functools.partial(clear_next, split, vl - split), out_shap...  8.72 us
    squeeze x6, local copies, waits for them, and re-layouts, local(): dxs = [y[1], yl[1], yr[1], do, py[1], pyl[1], pyr[1], pdo]  5.96 us
    unnamed x25, local copies, waits for them, and re-layouts  2.71 us
    ppermute x1, starting transfers between devices, local(): do = lax.ppermute(yr[1], 'tp', to_left)  2.68 us
  transfers between devices with their start and end apart: 9, of which 0 were waited for; matrix products, arithmetic and copies ran while one was open for 5% of the time, Pallas kernels for 18%

profile of v1, /device:TPU:112, one launch (start us, length us, event | category | flops | bytes accessed | tf_op | source)
XLA Modules:
  0.0 122.1 jit_solution(9753727161353827913)
XLA Ops:
  0.6 0.8 reshape.75
  1.4 0.1 and.12
  1.5 0.1 min.12
  1.6 0.7 reshape.77.g_ref.refs_18_
  2.3 18.1 %gather_fusion = bf16[512,2048]{1,0:T(8,128)(2,1)S(1)} fusion(bf16[8192,2048]{1,0:T(8,128)(2,1)} %param.7, s32[1024]{0:T(1024)S(1)} %pad_clamp_fusion), kind=kCustom, calls=%fused_computation | custom fusion | bytes 4196352 | tf_op jit(solution)/shard_map/gather | solution.py:292
  20.5 0.0 copy-start
  20.5 0.0 copy-start.1
  20.5 0.0 copy-start.2
  20.5 0.2 broadcast_select_fusion.p_ref
  20.7 1.1 copy-done
  21.9 0.1 copy-done.1
  21.9 0.1 copy-done.2
  22.0 39.0 %exchange.1 = (bf16[2,2,32,2048]{3,2,1,0:T(8,128)(2,1)S(1)}, f32[1,2048]{1,0:T(1,128)S(1)}) custom-call(bf16[8,64,2048]{2,1,0:T(8,128)(2,1)S(1)} %broadcast_select_fusion.p_ref, bf16[2,256,384]{2,1,0:T(8,128)(2,1)S(1)} %copy-done.1, bf16[2048,384]{1,0:T(8,128)(2,1)S(1)} %copy-done, bf16[1,2048]{1,0:T(2,128)(2,1)S(1)} %reshape.77.g_ref.refs_18_, ...), custom_call_target="tpu_custom_call" | custom-call | tf_op jit(solution)/shard_map/exchange/pallas_call | solution.py:295
  61.1 1.6 %collective-permute-start.1 = (bf16[2,2,32,2048]{3,2,1,0:T(8,128)(2,1)S(1)}, bf16[2,2,32,2048]{3,2,1,0:T(8,128)(2,1)S(1)}, u32[]{:S(2)}, u32[]{:S(2)}) collective-permute-start(bf16[2,2,32,2048]{3,2,1,0:T(8,128)(2,1)S(1)} %get-tuple-element.10), channel_id=1, source_target_pairs={{0,6},{1,7},{2,0},{3,1},{4,2},{5,3},{6,4},{7,5},{8,14},{9,15},{10,... | collective-permute-start | bytes 1572872 | tf_op jit(solution)/shard_map/ppermute | solution.py:320
  62.6 0.6 collective-permute-start
  63.2 0.8 slice_bitcast_fusion.10
  64.0 0.7 reshape.76.ids_ref
  64.7 13.8 %clear0.1.z_in = f32[8192,2048]{1,0:T(8,128)} custom-call(f32[1,2048]{1,0:T(1,128)} %copy-done.4), custom_call_target="tpu_custom_call" | custom-call | bytes 41943040 | tf_op jit(solution)/shard_map/clear0/pallas_call | solution.py:332
  78.5 0.8 slice_bitcast_fusion.3
  79.2 2.7 %collective-permute-start.7 = (bf16[2,32,2048]{2,1,0:T(8,128)(2,1)S(1)}, bf16[2,32,2048]{2,1,0:T(8,128)(2,1)S(1)}, u32[]{:S(2)}, u32[]{:S(2)}) collective-permute-start(bf16[2,32,2048]{2,1,0:T(8,128)(2,1)S(1)} %get-tuple-element.21.refs_10_), channel_id=1, source_target_pairs={{0,6},{1,7},{2,0},{3,1},{4,2},{5,3},{6,4},{7,5},{8,14},{9,15},{10,... | collective-permute-start | bytes 786440 | tf_op jit(solution)/shard_map/ppermute | solution.py:323
  81.9 0.8 slice_bitcast_fusion.4
  82.7 0.5 collective-permute-start.4
  83.3 0.8 slice_bitcast_fusion.2
  84.1 8.7 %clear1.1 = f32[8192,2048]{1,0:T(8,128)} custom-call(bf16[2,2,32,2048]{3,2,1,0:T(8,128)(2,1)} %copy-done.6, f32[8192,2048]{1,0:T(8,128)} %clear0.1.z_in), custom_call_target="tpu_custom_call", output_to_operand_aliasing={{}: (1, {})} | custom-call | bytes 25165824 | tf_op jit(solution)/shard_map/clear1/pallas_call | solution.py:340
  92.9 0.1 collective-permute-start.8
  93.0 0.5 collective-permute-start.6
  93.5 0.8 slice_bitcast_fusion
  94.3 1.9 %slice_bitcast_fusion.1 = (bf16[2,32,2048]{2,1,0:T(8,128)(2,1)}, bf16[2,32,2048]{2,1,0:T(8,128)(2,1)}) fusion(bf16[2,2,32,2048]{3,2,1,0:T(8,128)(2,1)} %collective-permute-done.4), kind=kLoop, calls=%fused_computation.3 | loop fusion | bytes 1048576 | tf_op jit(solution)/shard_map/squeeze | solution.py:351
  96.2 0.7 copy-done.10
  96.9 0.1 copy-done.11
  97.0 24.4 %finish.1 = (bf16[2,256,384]{2,1,0:T(8,128)(2,1)}, f32[2048,384]{1,0:T(8,128)}, f32[1024,8,2048]{2,1,0:T(8,128)}) custom-call(s32[512]{0:T(512)} %reshape.76.ids_ref, bf16[2,32,2048]{2,1,0:T(8,128)(2,1)} %get-tuple-element.33.refs_0_, bf16[2,32,2048]{2,1,0:T(8,128)(2,1)} %copy-done.8, ...), custom_call_target="tpu_custom_call", output_to_operand_aliasing={{2}: (20, {})} | custom-call | tf_op jit(solution)/shard_map/finish/pallas_call | solution.py:352
  121.5 0.6 copy.24
  (33 shorter events, 0.1 us)
Async XLA Ops:
  2.3 18.4 %copy-start.3 = (bf16[1,2048]{1,0:T(2,128)(2,1)}, bf16[1,2048]{1,0:T(2,128)(2,1)S(1)}, u32[]{:S(2)}) copy-start(bf16[1,2048]{1,0:T(2,128)(2,1)S(1)} %reshape.77.g_ref.refs_18_) | copy-start | bytes 12292
  20.5 1.4 %copy-start = (bf16[2048,384]{1,0:T(8,128)(2,1)S(1)}, bf16[2048,384]{1,0:T(8,128)(2,1)}, u32[]{:S(2)}) copy-start(bf16[2048,384]{1,0:T(8,128)(2,1)} %refs_16_.1) | copy-start | bytes 4718596
  20.5 1.5 %copy-start.1 = (bf16[2,256,384]{2,1,0:T(8,128)(2,1)S(1)}, bf16[2,256,384]{2,1,0:T(8,128)(2,1)}, u32[]{:S(2)}) copy-start(bf16[2,256,384]{2,1,0:T(8,128)(2,1)} %refs_17_.1) | copy-start | bytes 1179652
  20.5 1.5 %copy-start.2 = (bf16[2,32,2048]{2,1,0:T(8,128)(2,1)S(1)}, bf16[2,32,2048]{2,1,0:T(8,128)(2,1)}, u32[]{:S(2)}) copy-start(bf16[2,32,2048]{2,1,0:T(8,128)(2,1)} %dres_ref.1) | copy-start | bytes 786436
  61.1 2.9 %copy-start.4 = (f32[1,2048]{1,0:T(1,128)}, f32[1,2048]{1,0:T(1,128)S(1)}, u32[]{:S(2)}) copy-start(f32[1,2048]{1,0:T(1,128)S(1)} %get-tuple-element.11.tie_ref) | copy-start | bytes 24580
  61.1 17.4 %collective-permute-start.1 = (bf16[2,2,32,2048]{3,2,1,0:T(8,128)(2,1)S(1)}, bf16[2,2,32,2048]{3,2,1,0:T(8,128)(2,1)S(1)}, u32[]{:S(2)}, u32[]{:S(2)}) collective-permute-start(bf16[2,2,32,2048]{3,2,1,0:T(8,128)(2,1)S(1)} %get-tuple-element.10), channel_id=1, source_target_pairs={{0,6},{1,7},{2,0},{3,1},{4,2},{5,3},{6,4},{7,5},{8,14},{9,15},{10,... | collective-permute-start | bytes 1572872 | tf_op jit(solution)/shard_map/ppermute | solution.py:320
  62.6 20.6 %collective-permute-start.3 = (bf16[2,2,32,2048]{3,2,1,0:T(8,128)(2,1)S(1)}, bf16[2,2,32,2048]{3,2,1,0:T(8,128)(2,1)S(1)}, u32[]{:S(2)}, u32[]{:S(2)}) collective-permute-start(bf16[2,2,32,2048]{3,2,1,0:T(8,128)(2,1)S(1)} %get-tuple-element.10), channel_id=1, source_target_pairs={{0,1},{1,0},{2,3},{3,2},{4,5},{5,4},{6,7},{7,6},{8,9},{9,8},{10,11... | collective-permute-start | bytes 1572872 | tf_op jit(solution)/shard_map/ppermute | solution.py:321
  62.6 19.3 %collective-permute-start = (bf16[2,2,32,2048]{3,2,1,0:T(8,128)(2,1)S(1)}, bf16[2,2,32,2048]{3,2,1,0:T(8,128)(2,1)S(1)}, u32[]{:S(2)}, u32[]{:S(2)}) collective-permute-start(bf16[2,2,32,2048]{3,2,1,0:T(8,128)(2,1)S(1)} %get-tuple-element.10), channel_id=1, source_target_pairs={{0,2},{1,3},{2,4},{3,5},{4,6},{5,7},{6,0},{7,1},{8,10},{9,11},{10,... | collective-permute-start | bytes 1572872 | tf_op jit(solution)/shard_map/ppermute | solution.py:319
  79.2 13.6 %copy-start.7 = (bf16[2,32,2048]{2,1,0:T(8,128)(2,1)}, bf16[2,32,2048]{2,1,0:T(8,128)(2,1)S(1)}, u32[]{:S(2)}) copy-start(bf16[2,32,2048]{2,1,0:T(8,128)(2,1)S(1)} %get-tuple-element.21.refs_10_) | copy-start | bytes 786436
  79.2 13.6 %collective-permute-start.7 = (bf16[2,32,2048]{2,1,0:T(8,128)(2,1)S(1)}, bf16[2,32,2048]{2,1,0:T(8,128)(2,1)S(1)}, u32[]{:S(2)}, u32[]{:S(2)}) collective-permute-start(bf16[2,32,2048]{2,1,0:T(8,128)(2,1)S(1)} %get-tuple-element.21.refs_10_), channel_id=1, source_target_pairs={{0,6},{1,7},{2,0},{3,1},{4,2},{5,3},{6,4},{7,5},{8,14},{9,15},{10,... | collective-permute-start | bytes 786440 | tf_op jit(solution)/shard_map/ppermute | solution.py:323
  81.9 11.5 %collective-permute-start.5 = (bf16[2,2,32,2048]{3,2,1,0:T(8,128)(2,1)S(1)}, bf16[2,2,32,2048]{3,2,1,0:T(8,128)(2,1)S(1)}, u32[]{:S(2)}, u32[]{:S(2)}) collective-permute-start(bf16[2,2,32,2048]{3,2,1,0:T(8,128)(2,1)S(1)} %collective-permute-done.1), channel_id=1, source_target_pairs={{0,1},{1,0},{2,3},{3,2},{4,5},{5,4},{6,7},{7,6},{8,9},{9,8},{10,11... | collective-permute-start | bytes 1572872 | tf_op jit(solution)/shard_map/ppermute | solution.py:325
  81.9 2.2 %copy-start.6 = (bf16[2,2,32,2048]{3,2,1,0:T(8,128)(2,1)}, bf16[2,2,32,2048]{3,2,1,0:T(8,128)(2,1)S(1)}, u32[]{:S(2)}) copy-start(bf16[2,2,32,2048]{3,2,1,0:T(8,128)(2,1)S(1)} %collective-permute-done.tie_ref) | copy-start | bytes 1572868
  82.7 10.1 %copy-start.8 = (bf16[2,32,2048]{2,1,0:T(8,128)(2,1)}, bf16[2,32,2048]{2,1,0:T(8,128)(2,1)S(1)}, u32[]{:S(2)}) copy-start(bf16[2,32,2048]{2,1,0:T(8,128)(2,1)S(1)} %get-tuple-element.24.refs_1_) | copy-start | bytes 786436
  82.7 10.2 %collective-permute-start.2 = (bf16[2,32,2048]{2,1,0:T(8,128)(2,1)S(1)}, bf16[2,32,2048]{2,1,0:T(8,128)(2,1)}, u32[]{:S(2)}, u32[]{:S(2)}) collective-permute-start(bf16[2,32,2048]{2,1,0:T(8,128)(2,1)S(1)} %get-tuple-element.24.refs_1_), channel_id=1, source_target_pairs={{0,2},{1,3},{2,4},{3,5},{4,6},{5,7},{6,0},{7,1},{8,10},{9,11},{10,... | collective-permute-start | bytes 786440 | tf_op jit(solution)/shard_map/ppermute | solution.py:322
  82.7 11.6 %collective-permute-start.4 = (bf16[2,2,32,2048]{3,2,1,0:T(8,128)(2,1)S(1)}, bf16[2,2,32,2048]{3,2,1,0:T(8,128)(2,1)}, u32[]{:S(2)}, u32[]{:S(2)}) collective-permute-start(bf16[2,2,32,2048]{3,2,1,0:T(8,128)(2,1)S(1)} %collective-permute-done.tie_ref), channel_id=1, source_target_pairs={{0,1},{1,0},{2,3},{3,2},{4,5},{5,4},{6,7},{7,6},{8,9},{9,8},{10,11... | collective-permute-start | bytes 1572872 | tf_op jit(solution)/shard_map/ppermute | solution.py:324
  92.9 3.4 %copy-start.9 = (bf16[2,32,2048]{2,1,0:T(8,128)(2,1)}, bf16[2,32,2048]{2,1,0:T(8,128)(2,1)S(1)}, u32[]{:S(2)}) copy-start(bf16[2,32,2048]{2,1,0:T(8,128)(2,1)S(1)} %collective-permute-done.7.refs_11_) | copy-start | bytes 786436
  92.9 3.3 %collective-permute-start.8 = (bf16[2,32,2048]{2,1,0:T(8,128)(2,1)S(1)}, bf16[2,32,2048]{2,1,0:T(8,128)(2,1)S(1)}, u32[]{:S(2)}, u32[]{:S(2)}) collective-permute-start(bf16[2,32,2048]{2,1,0:T(8,128)(2,1)S(1)} %collective-permute-done.7.refs_11_), channel_id=1, source_target_pairs={{0,1},{1,0},{2,3},{3,2},{4,5},{5,4},{6,7},{7,6},{8,9},{9,8},{10,11... | collective-permute-start | bytes 786440 | tf_op jit(solution)/shard_map/ppermute | solution.py:327
  93.0 3.2 %collective-permute-start.6 = (bf16[2,32,2048]{2,1,0:T(8,128)(2,1)}, bf16[2,32,2048]{2,1,0:T(8,128)(2,1)S(1)}, u32[]{:S(2)}, u32[]{:S(2)}) collective-permute-start(bf16[2,32,2048]{2,1,0:T(8,128)(2,1)} %collective-permute-done.2.refs_3_), channel_id=1, source_target_pairs={{0,1},{1,0},{2,3},{3,2},{4,5},{5,4},{6,7},{7,6},{8,9},{9,8},{10,11... | collective-permute-start | bytes 786440 | tf_op jit(solution)/shard_map/ppermute | solution.py:326
  96.2 0.7 copy-start.10
  96.2 0.8 copy-start.11
  97.0 24.4 %copy-start.5 = (f32[1,2048]{1,0:T(1,128)S(1)}, f32[1,2048]{1,0:T(1,128)}, u32[]{:S(2)}) copy-start(f32[1,2048]{1,0:T(1,128)} %copy-done.4) | copy-start | bytes 24580

commit v2 on v0

v2 whole, which is shorter than its diff:
```python
import functools

import jax
import jax.numpy as jnp
from jax import lax
from jax.experimental import pallas as pl
from jax.experimental.pallas import tpu as pltpu
from jax.sharding import PartitionSpec as P

EPS = 1e-6
MESH = pl.DeviceIdType.MESH
VMEM = pl.BlockSpec(memory_space=pltpu.VMEM)
SMEM = pl.BlockSpec(memory_space=pltpu.SMEM)
ANY = pl.BlockSpec(memory_space=pl.ANY)
F32 = jnp.float32
BF16 = jnp.bfloat16
ROWS = 16
SLOTS = 128


def lookup(n, ids_ref, emb_ref, du_hbm, w_hbm, p_ref, d_ref, at_ref, row_ref, count_ref,
           du_s, w_s, buf, pf, sem, in_sem):
    me = lax.axis_index("tp")
    k, t = ids_ref.shape
    h = t // n
    d = emb_ref.shape[2]
    vl = emb_ref.shape[0] * 8
    lo = me * vl
    loads = [pltpu.make_async_copy(du_hbm, du_s, in_sem.at[0]), pltpu.make_async_copy(w_hbm, w_s, in_sem.at[1])]
    for c in loads:
        c.start()

    def find(m, owner, cnt):
        def one(j, cnt):
            v = ids_ref[m, owner * h + j] - lo
            own = (v >= 0) & (v < vl)

            @pl.when(own)
            def _():
                pltpu.make_async_copy(emb_ref.at[v // 8], buf.at[cnt], sem).start()
                at_ref[cnt] = owner * (k * h) + m * h + j
                row_ref[cnt] = v

            return cnt + own.astype(jnp.int32)

        return lax.fori_loop(0, h, one, cnt, unroll=8)

    cnt = jnp.int32(0)
    for m in range(k):
        cnt = lax.fori_loop(0, n, functools.partial(lambda m, o, c: find(m, o, c), m), cnt)
    count_ref[0] = cnt

    pf[...] = jnp.zeros_like(pf)
    for c in loads:
        c.wait()
    cw = 512
    for m in range(k):
        def cols(i, _):
            c0 = pl.multiple_of(i * cw, cw)
            v = lax.dot_general(du_s[m], w_s[pl.ds(c0, cw), :], (((1,), (1,)), ((), ())), preferred_element_type=F32)
            d_ref[:, m * h:(m + 1) * h, pl.ds(c0, cw)] = v.astype(BF16).reshape(n, h, cw)
            return 0

        lax.fori_loop(0, d // cw, cols, 0)

    sub = lax.broadcasted_iota(jnp.int32, (8, d), 0)

    def wait(i, _):
        pltpu.make_async_copy(emb_ref.at[0], buf.at[0], sem).wait()
        return 0

    lax.fori_loop(0, cnt, wait, 0)

    def place(i, _):
        x8 = buf[i].astype(F32)
        pf[pl.ds(at_ref[i], 1)] = jnp.sum(jnp.where(sub == row_ref[i] % 8, x8, 0.0), axis=0, keepdims=True)
        return 0

    lax.fori_loop(0, cnt, place, 0)

    def pack(i, _):
        r0 = pl.multiple_of(i * ROWS, ROWS)
        p_ref[pl.ds(r0, ROWS)] = pf[pl.ds(r0, ROWS)].astype(BF16)
        return 0

    lax.fori_loop(0, (k * t) // ROWS, pack, 0)


def exchange(n, p_ref, d_ref, g_ref, dres_ref, y_ref, dg_ref,
             prx, prd, sx, sd, rx, rd, nh_s, rs_s, dgs,
             pxs, pxr, pds, pdr, xs_sem, xr_sem, ds_sem, dr_sem, gs_sem, gr_sem):
    me = lax.axis_index("tp")
    chips = n // 2
    chip, core = me // 2, me % 2
    partner = chip * 2 + 1 - core
    right = ((chip + 1) % chips) * 2 + core
    left = ((chip + chips - 1) % chips) * 2 + core
    k, h, d = dres_ref.shape

    def dev(j, same):
        return ((chip + j) % chips) * 2 + (core if same else 1 - core)

    barrier = pltpu.get_barrier_semaphore()
    for o in range(1, n):
        pl.semaphore_signal(barrier, inc=1, device_id={"tp": (me + o) % n}, device_id_type=MESH)
    pl.semaphore_wait(barrier, n - 1)

    copies = []

    def send(src, dst, ss, rs, to):
        c = pltpu.make_async_remote_copy(src_ref=src, dst_ref=dst, send_sem=ss, recv_sem=rs,
                                         device_id={"tp": to}, device_id_type=MESH)
        c.start()
        copies.append(c)

    def arrived(dst, ss, rs):
        pltpu.make_async_remote_copy(src_ref=dst, dst_ref=dst, send_sem=ss, recv_sem=rs,
                                     device_id={"tp": partner}, device_id_type=MESH).wait_recv()

    def pair_x(j):
        send(p_ref.at[dev(j, False)], prx.at[j], pxs.at[j], pxr.at[j], partner)

    def pair_d(j):
        send(d_ref.at[dev(j, False)], prd.at[j], pds.at[j], pdr.at[j], partner)

    for f, j in ((pair_x, 2), (pair_d, 2), (pair_x, 1), (pair_x, 3), (pair_d, 1), (pair_d, 3), (pair_x, 0), (pair_d, 0)):
        f(j)

    def ring(r, ss, rs, direction, chunk, src):
        send(src, r.at[direction, chunk], ss.at[direction, chunk], rs.at[direction, chunk],
             right if direction == 0 else left)

    def half(ref, j, m):
        return ref.at[j, pl.ds(m * h, h)]

    def first_hops(j, s, r, ss, rs):
        if j == 2:
            ring(r, ss, rs, 0, 0, half(s, 2, 0))
            ring(r, ss, rs, 1, 0, half(s, 2, 1))
        if j == 1:
            ring(r, ss, rs, 0, 1, half(s, 1, 1))
        if j == 3:
            ring(r, ss, rs, 1, 1, half(s, 3, 0))

    def sum_x(j):
        arrived(prx.at[j], pxs.at[j], pxr.at[j])
        sx[j] = p_ref[dev(j, True)] + prx[j]
        first_hops(j, sx, rx, xs_sem, xr_sem)

    def sum_d(j):
        arrived(prd.at[j], pds.at[j], pdr.at[j])
        sd[j] = d_ref[dev(j, True)].astype(F32) + prd[j].astype(F32)
        first_hops(j, sd, rd, ds_sem, dr_sem)

    for f, j in ((sum_x, 2), (sum_d, 2), (sum_x, 1), (sum_x, 3), (sum_d, 1), (sum_d, 3), (sum_x, 0), (sum_d, 0)):
        f(j)

    arrived(rx.at[0, 0], xs_sem.at[0, 0], xr_sem.at[0, 0])
    sx[1, :h] = sx[1, :h] + rx[0, 0]
    ring(rx, xs_sem, xr_sem, 0, 2, half(sx, 1, 0))
    arrived(rx.at[1, 0], xs_sem.at[1, 0], xr_sem.at[1, 0])
    sx[3, h:] = sx[3, h:] + rx[1, 0]
    ring(rx, xs_sem, xr_sem, 1, 2, half(sx, 3, 1))

    pieces = h // ROWS
    last = (rd.at[0, 2], rd.at[1, 2])
    for dr, j, m in ((0, 1, 0), (1, 3, 1)):
        arrived(rd.at[dr, 0], ds_sem.at[dr, 0], dr_sem.at[dr, 0])
        sd[j, m * h:(m + 1) * h] = sd[j, m * h:(m + 1) * h] + rd[dr, 0]
        for i in range(pieces):
            rows = pl.ds(i * ROWS, ROWS)
            send(sd.at[j, pl.ds(m * h + i * ROWS, ROWS)], last[dr].at[rows], ds_sem.at[dr, 2 + i],
                 dr_sem.at[dr, 2 + i], right if dr == 0 else left)

    for dr, c in ((0, 1), (1, 1), (0, 2), (1, 2)):
        arrived(rx.at[dr, c], xs_sem.at[dr, c], xr_sem.at[dr, c])
    for m in range(k):
        ca, cb = (2, 1) if m == 0 else (1, 2)
        for i in range(pieces):
            rows = pl.ds(i * ROWS, ROWS)
            x = sx[0, pl.ds(m * h + i * ROWS, ROWS)] + rx[0, ca, rows] + rx[1, cb, rows]
            y_ref[0, m, rows] = x
            xf = x.astype(F32)
            rs = lax.rsqrt(jnp.mean(xf * xf, axis=-1, keepdims=True) + EPS)
            nh_s[m, rows] = xf * rs
            rs_s[m, rows] = jnp.broadcast_to(rs, (ROWS, rs_s.shape[-1]))

    gf = g_ref[...].astype(F32)
    dg = jnp.zeros((1, d), F32)

    def grad(m, i):
        rows = pl.ds(i * ROWS, ROWS)
        nh = nh_s[m, rows]
        gdn = gf * sd[0, pl.ds(m * h + i * ROWS, ROWS)]
        dxn = rs_s[m, rows, :1] * (gdn - nh * jnp.mean(nh * gdn, axis=-1, keepdims=True))
        y_ref[1, m, rows] = (dres_ref[m, rows].astype(F32) + dxn).astype(BF16)

    for dr in range(2):
        arrived(rd.at[dr, 1], ds_sem.at[dr, 1], dr_sem.at[dr, 1])
    for i in range(pieces):
        rows = pl.ds(i * ROWS, ROWS)
        for dr in range(2):
            arrived(last[dr].at[rows], ds_sem.at[dr, 2 + i], dr_sem.at[dr, 2 + i])
        for m in range(k):
            ca, cb = (2, 1) if m == 0 else (1, 2)
            dn = sd[0, pl.ds(m * h + i * ROWS, ROWS)] + rd[0, ca, rows] + rd[1, cb, rows]
            sd[0, pl.ds(m * h + i * ROWS, ROWS)] = dn
            dg = dg + jnp.sum(dn * nh_s[m, rows], axis=0, keepdims=True)
        if i == pieces - 1:
            dgs[me] = dg
            for o in range(1, n):
                send(dgs.at[me], dgs.at[me], gs_sem.at[o], gr_sem.at[me], (me + o) % n)
        for m in range(k):
            grad(m, i)

    for o in range(1, n):
        src = (me + o) % n
        arrived(dgs.at[src], gs_sem.at[o], gr_sem.at[src])
    total_dg = dgs[0]
    for i in range(1, n):
        total_dg = total_dg + dgs[i]
    dg_ref[...] = total_dg
    for c in copies:
        c.wait_send()


def zeros(z, de_ref, first, rows, sem):
    zr = z.shape[0]
    z[...] = jnp.zeros_like(z)
    cs = [pltpu.make_async_copy(z, de_ref.at[pl.ds(first // 8 + i * zr, zr)], sem)
          for i in range(rows // (8 * zr))]
    for c in cs:
        c.start()
    return cs


def clear_and_list(rows, y_ref, row_ref, count_ref, de_ref, x_ref, slot_ref, block_ref, blocks_ref, z, table, sem, x_sem):
    cs = zeros(z, de_ref, 0, rows, sem)
    out = pltpu.make_async_copy(y_ref.at[0], x_ref, x_sem)
    out.start()

    def reset(i, _):
        table[i] = -1
        return 0

    lax.fori_loop(0, table.shape[0], reset, 0, unroll=8)
    base = lax.axis_index("tp") * 0

    def one(i, used):
        b = row_ref[i] // 8
        s = table[b]
        fresh = s < 0
        s = jnp.where(fresh, used, s)
        table[b] = s
        block_ref[s] = b
        slot_ref[i] = s * 2 + fresh.astype(jnp.int32)
        return used + fresh.astype(jnp.int32)

    blocks_ref[0] = lax.fori_loop(0, count_ref[0], one, base)
    out.wait()
    for c in cs:
        c.wait()


def clear_rest(first, rows, y_ref, dg_ref, de_in, de_ref, z, sem):
    del y_ref, dg_ref, de_in
    for c in zeros(z, de_ref, first, rows, sem):
        c.wait()


def finish(n, at_ref, row_ref, slot_ref, block_ref, count_ref, blocks_ref, y0, yl, yr, xo, do, p0, pl_, pr, pxo, pdo,
           w_ref, du_ref, g_ref, de_in, u_ref, dw_ref, de_ref, n_s, dxf, acc, sem):
    del de_in
    me = lax.axis_index("tp")
    chips = n // 2
    chip, core = me // 2, me % 2
    k, h, d = xo.shape
    t = h * n
    gf = g_ref[...].astype(F32)
    pieces = []
    for c, parts in ((core, ((y0.at[0], y0.at[1]), (yl.at[0], yl.at[1]), (yr.at[0], yr.at[1]), (xo, do))),
                     (1 - core, ((p0.at[0], p0.at[1]), (pl_.at[0], pl_.at[1]), (pr.at[0], pr.at[1]), (pxo, pdo)))):
        for off, (x, dx) in zip((0, chips - 1, 1, 2), parts):
            pieces.append((((chip + off) % chips) * 2 + c, x, dx))

    for owner, _, dx in pieces:
        for m in range(k):
            for s in range(h // ROWS):
                dxf[pl.ds(pl.multiple_of(owner * (k * h) + m * h + s * ROWS, ROWS), ROWS)] = dx[m, pl.ds(s * ROWS, ROWS)].astype(F32)

    sub = lax.broadcasted_iota(jnp.int32, (8, d), 0)
    cnt, used = count_ref[0], blocks_ref[0]

    def drain(i, _):
        pltpu.make_async_copy(acc.at[0], de_ref.at[0], sem).wait()
        return 0

    def turn(q, _):
        @pl.when(q > 0)
        def _():
            lax.fori_loop(0, SLOTS, drain, 0)

        def one(i, _):
            code = slot_ref[i]
            s = code // 2 - q * SLOTS

            @pl.when((s >= 0) & (s < SLOTS))
            def _():
                row = jnp.where(sub == row_ref[i] % 8, jnp.broadcast_to(dxf[pl.ds(at_ref[i], 1)], (8, d)), 0.0)
                acc[s] = row + jnp.where(code % 2 == 1, jnp.zeros((8, d), F32), acc[s])

            return 0

        lax.fori_loop(0, cnt, one, 0)

        def put(i, _):
            pltpu.make_async_copy(acc.at[i], de_ref.at[block_ref[q * SLOTS + i]], sem).start()
            return 0

        lax.fori_loop(0, jnp.minimum(used - q * SLOTS, SLOTS), put, 0)
        return 0

    turns = (used + SLOTS - 1) // SLOTS
    lax.fori_loop(0, turns, turn, 0)

    for owner, x, _ in pieces:
        for m in range(k):
            for s in range(h // ROWS):
                xf = x[m, pl.ds(s * ROWS, ROWS)].astype(F32)
                rs = lax.rsqrt(jnp.mean(xf * xf, axis=-1, keepdims=True) + EPS)
                n_s[pl.ds(pl.multiple_of(m * t + owner * h + s * ROWS, ROWS), ROWS)] = ((xf * rs) * gf).astype(BF16)

    w = w_ref[...]
    for m in range(k):
        u_ref[m] = jnp.dot(n_s[m * t:(m + 1) * t], w, preferred_element_type=F32).astype(BF16)
    cw = 512

    def wgrad(i, _):
        c0 = pl.multiple_of(i * cw, cw)
        v = jnp.zeros((cw, w_ref.shape[1]), F32)
        for m in range(k):
            v = v + lax.dot_general(n_s[m * t:(m + 1) * t, pl.ds(c0, cw)], du_ref[m], (((0,), (0,)), ((), ())),
                                    preferred_element_type=F32)
        dw_ref[pl.ds(c0, cw)] = v
        return 0

    lax.fori_loop(0, d // cw, wgrad, 0)
    lax.fori_loop(0, used - jnp.maximum(turns - 1, 0) * SLOTS, drain, 0)


def solution(mesh):
    n = mesh.shape["tp"]
    chips = n // 2
    to_right = [(r, (r + 2) % n) for r in range(n)]
    to_left = [(r, (r + n - 2) % n) for r in range(n)]
    to_partner = [(r, r ^ 1) for r in range(n)]
    dma = pltpu.SemaphoreType.DMA

    def local(ids, emb, g, w, du, dres):
        k, t = ids.shape
        vl, d = emb.shape
        f = w.shape[1]
        h = t // n
        kt = k * t
        g2 = g.reshape(1, d)
        i32 = lambda *s: jax.ShapeDtypeStruct(s, jnp.int32)
        cost = lambda b: pl.CostEstimate(flops=0, bytes_accessed=b, transcendentals=0)

        rows, part, at, row, count = pl.pallas_call(
            functools.partial(lookup, n),
            out_shape=(jax.ShapeDtypeStruct((kt, d), BF16), jax.ShapeDtypeStruct((n, k * h, d), BF16),
                       i32(kt), i32(kt), i32(1)),
            in_specs=[SMEM, ANY, ANY, ANY],
            out_specs=(VMEM, VMEM, SMEM, SMEM, SMEM),
            scratch_shapes=[
                pltpu.VMEM((k, t, f), BF16), pltpu.VMEM((d, f), BF16), pltpu.VMEM((kt, 8, d), BF16),
                pltpu.VMEM((kt, d), F32), dma, dma((2,)),
            ],
            compiler_params=pltpu.CompilerParams(vmem_limit_bytes=32 << 20),
            name="lookup",
        )(ids, emb.reshape(vl // 8, 8, d), du, w)

        y, dg = pl.pallas_call(
            functools.partial(exchange, n),
            out_shape=(jax.ShapeDtypeStruct((2, k, h, d), BF16), jax.ShapeDtypeStruct((1, d), F32)),
            in_specs=[VMEM] * 4,
            out_specs=(VMEM, VMEM),
            scratch_shapes=[
                pltpu.VMEM((chips, k * h, d), BF16),
                pltpu.VMEM((chips, k * h, d), BF16),
                pltpu.VMEM((chips, k * h, d), BF16),
                pltpu.VMEM((chips, k * h, d), F32),
                pltpu.VMEM((2, 3, h, d), BF16),
                pltpu.VMEM((2, 3, h, d), F32),
                pltpu.VMEM((k, h, d), F32),
                pltpu.VMEM((k, h, 128), F32),
                pltpu.VMEM((n, 1, d), F32),
                dma((chips,)), dma((chips,)), dma((chips,)), dma((chips,)),
                dma((2, 3)), dma((2, 3)), dma((2, 2 + h // ROWS)), dma((2, 2 + h // ROWS)),
                dma((n,)), dma((n,)),
            ],
            compiler_params=pltpu.CompilerParams(collective_id=0, has_side_effects=True, vmem_limit_bytes=24 << 20),
            name="exchange",
        )(rows.reshape(n, k * h, d), part, g2, dres)

        yl = lax.ppermute(y, "tp", to_right)
        yr = lax.ppermute(y, "tp", to_left)
        py = lax.ppermute(y, "tp", to_partner)
        xo = lax.ppermute(yl[0], "tp", to_right)
        do = lax.ppermute(yr[1], "tp", to_left)
        pyl = lax.ppermute(yl, "tp", to_partner)
        pyr = lax.ppermute(yr, "tp", to_partner)
        pxo = lax.ppermute(xo, "tp", to_partner)
        pdo = lax.ppermute(do, "tp", to_partner)

        zr = 512
        split = (vl * 5 // 8) // zr * zr
        de_shape = jax.ShapeDtypeStruct((vl // 8, 8, d), F32)
        de, x, slot, block, blocks = pl.pallas_call(
            functools.partial(clear_and_list, split),
            out_shape=(de_shape, jax.ShapeDtypeStruct((k, h, d), BF16), i32(kt), i32(kt), i32(1)),
            in_specs=[VMEM, SMEM, SMEM],
            out_specs=(ANY, ANY, SMEM, SMEM, SMEM),
            scratch_shapes=[pltpu.VMEM((zr // 8, 8, d), F32), pltpu.SMEM((vl // 8,), jnp.int32), dma, dma],
            compiler_params=pltpu.CompilerParams(vmem_limit_bytes=8 << 20),
            cost_estimate=cost(split * d * 4),
            name="clear0",
        )(y, row, count)
        dgf = dg.reshape(d)
        de = pl.pallas_call(
            functools.partial(clear_rest, split, vl - split),
            out_shape=de_shape,
            in_specs=[ANY, ANY, ANY], out_specs=ANY,
            input_output_aliases={2: 0},
            scratch_shapes=[pltpu.VMEM((zr // 8, 8, d), F32), dma],
            compiler_params=pltpu.CompilerParams(vmem_limit_bytes=8 << 20),
            cost_estimate=cost((vl - split) * d * 4),
            name="clear1",
        )(yl, dgf, de)

        u, dw, de = pl.pallas_call(
            functools.partial(finish, n),
            out_shape=(jax.ShapeDtypeStruct((k, t, f), BF16), jax.ShapeDtypeStruct((d, f), F32), de_shape),
            in_specs=[SMEM] * 6 + [VMEM] * 13 + [ANY],
            out_specs=(VMEM, VMEM, ANY),
            input_output_aliases={19: 2},
            scratch_shapes=[
                pltpu.VMEM((kt, d), BF16),
                pltpu.VMEM((kt, d), F32),
                pltpu.VMEM((SLOTS, 8, d), F32),
                dma,
            ],
            compiler_params=pltpu.CompilerParams(vmem_limit_bytes=36 << 20),
            name="finish",
        )(at, row, slot, block, count, blocks, y, yl, yr, xo, do, py, pyl, pyr, pxo, pdo, w, du, g2, de)
        return u, x, de.reshape(vl, d), dw, dgf

    return jax.shard_map(
        local,
        mesh=mesh,
        in_specs=(P("dp", None), P("tp", None), P(None), P(None, "tp"), P("dp", None, "tp"), P("dp", "tp", None)),
        out_specs=(P("dp", None, "tp"), P("dp", "tp", None), P(("dp", "tp"), None), P(None, ("dp", "tp")), P("dp")),
        check_vma=False,
    )
```

time: 271 us -> 120 us (0.44)
  waiting for transfers between devices: 138 us -> 19.7 us
  Pallas kernels: 0 us -> 88.7 us
  matrix products: 72 us -> 0 us
  other arithmetic: 18.2 us -> 0 us
  blocking collectives: 14.2 us -> 0 us
  between operations: 13.8 us -> 0.78 us
  starting transfers between devices: 9.2 us -> 5.75 us
    psum x2 -> x0, waiting for transfers between devices: 108 us -> none  [micro(): x = lax.psum(xp, 'tp')]
    pallas_call x0 -> x5, Pallas kernels: none -> 88.7 us  [the longest x1 35.8 us: local(): pl.pallas_call(functools.partial(exchange, n), out_shape=(jax.ShapeDtypeS...]
    dot_general x8 -> x0, matrix products: 72 us -> none  [the longest x2 30.9 us: micro(): jnp.dot(oh, emb, preferred_element_type=jnp.float32).astype(jnp.bfloat16)]
    all_gather x2 -> x0, waiting for transfers between devices: 29.9 us -> none  [micro(): dxa = lax.all_gather(dx, 'tp', axis=0, tiled=True)]
    ppermute x0 -> x9, waiting for transfers between devices: none -> 19.7 us  [the longest x1 11.9 us: local(): yr = lax.ppermute(y, 'tp', to_left)]
    psum x1 -> x0, blocking collectives: 14.2 us -> none  [local(): dg = lax.psum(dg, 'tp')]
    all_to_all x2 -> x0, starting transfers between devices: 9.07 us -> none  [micro(): recv = lax.all_to_all(pdn, 'tp', 0, 0, tiled=True).reshape(groups, tl, d)]
    ppermute x0 -> x9, starting transfers between devices: none -> 5.75 us  [the longest x1 2.97 us: local(): do = lax.ppermute(yr[1], 'tp', to_left)]
  transfers between devices with their start and end apart: 6 -> 9, of which waited for: 4 -> 3; matrix products, arithmetic and copies ran while one was open for 7% -> 0% of each run, Pallas kernels for 0% -> 20%
where the time goes in v2:
time: 120 us; the launch traced here: 119 us
  Pallas kernels  88.7 us (74%)
  waiting for transfers between devices  19.7 us (16%)
  starting transfers between devices  5.75 us (5%)
  local copies, waits for them, and re-layouts  4.43 us (4%)
    pallas_call x1, Pallas kernels, local(): pl.pallas_call(functools.partial(exchange, n), out_shape=(jax.ShapeDtypeS...  35.8 us
    pallas_call x1, Pallas kernels, local(): pl.pallas_call(functools.partial(clear_and_list, split), out_shape=(de_sh...  15.6 us
    pallas_call x1, Pallas kernels, local(): pl.pallas_call(functools.partial(lookup, n), out_shape=(jax.ShapeDtypeStr...  14.9 us
    pallas_call x1, Pallas kernels, local(): pl.pallas_call(functools.partial(finish, n), out_shape=(jax.ShapeDtypeStr...  13.6 us
    ppermute x1, waiting for transfers between devices, local(): yr = lax.ppermute(y, 'tp', to_left)  11.9 us
    pallas_call x1, Pallas kernels, local(): pl.pallas_call(functools.partial(clear_rest, split, vl - split), out_shap...  8.72 us
    ppermute x1, waiting for transfers between devices, local(): do = lax.ppermute(yr[1], 'tp', to_left)  4.26 us
    unnamed x13, local copies, waits for them, and re-layouts  3.7 us
  transfers between devices with their start and end apart: 9, of which 3 were waited for; matrix products, arithmetic and copies ran while one was open for 0% of the time, Pallas kernels for 20%

profile of v2, /device:TPU:112, one launch (start us, length us, event | category | flops | bytes accessed | tf_op | source)
XLA Modules:
  0.0 119.4 jit_solution(5465717537404569035)
XLA Ops:
  0.6 0.7 reshape.27.g_ref
  1.3 1.4 %copy-done = bf16[2048,384]{1,0:T(8,128)(2,1)S(1)} copy-done((bf16[2048,384]{1,0:T(8,128)(2,1)S(1)}, bf16[2048,384]{1,0:T(8,128)(2,1)}, u32[]{:S(2)}) %copy-start) | copy-done | bytes 1572888
  2.7 1.0 copy-done.2
  3.7 0.7 copy-done.5
  4.4 14.9 %lookup.1 = (bf16[512,2048]{1,0:T(8,128)(2,1)S(1)}, bf16[8,64,2048]{2,1,0:T(8,128)(2,1)S(1)}, s32[512]{0:T(512)S(1)}, s32[512]{0:T(512)S(1)}, s32[1]{0:T(128)}) custom-call(s32[2,256]{1,0:T(2,128)S(1)} %copy-done.5, bf16[1024,8,2048]{2,1,0:T(8,128)(2,1)} %bitcast.11, bf16[2,256,384]{2,1,0:T(8,128)(2,1)S(1)} %copy-done.2, bf16[2048,384]{1,0:T(8,128)(2,1)S(1)} %copy-done), custom_call_target="tpu_custom_call" | custom-call | tf_op jit(solution)/shard_map/lookup/pallas_call | solution.py:369
  19.3 0.0 copy-done.4
  19.3 35.8 %exchange.1 = (bf16[2,2,32,2048]{3,2,1,0:T(8,128)(2,1)S(1)}, f32[1,2048]{1,0:T(1,128)S(1)}) custom-call(bf16[8,64,2048]{2,1,0:T(8,128)(2,1)S(1)} %bitcast.8, bf16[8,64,2048]{2,1,0:T(8,128)(2,1)S(1)} %get-tuple-element.23.d_ref, bf16[1,2048]{1,0:T(2,128)(2,1)S(1)} %reshape.27.g_ref, bf16[2,32,2048]{2,1,0:T(8,128)(2,1)S(1)} %copy-done.4), custom_call_target="tpu_custom_call" | custom-call | tf_op jit(solution)/shard_map/exchange/pallas_call | solution.py:383
  55.1 1.8 %collective-permute-start.1 = (bf16[2,2,32,2048]{3,2,1,0:T(8,128)(2,1)S(1)}, bf16[2,2,32,2048]{3,2,1,0:T(8,128)(2,1)S(1)}, u32[]{:S(2)}, u32[]{:S(2)}) collective-permute-start(bf16[2,2,32,2048]{3,2,1,0:T(8,128)(2,1)S(1)} %get-tuple-element.24.y_ref.y0), channel_id=1, source_target_pairs={{0,6},{1,7},{2,0},{3,1},{4,2},{5,3},{6,4},{7,5},{8,14},{9,15},{10,... | collective-permute-start | bytes 1572872 | tf_op jit(solution)/shard_map/ppermute | solution.py:407
  56.9 0.3 collective-permute-start
  57.3 0.0 collective-permute-start.4
  57.3 11.9 %collective-permute-done.1.yr = bf16[2,2,32,2048]{3,2,1,0:T(8,128)(2,1)S(1)} collective-permute-done((bf16[2,2,32,2048]{3,2,1,0:T(8,128)(2,1)S(1)}, bf16[2,2,32,2048]{3,2,1,0:T(8,128)(2,1)S(1)}, u32[]{:S(2)}, u32[]{:S(2)}) %collective-permute-start.1) | collective-permute-done | bytes 524320 | tf_op jit(solution)/shard_map/ppermute | solution.py:407
  69.2 3.0 %collective-permute-start.3 = (bf16[2,32,2048]{2,1,0:T(8,128)(2,1)S(1)}, bf16[2,32,2048]{2,1,0:T(8,128)(2,1)S(1)}, u32[]{:S(2)}, u32[]{:S(2)}) collective-permute-start(bf16[2,32,2048]{2,1,0:T(8,128)(2,1)S(1)} %slice_bitcast_fusion), channel_id=1, source_target_pairs={{0,6},{1,7},{2,0},{3,1},{4,2},{5,3},{6,4},{7,5},{8,14},{9,15},{10,... | collective-permute-start | bytes 786440 | tf_op jit(solution)/shard_map/ppermute | solution.py:410
  72.2 0.0 collective-permute-done.y_ref.yl
  72.2 0.1 collective-permute-start.2
  72.3 0.1 collective-permute-start.6
  72.4 0.5 collective-permute-start.5
  72.9 4.3 %collective-permute-done.3.do = bf16[2,32,2048]{2,1,0:T(8,128)(2,1)S(1)} collective-permute-done((bf16[2,32,2048]{2,1,0:T(8,128)(2,1)S(1)}, bf16[2,32,2048]{2,1,0:T(8,128)(2,1)S(1)}, u32[]{:S(2)}, u32[]{:S(2)}) %collective-permute-start.3) | collective-permute-done | bytes 262176 | tf_op jit(solution)/shard_map/ppermute | solution.py:410
  77.1 0.0 collective-permute-start.8
  77.1 3.5 %collective-permute-done.2.xo = bf16[2,32,2048]{2,1,0:T(8,128)(2,1)S(1)} collective-permute-done((bf16[2,32,2048]{2,1,0:T(8,128)(2,1)S(1)}, bf16[2,32,2048]{2,1,0:T(8,128)(2,1)S(1)}, u32[]{:S(2)}, u32[]{:S(2)}) %collective-permute-start.2) | collective-permute-done | bytes 262176 | tf_op jit(solution)/shard_map/ppermute | solution.py:409
  80.7 0.0 collective-permute-start.7
  80.7 15.6 %clear0.1 = (f32[1024,8,2048]{2,1,0:T(8,128)}, bf16[2,32,2048]{2,1,0:T(8,128)(2,1)}, s32[512]{0:T(512)S(1)}, s32[512]{0:T(512)S(1)}, s32[1]{0:T(128)}) custom-call(bf16[2,2,32,2048]{3,2,1,0:T(8,128)(2,1)S(1)} %get-tuple-element.24.y_ref.y0, s32[512]{0:T(512)S(1)} %get-tuple-element.21.row_ref, s32[1]{0:T(128)} %get-tuple-element.25.count_ref), custom_call_target="tpu_custom_call" | custom-call | bytes 41943040 | tf_op jit(solution)/shard_map/clear0/pallas_call | solution.py:419
  96.3 0.0 copy-start.1
  96.3 0.0 copy-start.3
  96.3 8.7 %clear1.1.de_in = f32[1024,8,2048]{2,1,0:T(8,128)} custom-call(bf16[2,2,32,2048]{3,2,1,0:T(8,128)(2,1)S(1)} %collective-permute-done.y_ref.yl, f32[2048]{0:T(1024)S(1)} %bitcast.9, f32[1024,8,2048]{2,1,0:T(8,128)} %get-tuple-element.30.de_in), custom_call_target="tpu_custom_call", output_to_operand_aliasing={{}: (2, {})} | custom-call | bytes 25165824 | tf_op jit(solution)/shard_map/clear1/pallas_call | solution.py:430
  105.1 0.0 collective-permute-done.4.p0
  105.1 0.0 collective-permute-done.8.pdo
  105.1 0.0 collective-permute-done.6.pr
  105.1 0.0 collective-permute-done.7.pxo
  105.1 0.0 collective-permute-done.5.pl_
  105.1 0.0 copy-done.1
  105.1 13.6 %finish.1 = (bf16[2,256,384]{2,1,0:T(8,128)(2,1)}, f32[2048,384]{1,0:T(8,128)}, f32[1024,8,2048]{2,1,0:T(8,128)}) custom-call(s32[512]{0:T(512)S(1)} %get-tuple-element.20.at_ref, s32[512]{0:T(512)S(1)} %get-tuple-element.21.row_ref, s32[512]{0:T(512)S(1)} %get-tuple-element.26.slot_ref, ...), custom_call_target="tpu_custom_call", output_to_operand_aliasing={{2}: (19, {})} | custom-call | tf_op jit(solution)/shard_map/finish/pallas_call | solution.py:441
  118.8 0.6 copy.16
  (7 shorter events, 0.0 us)
Async XLA Ops:
  1.3 1.4 %copy-start = (bf16[2048,384]{1,0:T(8,128)(2,1)S(1)}, bf16[2048,384]{1,0:T(8,128)(2,1)}, u32[]{:S(2)}) copy-start(bf16[2048,384]{1,0:T(8,128)(2,1)} %w_ref.1) | copy-start | bytes 4718596
  2.7 1.0 copy-start.2
  3.7 0.7 copy-start.5
  4.4 14.9 %copy-start.4 = (bf16[2,32,2048]{2,1,0:T(8,128)(2,1)S(1)}, bf16[2,32,2048]{2,1,0:T(8,128)(2,1)}, u32[]{:S(2)}) copy-start(bf16[2,32,2048]{2,1,0:T(8,128)(2,1)} %dres_ref.1) | copy-start | bytes 786436
  55.1 14.0 %collective-permute-start.1 = (bf16[2,2,32,2048]{3,2,1,0:T(8,128)(2,1)S(1)}, bf16[2,2,32,2048]{3,2,1,0:T(8,128)(2,1)S(1)}, u32[]{:S(2)}, u32[]{:S(2)}) collective-permute-start(bf16[2,2,32,2048]{3,2,1,0:T(8,128)(2,1)S(1)} %get-tuple-element.24.y_ref.y0), channel_id=1, source_target_pairs={{0,6},{1,7},{2,0},{3,1},{4,2},{5,3},{6,4},{7,5},{8,14},{9,15},{10,... | collective-permute-start | bytes 1572872 | tf_op jit(solution)/shard_map/ppermute | solution.py:407
  56.9 15.3 %collective-permute-start = (bf16[2,2,32,2048]{3,2,1,0:T(8,128)(2,1)S(1)}, bf16[2,2,32,2048]{3,2,1,0:T(8,128)(2,1)S(1)}, u32[]{:S(2)}, u32[]{:S(2)}) collective-permute-start(bf16[2,2,32,2048]{3,2,1,0:T(8,128)(2,1)S(1)} %get-tuple-element.24.y_ref.y0), channel_id=1, source_target_pairs={{0,2},{1,3},{2,4},{3,5},{4,6},{5,7},{6,0},{7,1},{8,10},{9,11},{10,... | collective-permute-start | bytes 1572872 | tf_op jit(solution)/shard_map/ppermute | solution.py:406
  57.3 47.8 %collective-permute-start.4 = (bf16[2,2,32,2048]{3,2,1,0:T(8,128)(2,1)S(1)}, bf16[2,2,32,2048]{3,2,1,0:T(8,128)(2,1)S(1)}, u32[]{:S(2)}, u32[]{:S(2)}) collective-permute-start(bf16[2,2,32,2048]{3,2,1,0:T(8,128)(2,1)S(1)} %get-tuple-element.24.y_ref.y0), channel_id=1, source_target_pairs={{0,1},{1,0},{2,3},{3,2},{4,5},{5,4},{6,7},{7,6},{8,9},{9,8},{10,11... | collective-permute-start | bytes 1572872 | tf_op jit(solution)/shard_map/ppermute | solution.py:408
  69.2 7.9 %collective-permute-start.3 = (bf16[2,32,2048]{2,1,0:T(8,128)(2,1)S(1)}, bf16[2,32,2048]{2,1,0:T(8,128)(2,1)S(1)}, u32[]{:S(2)}, u32[]{:S(2)}) collective-permute-start(bf16[2,32,2048]{2,1,0:T(8,128)(2,1)S(1)} %slice_bitcast_fusion), channel_id=1, source_target_pairs={{0,6},{1,7},{2,0},{3,1},{4,2},{5,3},{6,4},{7,5},{8,14},{9,15},{10,... | collective-permute-start | bytes 786440 | tf_op jit(solution)/shard_map/ppermute | solution.py:410
  72.2 8.5 %collective-permute-start.2 = (bf16[2,32,2048]{2,1,0:T(8,128)(2,1)S(1)}, bf16[2,32,2048]{2,1,0:T(8,128)(2,1)S(1)}, u32[]{:S(2)}, u32[]{:S(2)}) collective-permute-start(bf16[2,32,2048]{2,1,0:T(8,128)(2,1)S(1)} %slice_bitcast_fusion.1), channel_id=1, source_target_pairs={{0,2},{1,3},{2,4},{3,5},{4,6},{5,7},{6,0},{7,1},{8,10},{9,11},{10,... | collective-permute-start | bytes 786440 | tf_op jit(solution)/shard_map/ppermute | solution.py:409
  72.3 32.8 %collective-permute-start.6 = (bf16[2,2,32,2048]{3,2,1,0:T(8,128)(2,1)S(1)}, bf16[2,2,32,2048]{3,2,1,0:T(8,128)(2,1)S(1)}, u32[]{:S(2)}, u32[]{:S(2)}) collective-permute-start(bf16[2,2,32,2048]{3,2,1,0:T(8,128)(2,1)S(1)} %collective-permute-done.1.yr), channel_id=1, source_target_pairs={{0,1},{1,0},{2,3},{3,2},{4,5},{5,4},{6,7},{7,6},{8,9},{9,8},{10,11... | collective-permute-start | bytes 1572872 | tf_op jit(solution)/shard_map/ppermute | solution.py:412
  72.4 32.7 %collective-permute-start.5 = (bf16[2,2,32,2048]{3,2,1,0:T(8,128)(2,1)S(1)}, bf16[2,2,32,2048]{3,2,1,0:T(8,128)(2,1)S(1)}, u32[]{:S(2)}, u32[]{:S(2)}) collective-permute-start(bf16[2,2,32,2048]{3,2,1,0:T(8,128)(2,1)S(1)} %collective-permute-done.y_ref.yl), channel_id=1, source_target_pairs={{0,1},{1,0},{2,3},{3,2},{4,5},{5,4},{6,7},{7,6},{8,9},{9,8},{10,11... | collective-permute-start | bytes 1572872 | tf_op jit(solution)/shard_map/ppermute | solution.py:411
  77.1 27.9 %collective-permute-start.8 = (bf16[2,32,2048]{2,1,0:T(8,128)(2,1)S(1)}, bf16[2,32,2048]{2,1,0:T(8,128)(2,1)S(1)}, u32[]{:S(2)}, u32[]{:S(2)}) collective-permute-start(bf16[2,32,2048]{2,1,0:T(8,128)(2,1)S(1)} %collective-permute-done.3.do), channel_id=1, source_target_pairs={{0,1},{1,0},{2,3},{3,2},{4,5},{5,4},{6,7},{7,6},{8,9},{9,8},{10,11... | collective-permute-start | bytes 786440 | tf_op jit(solution)/shard_map/ppermute | solution.py:414
  80.7 24.4 %collective-permute-start.7 = (bf16[2,32,2048]{2,1,0:T(8,128)(2,1)S(1)}, bf16[2,32,2048]{2,1,0:T(8,128)(2,1)S(1)}, u32[]{:S(2)}, u32[]{:S(2)}) collective-permute-start(bf16[2,32,2048]{2,1,0:T(8,128)(2,1)S(1)} %collective-permute-done.2.xo), channel_id=1, source_target_pairs={{0,1},{1,0},{2,3},{3,2},{4,5},{5,4},{6,7},{7,6},{8,9},{9,8},{10,11... | collective-permute-start | bytes 786440 | tf_op jit(solution)/shard_map/ppermute | solution.py:413
  96.3 8.8 %copy-start.1 = (bf16[2048,384]{1,0:T(8,128)(2,1)S(1)}, bf16[2048,384]{1,0:T(8,128)(2,1)}, u32[]{:S(2)}) copy-start(bf16[2048,384]{1,0:T(8,128)(2,1)} %w_ref.1) | copy-start | bytes 4718596
  96.3 8.8 %copy-start.3 = (bf16[2,256,384]{2,1,0:T(8,128)(2,1)S(1)}, bf16[2,256,384]{2,1,0:T(8,128)(2,1)}, u32[]{:S(2)}) copy-start(bf16[2,256,384]{2,1,0:T(8,128)(2,1)} %du_ref.1) | copy-start | bytes 1179652

commit v3 on v2

--- a/solution.py
+++ b/solution.py
@@ -7,62 +7,49 @@
 from jax.experimental.pallas import tpu as pltpu
 from jax.sharding import PartitionSpec as P
 
+
 EPS = 1e-6
 MESH = pl.DeviceIdType.MESH
 VMEM = pl.BlockSpec(memory_space=pltpu.VMEM)
 SMEM = pl.BlockSpec(memory_space=pltpu.SMEM)
 ANY = pl.BlockSpec(memory_space=pl.ANY)
+HBM = pl.BlockSpec(memory_space=pltpu.HBM)
 F32 = jnp.float32
 BF16 = jnp.bfloat16
 ROWS = 16
 SLOTS = 128
 
 
-def lookup(n, ids_ref, emb_ref, du_hbm, w_hbm, p_ref, d_ref, at_ref, row_ref, count_ref,
-           du_s, w_s, buf, pf, sem, in_sem):
+def lookup(n, ids_ref, emb_ref, p_ref, at_ref, row_ref, count_ref, buf, pf, found, sem):
     me = lax.axis_index("tp")
     k, t = ids_ref.shape
     h = t // n
     d = emb_ref.shape[2]
     vl = emb_ref.shape[0] * 8
     lo = me * vl
-    loads = [pltpu.make_async_copy(du_hbm, du_s, in_sem.at[0]), pltpu.make_async_copy(w_hbm, w_s, in_sem.at[1])]
-    for c in loads:
-        c.start()
-
-    def find(m, owner, cnt):
-        def one(j, cnt):
-            v = ids_ref[m, owner * h + j] - lo
-            own = (v >= 0) & (v < vl)
-
-            @pl.when(own)
-            def _():
-                pltpu.make_async_copy(emb_ref.at[v // 8], buf.at[cnt], sem).start()
-                at_ref[cnt] = owner * (k * h) + m * h + j
-                row_ref[cnt] = v
-
-            return cnt + own.astype(jnp.int32)
-
-        return lax.fori_loop(0, h, one, cnt, unroll=8)
 
     cnt = jnp.int32(0)
     for m in range(k):
-        cnt = lax.fori_loop(0, n, functools.partial(lambda m, o, c: find(m, o, c), m), cnt)
+        def find(i, cnt):
+            v = ids_ref[m, i]
+            found[cnt] = i
+            return cnt + ((v >= lo) & (v < lo + vl)).astype(jnp.int32)
+
+        first = cnt
+        cnt = lax.fori_loop(0, t, find, first, unroll=16)
+
+        def fetch(c, _):
+            i = found[c]
+            v = ids_ref[m, i] - lo
+            pltpu.make_async_copy(emb_ref.at[v // 8], buf.at[c], sem).start()
+            at_ref[c] = (i // h) * (k * h) + m * h + i % h
+            row_ref[c] = v
+            return 0
+
+        lax.fori_loop(first, cnt, fetch, 0)
     count_ref[0] = cnt
 
     pf[...] = jnp.zeros_like(pf)
-    for c in loads:
-        c.wait()
-    cw = 512
-    for m in range(k):
-        def cols(i, _):
-            c0 = pl.multiple_of(i * cw, cw)
-            v = lax.dot_general(du_s[m], w_s[pl.ds(c0, cw), :], (((1,), (1,)), ((), ())), preferred_element_type=F32)
-            d_ref[:, m * h:(m + 1) * h, pl.ds(c0, cw)] = v.astype(BF16).reshape(n, h, cw)
-            return 0
-
-        lax.fori_loop(0, d // cw, cols, 0)
-
     sub = lax.broadcasted_iota(jnp.int32, (8, d), 0)
 
     def wait(i, _):
@@ -70,13 +57,19 @@
         return 0
 
     lax.fori_loop(0, cnt, wait, 0)
-
-    def place(i, _):
-        x8 = buf[i].astype(F32)
-        pf[pl.ds(at_ref[i], 1)] = jnp.sum(jnp.where(sub == row_ref[i] % 8, x8, 0.0), axis=0, keepdims=True)
-        return 0
-
-    lax.fori_loop(0, cnt, place, 0)
+    step = 4
+
+    def place(q, _):
+        rows = []
+        for u in range(step):
+            i = jnp.minimum(q * step + u, cnt - 1)
+            x8 = buf[i].astype(F32)
+            rows.append((at_ref[i], jnp.sum(jnp.where(sub == row_ref[i] % 8, x8, 0.0), axis=0, keepdims=True)))
+        for at, x in rows:
+            pf[pl.ds(at, 1)] = x
+        return 0
+
+    lax.fori_loop(0, (cnt + step - 1) // step, place, 0)
 
     def pack(i, _):
         r0 = pl.multiple_of(i * ROWS, ROWS)
@@ -86,8 +79,8 @@
     lax.fori_loop(0, (k * t) // ROWS, pack, 0)
 
 
-def exchange(n, p_ref, d_ref, g_ref, dres_ref, y_ref, dg_ref,
-             prx, prd, sx, sd, rx, rd, nh_s, rs_s, dgs,
+def exchange(n, p_ref, du_ref, w_ref, g_ref, dres_ref, y_ref, dg_ref,
+             d_ref, prx, prd, sx, sd, rx, rd, nh_s, rs_s, dgs,
              pxs, pxr, pds, pdr, xs_sem, xr_sem, ds_sem, dr_sem, gs_sem, gr_sem):
     me = lax.axis_index("tp")
     chips = n // 2
@@ -123,8 +116,8 @@
     def pair_d(j):
         send(d_ref.at[dev(j, False)], prd.at[j], pds.at[j], pdr.at[j], partner)
 
-    for f, j in ((pair_x, 2), (pair_d, 2), (pair_x, 1), (pair_x, 3), (pair_d, 1), (pair_d, 3), (pair_x, 0), (pair_d, 0)):
-        f(j)
+    for j in (2, 1, 3, 0):
+        pair_x(j)
 
     def ring(r, ss, rs, direction, chunk, src):
         send(src, r.at[direction, chunk], ss.at[direction, chunk], rs.at[direction, chunk],
@@ -152,8 +145,22 @@
         sd[j] = d_ref[dev(j, True)].astype(F32) + prd[j].astype(F32)
         first_hops(j, sd, rd, ds_sem, dr_sem)
 
-    for f, j in ((sum_x, 2), (sum_d, 2), (sum_x, 1), (sum_x, 3), (sum_d, 1), (sum_d, 3), (sum_x, 0), (sum_d, 0)):
-        f(j)
+    for j in (2, 1, 3):
+        sum_x(j)
+    cw = 512
+    for m in range(k):
+        def cols(i, _):
+            c0 = pl.multiple_of(i * cw, cw)
+            v = lax.dot_general(du_ref[m], w_ref[pl.ds(c0, cw), :], (((1,), (1,)), ((), ())), preferred_element_type=F32)
+            d_ref[:, m * h:(m + 1) * h, pl.ds(c0, cw)] = v.astype(BF16).reshape(n, h, cw)
+            return 0
+
+        lax.fori_loop(0, d // cw, cols, 0)
+    for j in (2, 1, 3, 0):
+        pair_d(j)
+    for j in (2, 1, 3, 0):
+        sum_d(j)
+    sum_x(0)
 
     arrived(rx.at[0, 0], xs_sem.at[0, 0], xr_sem.at[0, 0])
     sx[1, :h] = sx[1, :h] + rx[0, 0]
@@ -185,7 +192,7 @@
             nh_s[m, rows] = xf * rs
             rs_s[m, rows] = jnp.broadcast_to(rs, (ROWS, rs_s.shape[-1]))
 
-    gf = g_ref[...].astype(F32)
+    gf = g_ref[...].astype(F32).reshape(1, d)
     dg = jnp.zeros((1, d), F32)
 
     def grad(m, i):
@@ -262,8 +269,9 @@
         c.wait()
 
 
-def clear_rest(first, rows, y_ref, dg_ref, de_in, de_ref, z, sem):
-    del y_ref, dg_ref, de_in
+def clear_rest(first, rows, y_ref, dg_in, de_in, de_ref, dg_ref, z, sem):
+    del y_ref, de_in
+    dg_ref[...] = dg_in[...].reshape(dg_ref.shape)
     for c in zeros(z, de_ref, first, rows, sem):
         c.wait()
 
@@ -276,7 +284,7 @@
     chip, core = me // 2, me % 2
     k, h, d = xo.shape
     t = h * n
-    gf = g_ref[...].astype(F32)
+    gf = g_ref[...].astype(F32).reshape(1, d)
     pieces = []
     for c, parts in ((core, ((y0.at[0], y0.at[1]), (yl.at[0], yl.at[1]), (yr.at[0], yr.at[1]), (xo, do))),
                      (1 - core, ((p0.at[0], p0.at[1]), (pl_.at[0], pl_.at[1]), (pr.at[0], pr.at[1]), (pxo, pdo)))):
@@ -356,36 +364,35 @@
     to_partner = [(r, r ^ 1) for r in range(n)]
     dma = pltpu.SemaphoreType.DMA
 
-    def local(ids, emb, g, w, du, dres):
+    def step(ids, emb, g, w, du, dres):
         k, t = ids.shape
         vl, d = emb.shape
         f = w.shape[1]
         h = t // n
         kt = k * t
-        g2 = g.reshape(1, d)
         i32 = lambda *s: jax.ShapeDtypeStruct(s, jnp.int32)
         cost = lambda b: pl.CostEstimate(flops=0, bytes_accessed=b, transcendentals=0)
 
-        rows, part, at, row, count = pl.pallas_call(
+        rows, at, row, count = pl.pallas_call(
             functools.partial(lookup, n),
-            out_shape=(jax.ShapeDtypeStruct((kt, d), BF16), jax.ShapeDtypeStruct((n, k * h, d), BF16),
-                       i32(kt), i32(kt), i32(1)),
-            in_specs=[SMEM, ANY, ANY, ANY],
-            out_specs=(VMEM, VMEM, SMEM, SMEM, SMEM),
+            out_shape=(jax.ShapeDtypeStruct((kt, d), BF16), i32(kt), i32(kt), i32(1)),
+            in_specs=[SMEM, HBM],
+            out_specs=(VMEM, SMEM, SMEM, SMEM),
             scratch_shapes=[
-                pltpu.VMEM((k, t, f), BF16), pltpu.VMEM((d, f), BF16), pltpu.VMEM((kt, 8, d), BF16),
-                pltpu.VMEM((kt, d), F32), dma, dma((2,)),
+                pltpu.VMEM((kt, 8, d), BF16), pltpu.VMEM((kt, d), F32), pltpu.SMEM((kt + 1,), jnp.int32), dma,
             ],
             compiler_params=pltpu.CompilerParams(vmem_limit_bytes=32 << 20),
+            cost_estimate=cost(4 << 20),
             name="lookup",
-        )(ids, emb.reshape(vl // 8, 8, d), du, w)
+        )(ids, emb.reshape(vl // 8, 8, d))
 
         y, dg = pl.pallas_call(
             functools.partial(exchange, n),
             out_shape=(jax.ShapeDtypeStruct((2, k, h, d), BF16), jax.ShapeDtypeStruct((1, d), F32)),
-            in_specs=[VMEM] * 4,
+            in_specs=[VMEM] * 5,
             out_specs=(VMEM, VMEM),
             scratch_shapes=[
+                pltpu.VMEM((n, k * h, d), BF16),
                 pltpu.VMEM((chips, k * h, d), BF16),
                 pltpu.VMEM((chips, k * h, d), BF16),
                 pltpu.VMEM((chips, k * h, d), BF16),
@@ -399,19 +406,22 @@
                 dma((2, 3)), dma((2, 3)), dma((2, 2 + h // ROWS)), dma((2, 2 + h // ROWS)),
                 dma((n,)), dma((n,)),
             ],
-            compiler_params=pltpu.CompilerParams(collective_id=0, has_side_effects=True, vmem_limit_bytes=24 << 20),
+            compiler_params=pltpu.CompilerParams(collective_id=0, has_side_effects=True, vmem_limit_bytes=28 << 20),
             name="exchange",
-        )(rows.reshape(n, k * h, d), part, g2, dres)
-
-        yl = lax.ppermute(y, "tp", to_right)
-        yr = lax.ppermute(y, "tp", to_left)
-        py = lax.ppermute(y, "tp", to_partner)
-        xo = lax.ppermute(yl[0], "tp", to_right)
-        do = lax.ppermute(yr[1], "tp", to_left)
-        pyl = lax.ppermute(yl, "tp", to_partner)
-        pyr = lax.ppermute(yr, "tp", to_partner)
-        pxo = lax.ppermute(xo, "tp", to_partner)
-        pdo = lax.ppermute(do, "tp", to_partner)
+        )(rows.reshape(n, k * h, d), du, w, g, dres)
+
+        def move(v, perm):
+            return lax.ppermute(v, "tp", perm)
+
+        yl = move(y, to_right)
+        yr = move(y, to_left)
+        py = move(y, to_partner)
+        xo = move(yl[0], to_right)
+        do = move(yr[1], to_left)
+        pyl = move(yl, to_partner)
+        pyr = move(yr, to_partner)
+        pxo = move(xo, to_partner)
+        pdo = move(do, to_partner)
 
         zr = 512
         split = (vl * 5 // 8) // zr * zr
@@ -426,17 +436,16 @@
             cost_estimate=cost(split * d * 4),
             name="clear0",
         )(y, row, count)
-        dgf = dg.reshape(d)
-        de = pl.pallas_call(
+        de, dgf = pl.pallas_call(
             functools.partial(clear_rest, split, vl - split),
-            out_shape=de_shape,
-            in_specs=[ANY, ANY, ANY], out_specs=ANY,
+            out_shape=(de_shape, jax.ShapeDtypeStruct((d,), F32)),
+            in_specs=[ANY, VMEM, ANY], out_specs=(ANY, VMEM),
             input_output_aliases={2: 0},
             scratch_shapes=[pltpu.VMEM((zr // 8, 8, d), F32), dma],
             compiler_params=pltpu.CompilerParams(vmem_limit_bytes=8 << 20),
             cost_estimate=cost((vl - split) * d * 4),
             name="clear1",
-        )(yl, dgf, de)
+        )(yl, dg, de)
 
         u, dw, de = pl.pallas_call(
             functools.partial(finish, n),
@@ -452,11 +461,11 @@
             ],
             compiler_params=pltpu.CompilerParams(vmem_limit_bytes=36 << 20),
             name="finish",
-        )(at, row, slot, block, count, blocks, y, yl, yr, xo, do, py, pyl, pyr, pxo, pdo, w, du, g2, de)
+        )(at, row, slot, block, count, blocks, y, yl, yr, xo, do, py, pyl, pyr, pxo, pdo, w, du, g, de)
         return u, x, de.reshape(vl, d), dw, dgf
 
     return jax.shard_map(
-        local,
+        step,
         mesh=mesh,
         in_specs=(P("dp", None), P("tp", None), P(None), P(None, "tp"), P("dp", None, "tp"), P("dp", "tp", None)),
         out_specs=(P("dp", None, "tp"), P("dp", "tp", None), P(("dp", "tp"), None), P(None, ("dp", "tp")), P("dp")),

time: 120 us -> 111 us (0.925)
  Pallas kernels: 88.7 us -> 83.4 us
  local copies, waits for them, and re-layouts: 4.43 us -> 0.88 us
    pallas_call x5, Pallas kernels: 88.7 us -> 83.4 us  [the longest x1 35.9 us: step(): pl.pallas_call(functools.partial(exchange, n), out_shape=(jax.ShapeDtypeS...]
    unnamed x13 -> x10, local copies, waits for them, and re-layouts: 3.7 us -> 0.84 us
  transfers between devices with their start and end apart: 9 -> 9, of which waited for: 3 -> 3; matrix products, arithmetic and copies ran while one was open for 0% -> 0% of each run, Pallas kernels for 20% -> 23%
where the time goes in v3:
time: 111 us
  Pallas kernels  83.4 us (75%)
  waiting for transfers between devices  19.7 us (18%)
  starting transfers between devices  5.75 us (5%)
    pallas_call x1, Pallas kernels, step(): pl.pallas_call(functools.partial(exchange, n), out_shape=(jax.ShapeDtypeS...  35.9 us
    ppermute x9, waiting for transfers between devices, move(): return lax.ppermute(v, 'tp', perm)  19.7 us
    pallas_call x1, Pallas kernels, step(): pl.pallas_call(functools.partial(clear_and_list, split), out_shape=(de_sh...  15.7 us
    pallas_call x1, Pallas kernels, step(): pl.pallas_call(functools.partial(finish, n), out_shape=(jax.ShapeDtypeStr...  13.4 us
    pallas_call x1, Pallas kernels, step(): pl.pallas_call(functools.partial(clear_rest, split, vl - split), out_shap...  9.32 us
    pallas_call x1, Pallas kernels, step(): pl.pallas_call(functools.partial(lookup, n), out_shape=(jax.ShapeDtypeStr...  9.13 us
    ppermute x9, starting transfers between devices, move(): return lax.ppermute(v, 'tp', perm)  5.75 us
  transfers between devices with their start and end apart: 9, of which 3 were waited for; matrix products, arithmetic and copies ran while one was open for 0% of the time, Pallas kernels for 23%

profile of v3, /device:TPU:112, one launch (start us, length us, event | category | flops | bytes accessed | tf_op | source)
XLA Modules:
  0.0 110.6 jit_solution(10647523516209755907)
XLA Ops:
  0.6 0.0 copy-start.1
  0.6 0.0 copy-start
  0.7 0.0 copy-start.3
  0.7 0.0 copy-start.2
  0.7 0.8 copy-done.4
  1.5 9.1 %lookup.1 = (bf16[512,2048]{1,0:T(8,128)(2,1)S(1)}, s32[512]{0:T(512)S(1)}, s32[512]{0:T(512)S(1)}, s32[1]{0:T(128)}) custom-call(s32[2,256]{1,0:T(2,128)S(1)} %copy-done.4, bf16[1024,8,2048]{2,1,0:T(8,128)(2,1)} %bitcast.8), custom_call_target="tpu_custom_call" | custom-call | bytes 4194304 | tf_op jit(solution)/shard_map/lookup/pallas_call | solution.py:376
  10.6 0.0 copy-done.1
  10.7 0.0 copy-done
  10.7 0.0 copy-done.3
  10.7 0.0 copy-done.2
  10.7 35.9 %exchange.1 = (bf16[2,2,32,2048]{3,2,1,0:T(8,128)(2,1)S(1)}, f32[1,2048]{1,0:T(1,128)S(1)}) custom-call(bf16[8,64,2048]{2,1,0:T(8,128)(2,1)S(1)} %bitcast.7, bf16[2,256,384]{2,1,0:T(8,128)(2,1)S(1)} %copy-done.1, bf16[2048,384]{1,0:T(8,128)(2,1)S(1)} %copy-done, bf16[2048]{0:T(1024)(128)(2,1)S(1)} %copy-done.3, bf16[2,32,2048]{2,1,0:T(8,128)(2,1)S(1)} %copy-done.2), custom_call_target="tpu_custom_call" | custom-call | tf_op jit(solution)/shard_map/exchange/pallas_call | solution.py:389
  46.6 1.8 %collective-permute-start.1 = (bf16[2,2,32,2048]{3,2,1,0:T(8,128)(2,1)S(1)}, bf16[2,2,32,2048]{3,2,1,0:T(8,128)(2,1)S(1)}, u32[]{:S(2)}, u32[]{:S(2)}) collective-permute-start(bf16[2,2,32,2048]{3,2,1,0:T(8,128)(2,1)S(1)} %get-tuple-element.24.y_ref.y0), channel_id=1, source_target_pairs={{0,6},{1,7},{2,0},{3,1},{4,2},{5,3},{6,4},{7,5},{8,14},{9,15},{10,... | collective-permute-start | bytes 1572872 | tf_op jit(solution)/shard_map/ppermute | solution.py:414
  48.3 0.3 collective-permute-start
  48.7 0.0 collective-permute-start.4
  48.7 11.9 %collective-permute-done.1.yr = bf16[2,2,32,2048]{3,2,1,0:T(8,128)(2,1)S(1)} collective-permute-done((bf16[2,2,32,2048]{3,2,1,0:T(8,128)(2,1)S(1)}, bf16[2,2,32,2048]{3,2,1,0:T(8,128)(2,1)S(1)}, u32[]{:S(2)}, u32[]{:S(2)}) %collective-permute-start.1) | collective-permute-done | bytes 524320 | tf_op jit(solution)/shard_map/ppermute | solution.py:414
  60.6 3.0 %collective-permute-start.3 = (bf16[2,32,2048]{2,1,0:T(8,128)(2,1)S(1)}, bf16[2,32,2048]{2,1,0:T(8,128)(2,1)S(1)}, u32[]{:S(2)}, u32[]{:S(2)}) collective-permute-start(bf16[2,32,2048]{2,1,0:T(8,128)(2,1)S(1)} %slice_bitcast_fusion), channel_id=1, source_target_pairs={{0,6},{1,7},{2,0},{3,1},{4,2},{5,3},{6,4},{7,5},{8,14},{9,15},{10,... | collective-permute-start | bytes 786440 | tf_op jit(solution)/shard_map/ppermute | solution.py:414
  63.6 0.0 collective-permute-done.y_ref.yl
  63.6 0.1 collective-permute-start.2
  63.7 0.1 collective-permute-start.6
  63.8 0.5 collective-permute-start.5
  64.3 4.3 %collective-permute-done.3.do = bf16[2,32,2048]{2,1,0:T(8,128)(2,1)S(1)} collective-permute-done((bf16[2,32,2048]{2,1,0:T(8,128)(2,1)S(1)}, bf16[2,32,2048]{2,1,0:T(8,128)(2,1)S(1)}, u32[]{:S(2)}, u32[]{:S(2)}) %collective-permute-start.3) | collective-permute-done | bytes 262176 | tf_op jit(solution)/shard_map/ppermute | solution.py:414
  68.6 0.0 collective-permute-start.8
  68.6 3.5 %collective-permute-done.2.xo = bf16[2,32,2048]{2,1,0:T(8,128)(2,1)S(1)} collective-permute-done((bf16[2,32,2048]{2,1,0:T(8,128)(2,1)S(1)}, bf16[2,32,2048]{2,1,0:T(8,128)(2,1)S(1)}, u32[]{:S(2)}, u32[]{:S(2)}) %collective-permute-start.2) | collective-permute-done | bytes 262176 | tf_op jit(solution)/shard_map/ppermute | solution.py:414
  72.1 0.0 collective-permute-start.7
  72.1 15.7 %clear0.1 = (f32[1024,8,2048]{2,1,0:T(8,128)}, bf16[2,32,2048]{2,1,0:T(8,128)(2,1)}, s32[512]{0:T(512)S(1)}, s32[512]{0:T(512)S(1)}, s32[1]{0:T(128)}) custom-call(bf16[2,2,32,2048]{3,2,1,0:T(8,128)(2,1)S(1)} %get-tuple-element.24.y_ref.y0, s32[512]{0:T(512)S(1)} %get-tuple-element.22.row_ref, s32[1]{0:T(128)} %get-tuple-element.25.count_ref), custom_call_target="tpu_custom_call" | custom-call | bytes 41943040 | tf_op jit(solution)/shard_map/clear0/pallas_call | solution.py:429
  87.8 9.3 %clear1.1 = (f32[1024,8,2048]{2,1,0:T(8,128)}, f32[2048]{0:T(1024)}) custom-call(bf16[2,2,32,2048]{3,2,1,0:T(8,128)(2,1)S(1)} %collective-permute-done.y_ref.yl, f32[1,2048]{1,0:T(1,128)S(1)} %get-tuple-element.29.dg_in, f32[1024,8,2048]{2,1,0:T(8,128)} %get-tuple-element.30.de_in), custom_call_target="tpu_custom_call", output_to_operand_aliasing={{0}: (2, {})} | custom-call | bytes 25165824 | tf_op jit(solution)/shard_map/clear1/pallas_call | solution.py:439
  97.1 0.0 collective-permute-done.4.p0
  97.1 0.0 collective-permute-done.8.pdo
  97.1 0.0 collective-permute-done.6.pr
  97.2 0.0 collective-permute-done.7.pxo
  97.2 0.0 collective-permute-done.5.pl_
  97.2 13.4 %finish.1 = (bf16[2,256,384]{2,1,0:T(8,128)(2,1)}, f32[2048,384]{1,0:T(8,128)}, f32[1024,8,2048]{2,1,0:T(8,128)}) custom-call(s32[512]{0:T(512)S(1)} %get-tuple-element.21.at_ref, s32[512]{0:T(512)S(1)} %get-tuple-element.22.row_ref, s32[512]{0:T(512)S(1)} %get-tuple-element.26.slot_ref, ...), custom_call_target="tpu_custom_call", output_to_operand_aliasing={{2}: (19, {})} | custom-call | tf_op jit(solution)/shard_map/finish/pallas_call | solution.py:450
  (3 shorter events, 0.0 us)
Async XLA Ops:
  0.6 10.0 %copy-start.1 = (bf16[2,256,384]{2,1,0:T(8,128)(2,1)S(1)}, bf16[2,256,384]{2,1,0:T(8,128)(2,1)}, u32[]{:S(2)}) copy-start(bf16[2,256,384]{2,1,0:T(8,128)(2,1)} %du_ref.3) | copy-start | bytes 1179652
  0.6 10.0 %copy-start = (bf16[2048,384]{1,0:T(8,128)(2,1)S(1)}, bf16[2048,384]{1,0:T(8,128)(2,1)}, u32[]{:S(2)}) copy-start(bf16[2048,384]{1,0:T(8,128)(2,1)} %w_ref.3) | copy-start | bytes 4718596
  0.7 10.0 %copy-start.3 = (bf16[2048]{0:T(1024)(128)(2,1)S(1)}, bf16[2048]{0:T(1024)(128)(2,1)}, u32[]{:S(2)}) copy-start(bf16[2048]{0:T(1024)(128)(2,1)} %g_ref.3) | copy-start | bytes 12292
  0.7 10.0 %copy-start.2 = (bf16[2,32,2048]{2,1,0:T(8,128)(2,1)S(1)}, bf16[2,32,2048]{2,1,0:T(8,128)(2,1)}, u32[]{:S(2)}) copy-start(bf16[2,32,2048]{2,1,0:T(8,128)(2,1)} %dres_ref.1) | copy-start | bytes 786436
  0.7 0.8 copy-start.4
  46.6 14.0 %collective-permute-start.1 = (bf16[2,2,32,2048]{3,2,1,0:T(8,128)(2,1)S(1)}, bf16[2,2,32,2048]{3,2,1,0:T(8,128)(2,1)S(1)}, u32[]{:S(2)}, u32[]{:S(2)}) collective-permute-start(bf16[2,2,32,2048]{3,2,1,0:T(8,128)(2,1)S(1)} %get-tuple-element.24.y_ref.y0), channel_id=1, source_target_pairs={{0,6},{1,7},{2,0},{3,1},{4,2},{5,3},{6,4},{7,5},{8,14},{9,15},{10,... | collective-permute-start | bytes 1572872 | tf_op jit(solution)/shard_map/ppermute | solution.py:414
  48.3 15.3 %collective-permute-start = (bf16[2,2,32,2048]{3,2,1,0:T(8,128)(2,1)S(1)}, bf16[2,2,32,2048]{3,2,1,0:T(8,128)(2,1)S(1)}, u32[]{:S(2)}, u32[]{:S(2)}) collective-permute-start(bf16[2,2,32,2048]{3,2,1,0:T(8,128)(2,1)S(1)} %get-tuple-element.24.y_ref.y0), channel_id=1, source_target_pairs={{0,2},{1,3},{2,4},{3,5},{4,6},{5,7},{6,0},{7,1},{8,10},{9,11},{10,... | collective-permute-start | bytes 1572872 | tf_op jit(solution)/shard_map/ppermute | solution.py:414
  48.7 48.4 %collective-permute-start.4 = (bf16[2,2,32,2048]{3,2,1,0:T(8,128)(2,1)S(1)}, bf16[2,2,32,2048]{3,2,1,0:T(8,128)(2,1)S(1)}, u32[]{:S(2)}, u32[]{:S(2)}) collective-permute-start(bf16[2,2,32,2048]{3,2,1,0:T(8,128)(2,1)S(1)} %get-tuple-element.24.y_ref.y0), channel_id=1, source_target_pairs={{0,1},{1,0},{2,3},{3,2},{4,5},{5,4},{6,7},{7,6},{8,9},{9,8},{10,11... | collective-permute-start | bytes 1572872 | tf_op jit(solution)/shard_map/ppermute | solution.py:414
  60.6 8.0 %collective-permute-start.3 = (bf16[2,32,2048]{2,1,0:T(8,128)(2,1)S(1)}, bf16[2,32,2048]{2,1,0:T(8,128)(2,1)S(1)}, u32[]{:S(2)}, u32[]{:S(2)}) collective-permute-start(bf16[2,32,2048]{2,1,0:T(8,128)(2,1)S(1)} %slice_bitcast_fusion), channel_id=1, source_target_pairs={{0,6},{1,7},{2,0},{3,1},{4,2},{5,3},{6,4},{7,5},{8,14},{9,15},{10,... | collective-permute-start | bytes 786440 | tf_op jit(solution)/shard_map/ppermute | solution.py:414
  63.6 8.5 %collective-permute-start.2 = (bf16[2,32,2048]{2,1,0:T(8,128)(2,1)S(1)}, bf16[2,32,2048]{2,1,0:T(8,128)(2,1)S(1)}, u32[]{:S(2)}, u32[]{:S(2)}) collective-permute-start(bf16[2,32,2048]{2,1,0:T(8,128)(2,1)S(1)} %slice_bitcast_fusion.1), channel_id=1, source_target_pairs={{0,2},{1,3},{2,4},{3,5},{4,6},{5,7},{6,0},{7,1},{8,10},{9,11},{10,... | collective-permute-start | bytes 786440 | tf_op jit(solution)/shard_map/ppermute | solution.py:414
  63.7 33.4 %collective-permute-start.6 = (bf16[2,2,32,2048]{3,2,1,0:T(8,128)(2,1)S(1)}, bf16[2,2,32,2048]{3,2,1,0:T(8,128)(2,1)S(1)}, u32[]{:S(2)}, u32[]{:S(2)}) collective-permute-start(bf16[2,2,32,2048]{3,2,1,0:T(8,128)(2,1)S(1)} %collective-permute-done.1.yr), channel_id=1, source_target_pairs={{0,1},{1,0},{2,3},{3,2},{4,5},{5,4},{6,7},{7,6},{8,9},{9,8},{10,11... | collective-permute-start | bytes 1572872 | tf_op jit(solution)/shard_map/ppermute | solution.py:414
  63.8 33.3 %collective-permute-start.5 = (bf16[2,2,32,2048]{3,2,1,0:T(8,128)(2,1)S(1)}, bf16[2,2,32,2048]{3,2,1,0:T(8,128)(2,1)S(1)}, u32[]{:S(2)}, u32[]{:S(2)}) collective-permute-start(bf16[2,2,32,2048]{3,2,1,0:T(8,128)(2,1)S(1)} %collective-permute-done.y_ref.yl), channel_id=1, source_target_pairs={{0,1},{1,0},{2,3},{3,2},{4,5},{5,4},{6,7},{7,6},{8,9},{9,8},{10,11... | collective-permute-start | bytes 1572872 | tf_op jit(solution)/shard_map/ppermute | solution.py:414
  68.6 28.5 %collective-permute-start.8 = (bf16[2,32,2048]{2,1,0:T(8,128)(2,1)S(1)}, bf16[2,32,2048]{2,1,0:T(8,128)(2,1)S(1)}, u32[]{:S(2)}, u32[]{:S(2)}) collective-permute-start(bf16[2,32,2048]{2,1,0:T(8,128)(2,1)S(1)} %collective-permute-done.3.do), channel_id=1, source_target_pairs={{0,1},{1,0},{2,3},{3,2},{4,5},{5,4},{6,7},{7,6},{8,9},{9,8},{10,11... | collective-permute-start | bytes 786440 | tf_op jit(solution)/shard_map/ppermute | solution.py:414
  72.1 25.0 %collective-permute-start.7 = (bf16[2,32,2048]{2,1,0:T(8,128)(2,1)S(1)}, bf16[2,32,2048]{2,1,0:T(8,128)(2,1)S(1)}, u32[]{:S(2)}, u32[]{:S(2)}) collective-permute-start(bf16[2,32,2048]{2,1,0:T(8,128)(2,1)S(1)} %collective-permute-done.2.xo), channel_id=1, source_target_pairs={{0,1},{1,0},{2,3},{3,2},{4,5},{5,4},{6,7},{7,6},{8,9},{9,8},{10,11... | collective-permute-start | bytes 786440 | tf_op jit(solution)/shard_map/ppermute | solution.py:414

commit v4 on v3

--- a/solution.py
+++ b/solution.py
@@ -20,7 +20,11 @@
 SLOTS = 128
 
 
-def lookup(n, ids_ref, emb_ref, p_ref, at_ref, row_ref, count_ref, buf, pf, found, sem):
+def slab(i, m, k, h):
+    return lax.div(i, h) * (k * h) + m * h + lax.rem(i, h)
+
+
+def lookup(n, ids_ref, emb_ref, p_ref, buf, pf, found, at_s, row_s, sem):
     me = lax.axis_index("tp")
     k, t = ids_ref.shape
     h = t // n
@@ -41,13 +45,12 @@
         def fetch(c, _):
             i = found[c]
             v = ids_ref[m, i] - lo
-            pltpu.make_async_copy(emb_ref.at[v // 8], buf.at[c], sem).start()
-            at_ref[c] = (i // h) * (k * h) + m * h + i % h
-            row_ref[c] = v
+            pltpu.make_async_copy(emb_ref.at[lax.div(v, 8)], buf.at[c], sem).start()
+            at_s[c] = slab(i, m, k, h)
+            row_s[c] = lax.rem(v, 8)
             return 0
 
         lax.fori_loop(first, cnt, fetch, 0)
-    count_ref[0] = cnt
 
     pf[...] = jnp.zeros_like(pf)
     sub = lax.broadcasted_iota(jnp.int32, (8, d), 0)
@@ -64,12 +67,12 @@
         for u in range(step):
             i = jnp.minimum(q * step + u, cnt - 1)
             x8 = buf[i].astype(F32)
-            rows.append((at_ref[i], jnp.sum(jnp.where(sub == row_ref[i] % 8, x8, 0.0), axis=0, keepdims=True)))
+            rows.append((at_s[i], jnp.sum(jnp.where(sub == row_s[i], x8, 0.0), axis=0, keepdims=True)))
         for at, x in rows:
             pf[pl.ds(at, 1)] = x
         return 0
 
-    lax.fori_loop(0, (cnt + step - 1) // step, place, 0)
+    lax.fori_loop(0, lax.div(cnt + step - 1, step), place, 0)
 
     def pack(i, _):
         r0 = pl.multiple_of(i * ROWS, ROWS)
@@ -234,70 +237,131 @@
 def zeros(z, de_ref, first, rows, sem):
     zr = z.shape[0]
     z[...] = jnp.zeros_like(z)
-    cs = [pltpu.make_async_copy(z, de_ref.at[pl.ds(first // 8 + i * zr, zr)], sem)
-          for i in range(rows // (8 * zr))]
+    cs = [pltpu.make_async_copy(z, de_ref.at[pl.ds(first // 8 + i * zr, zr)], sem) for i in range(rows // (8 * zr))]
     for c in cs:
         c.start()
     return cs
 
 
-def clear_and_list(rows, y_ref, row_ref, count_ref, de_ref, x_ref, slot_ref, block_ref, blocks_ref, z, table, sem, x_sem):
+def clear_and_list(n, rows, y_ref, ids_hbm, de_ref, x_ref, plan_ref, z, ids, found, table, plan, sem, x_sem, s_sem):
+    load = pltpu.make_async_copy(ids_hbm, ids, s_sem.at[0])
+    load.start()
     cs = zeros(z, de_ref, 0, rows, sem)
     out = pltpu.make_async_copy(y_ref.at[0], x_ref, x_sem)
     out.start()
+    k, t = ids.shape
+    h, kt = t // n, k * t
+    vl = de_ref.shape[0] * 8
+    lo = lax.axis_index("tp") * vl
 
     def reset(i, _):
         table[i] = -1
         return 0
 
     lax.fori_loop(0, table.shape[0], reset, 0, unroll=8)
-    base = lax.axis_index("tp") * 0
-
-    def one(i, used):
-        b = row_ref[i] // 8
-        s = table[b]
-        fresh = s < 0
-        s = jnp.where(fresh, used, s)
-        table[b] = s
-        block_ref[s] = b
-        slot_ref[i] = s * 2 + fresh.astype(jnp.int32)
-        return used + fresh.astype(jnp.int32)
-
-    blocks_ref[0] = lax.fori_loop(0, count_ref[0], one, base)
+    load.wait()
+    cnt, used = jnp.int32(0), jnp.int32(0)
+    for m in range(k):
+        def find(i, cnt):
+            v = ids[m, i]
+            found[cnt] = i
+            return cnt + ((v >= lo) & (v < lo + vl)).astype(jnp.int32)
+
+        first = cnt
+        cnt = lax.fori_loop(0, t, find, first, unroll=16)
+
+        def one(c, used):
+            i = found[c]
+            v = ids[m, i] - lo
+            b = lax.div(v, 8)
+            s = table[b]
+            fresh = (s < 0).astype(jnp.int32)
+            s = jnp.where(s < 0, used, s)
+            table[b] = s
+            plan[c] = slab(i, m, k, h)
+            plan[kt + c] = s * 16 + lax.rem(v, 8) * 2 + fresh
+            plan[2 * kt + s] = b
+            return used + fresh
+
+        used = lax.fori_loop(first, cnt, one, used)
+    plan[3 * kt] = cnt
+    plan[3 * kt + 1] = used
+    store = pltpu.make_async_copy(plan, plan_ref, s_sem.at[1])
+    store.start()
+    store.wait()
     out.wait()
     for c in cs:
         c.wait()
 
 
-def clear_rest(first, rows, y_ref, dg_in, de_in, de_ref, dg_ref, z, sem):
-    del y_ref, de_in
-    dg_ref[...] = dg_in[...].reshape(dg_ref.shape)
-    for c in zeros(z, de_ref, first, rows, sem):
-        c.wait()
-
-
-def finish(n, at_ref, row_ref, slot_ref, block_ref, count_ref, blocks_ref, y0, yl, yr, xo, do, p0, pl_, pr, pxo, pdo,
-           w_ref, du_ref, g_ref, de_in, u_ref, dw_ref, de_ref, n_s, dxf, acc, sem):
-    del de_in
+def project(parts, w_ref, du_ref, g_ref, u_ref, n_g, du_g, u_g, u_sem, emit):
+    _, x0 = parts[0]
+    k, h, d = x0.shape
+    gf = g_ref[...].astype(F32).reshape(1, d)
+    for p, (owner, x) in enumerate(parts):
+        for m in range(k):
+            base = p * (k * h) + m * h
+            du_g[base:base + h] = du_ref[m, pl.ds(pl.multiple_of(owner * h, h), h)]
+            for s in range(h // ROWS):
+                xf = x[m, pl.ds(s * ROWS, ROWS)].astype(F32)
+                rs = lax.rsqrt(jnp.mean(xf * xf, axis=-1, keepdims=True) + EPS)
+                n_g[base + s * ROWS:base + (s + 1) * ROWS] = ((xf * rs) * gf).astype(BF16)
+    u_g[...] = jnp.dot(n_g[...], w_ref[...], preferred_element_type=F32).astype(BF16)
+    cs = []
+    for p, (owner, _) in enumerate(parts):
+        for m in range(k):
+            cs.append(pltpu.make_async_copy(u_g.at[pl.ds(p * (k * h) + m * h, h)],
+                                            u_ref.at[m, pl.ds(pl.multiple_of(owner * h, h), h)], u_sem))
+    for c in cs:
+        c.start()
+    cw = 512
+    for i in range(d // cw):
+        emit(i, cw, lax.dot_general(n_g[:, i * cw:(i + 1) * cw], du_g[...], (((0,), (0,)), ((), ())),
+                                    preferred_element_type=F32))
+    return cs
+
+
+def near_and_far(n):
     me = lax.axis_index("tp")
     chips = n // 2
     chip, core = me // 2, me % 2
+    at = lambda off, c: ((chip + off) % chips) * 2 + c
+    near = [at(0, core), at(chips - 1, core), at(1, core), at(0, 1 - core)]
+    far = [at(2, core), at(chips - 1, 1 - core), at(1, 1 - core), at(2, 1 - core)]
+    return near, far
+
+
+def clear_rest(n, first, rows, y0, yl, yr, p0, w_ref, du_ref, g_ref, dg_in, de_in, de_ref, dg_ref, u_ref, dw_ref,
+               z, n_g, du_g, u_g, sem, u_sem):
+    del de_in
+    cs = zeros(z, de_ref, first, rows, sem)
+    dg_ref[...] = dg_in[...].reshape(dg_ref.shape)
+
+    def emit(i, cw, v):
+        dw_ref[i * cw:(i + 1) * cw] = v
+
+    near, _ = near_and_far(n)
+    us = project([(o, v.at[0]) for o, v in zip(near, (y0, yl, yr, p0))], w_ref, du_ref, g_ref, u_ref,
+                 n_g, du_g, u_g, u_sem, emit)
+    for c in us + cs:
+        c.wait()
+
+
+def finish(n, plan, y0, yl, yr, p0, xo, do, pl_, pr, pxo, pdo, w_ref, du_ref, g_ref, dw_in, u_in, de_in,
+           u_ref, dw_ref, de_ref, dxf, acc, n_g, du_g, u_g, dw_s, sem, u_sem, w_sem):
+    del de_in, u_in
     k, h, d = xo.shape
-    t = h * n
-    gf = g_ref[...].astype(F32).reshape(1, d)
-    pieces = []
-    for c, parts in ((core, ((y0.at[0], y0.at[1]), (yl.at[0], yl.at[1]), (yr.at[0], yr.at[1]), (xo, do))),
-                     (1 - core, ((p0.at[0], p0.at[1]), (pl_.at[0], pl_.at[1]), (pr.at[0], pr.at[1]), (pxo, pdo)))):
-        for off, (x, dx) in zip((0, chips - 1, 1, 2), parts):
-            pieces.append((((chip + off) % chips) * 2 + c, x, dx))
-
-    for owner, _, dx in pieces:
+    kt = k * h * n
+    near, far = near_and_far(n)
+    dxs = list(zip(near, (y0.at[1], yl.at[1], yr.at[1], p0.at[1]))) + list(zip(far, (do, pl_.at[1], pr.at[1], pdo)))
+    for owner, dx in dxs:
         for m in range(k):
             for s in range(h // ROWS):
                 dxf[pl.ds(pl.multiple_of(owner * (k * h) + m * h + s * ROWS, ROWS), ROWS)] = dx[m, pl.ds(s * ROWS, ROWS)].astype(F32)
 
     sub = lax.broadcasted_iota(jnp.int32, (8, d), 0)
-    cnt, used = count_ref[0], blocks_ref[0]
+    cnt, used = plan[3 * kt], plan[3 * kt + 1]
+    step = 4
 
     def drain(i, _):
         pltpu.make_async_copy(acc.at[0], de_ref.at[0], sem).wait()
@@ -308,51 +372,43 @@
         def _():
             lax.fori_loop(0, SLOTS, drain, 0)
 
-        def one(i, _):
-            code = slot_ref[i]
-            s = code // 2 - q * SLOTS
-
-            @pl.when((s >= 0) & (s < SLOTS))
-            def _():
-                row = jnp.where(sub == row_ref[i] % 8, jnp.broadcast_to(dxf[pl.ds(at_ref[i], 1)], (8, d)), 0.0)
-                acc[s] = row + jnp.where(code % 2 == 1, jnp.zeros((8, d), F32), acc[s])
-
+        def some(b, _):
+            todo = []
+            for e in range(step):
+                i = b * step + e
+                c = jnp.minimum(i, cnt - 1)
+                code = plan[kt + c]
+                s = (code >> 4) - q * SLOTS
+                s = jnp.where((i < cnt) & (s >= 0) & (s < SLOTS), s, SLOTS)
+                todo.append((s, (code >> 1) & 7, (code & 1) == 1, dxf[pl.ds(plan[c], 1)]))
+            for s, r, fresh, x in todo:
+                old = jnp.where(fresh, jnp.zeros((8, d), F32), acc[s])
+                acc[s] = old + jnp.where(sub == r, jnp.broadcast_to(x, (8, d)), 0.0)
             return 0
 
-        lax.fori_loop(0, cnt, one, 0)
+        lax.fori_loop(0, lax.div(cnt + step - 1, step), some, 0)
 
         def put(i, _):
-            pltpu.make_async_copy(acc.at[i], de_ref.at[block_ref[q * SLOTS + i]], sem).start()
+            pltpu.make_async_copy(acc.at[i], de_ref.at[plan[2 * kt + q * SLOTS + i]], sem).start()
             return 0
 
         lax.fori_loop(0, jnp.minimum(used - q * SLOTS, SLOTS), put, 0)
         return 0
 
-    turns = (used + SLOTS - 1) // SLOTS
+    turns = lax.div(used + SLOTS - 1, SLOTS)
     lax.fori_loop(0, turns, turn, 0)
 
-    for owner, x, _ in pieces:
-        for m in range(k):
-            for s in range(h // ROWS):
-                xf = x[m, pl.ds(s * ROWS, ROWS)].astype(F32)
-                rs = lax.rsqrt(jnp.mean(xf * xf, axis=-1, keepdims=True) + EPS)
-                n_s[pl.ds(pl.multiple_of(m * t + owner * h + s * ROWS, ROWS), ROWS)] = ((xf * rs) * gf).astype(BF16)
-
-    w = w_ref[...]
-    for m in range(k):
-        u_ref[m] = jnp.dot(n_s[m * t:(m + 1) * t], w, preferred_element_type=F32).astype(BF16)
-    cw = 512
-
-    def wgrad(i, _):
-        c0 = pl.multiple_of(i * cw, cw)
-        v = jnp.zeros((cw, w_ref.shape[1]), F32)
-        for m in range(k):
-            v = v + lax.dot_general(n_s[m * t:(m + 1) * t, pl.ds(c0, cw)], du_ref[m], (((0,), (0,)), ((), ())),
-                                    preferred_element_type=F32)
-        dw_ref[pl.ds(c0, cw)] = v
-        return 0
-
-    lax.fori_loop(0, d // cw, wgrad, 0)
+    ws = []
+
+    def emit(i, cw, v):
+        rows = pl.ds(i * cw, cw)
+        dw_s[rows] = dw_in[rows] + v
+        ws.append(pltpu.make_async_copy(dw_s.at[rows], dw_ref.at[rows], w_sem))
+        ws[-1].start()
+
+    us = project(list(zip(far, (xo, pl_.at[0], pr.at[0], pxo))), w_ref, du_ref, g_ref, u_ref, n_g, du_g, u_g, u_sem, emit)
+    for c in us + ws:
+        c.wait()
     lax.fori_loop(0, used - jnp.maximum(turns - 1, 0) * SLOTS, drain, 0)
 
 
@@ -373,13 +429,14 @@
         i32 = lambda *s: jax.ShapeDtypeStruct(s, jnp.int32)
         cost = lambda b: pl.CostEstimate(flops=0, bytes_accessed=b, transcendentals=0)
 
-        rows, at, row, count = pl.pallas_call(
+        rows = pl.pallas_call(
             functools.partial(lookup, n),
-            out_shape=(jax.ShapeDtypeStruct((kt, d), BF16), i32(kt), i32(kt), i32(1)),
+            out_shape=jax.ShapeDtypeStruct((kt, d), BF16),
             in_specs=[SMEM, HBM],
-            out_specs=(VMEM, SMEM, SMEM, SMEM),
+            out_specs=VMEM,
             scratch_shapes=[
-                pltpu.VMEM((kt, 8, d), BF16), pltpu.VMEM((kt, d), F32), pltpu.SMEM((kt + 1,), jnp.int32), dma,
+                pltpu.VMEM((kt, 8, d), BF16), pltpu.VMEM((kt, d), F32), pltpu.SMEM((kt + 1,), jnp.int32),
+                pltpu.SMEM((kt,), jnp.int32), pltpu.SMEM((kt,), jnp.int32), dma,
             ],
             compiler_params=pltpu.CompilerParams(vmem_limit_bytes=32 << 20),
             cost_estimate=cost(4 << 20),
@@ -423,45 +480,48 @@
         pxo = move(xo, to_partner)
         pdo = move(do, to_partner)
 
-        zr = 512
-        split = (vl * 5 // 8) // zr * zr
+        zr = 16
+        split = (vl * 5 // 8) // (8 * zr) * (8 * zr)
         de_shape = jax.ShapeDtypeStruct((vl // 8, 8, d), F32)
-        de, x, slot, block, blocks = pl.pallas_call(
-            functools.partial(clear_and_list, split),
-            out_shape=(de_shape, jax.ShapeDtypeStruct((k, h, d), BF16), i32(kt), i32(kt), i32(1)),
-            in_specs=[VMEM, SMEM, SMEM],
-            out_specs=(ANY, ANY, SMEM, SMEM, SMEM),
-            scratch_shapes=[pltpu.VMEM((zr // 8, 8, d), F32), pltpu.SMEM((vl // 8,), jnp.int32), dma, dma],
+        u_shape = jax.ShapeDtypeStruct((k, t, f), BF16)
+        dw_shape = jax.ShapeDtypeStruct((d, f), F32)
+        size = 3 * kt + 128
+        some = n // 2 * k * h
+        smem = lambda *s: pltpu.SMEM(s, jnp.int32)
+        group = [pltpu.VMEM((some, d), BF16), pltpu.VMEM((some, f), BF16), pltpu.VMEM((some, f), BF16)]
+        de, x, plan = pl.pallas_call(
+            functools.partial(clear_and_list, n, split),
+            out_shape=(de_shape, jax.ShapeDtypeStruct((k, h, d), BF16), i32(size)),
+            in_specs=[VMEM, ANY],
+            out_specs=(ANY, ANY, ANY),
+            scratch_shapes=[pltpu.VMEM((zr, 8, d), F32), smem(k, t), smem(kt + 1), smem(vl // 8), smem(size),
+                            dma, dma, dma((2,))],
             compiler_params=pltpu.CompilerParams(vmem_limit_bytes=8 << 20),
             cost_estimate=cost(split * d * 4),
             name="clear0",
-        )(y, row, count)
-        de, dgf = pl.pallas_call(
-            functools.partial(clear_rest, split, vl - split),
-            out_shape=(de_shape, jax.ShapeDtypeStruct((d,), F32)),
-            in_specs=[ANY, VMEM, ANY], out_specs=(ANY, VMEM),
-            input_output_aliases={2: 0},
-            scratch_shapes=[pltpu.VMEM((zr // 8, 8, d), F32), dma],
-            compiler_params=pltpu.CompilerParams(vmem_limit_bytes=8 << 20),
+        )(y, ids)
+        de, dgf, u, dwa = pl.pallas_call(
+            functools.partial(clear_rest, n, split, vl - split),
+            out_shape=(de_shape, jax.ShapeDtypeStruct((d,), F32), u_shape, dw_shape),
+            in_specs=[VMEM] * 8 + [ANY], out_specs=(ANY, VMEM, ANY, VMEM),
+            input_output_aliases={8: 0},
+            scratch_shapes=[pltpu.VMEM((zr, 8, d), F32)] + group + [dma, dma],
+            compiler_params=pltpu.CompilerParams(vmem_limit_bytes=12 << 20),
             cost_estimate=cost((vl - split) * d * 4),
             name="clear1",
-        )(yl, dg, de)
+        )(y, yl, yr, py, w, du, g, dg, de)
 
         u, dw, de = pl.pallas_call(
             functools.partial(finish, n),
-            out_shape=(jax.ShapeDtypeStruct((k, t, f), BF16), jax.ShapeDtypeStruct((d, f), F32), de_shape),
-            in_specs=[SMEM] * 6 + [VMEM] * 13 + [ANY],
-            out_specs=(VMEM, VMEM, ANY),
-            input_output_aliases={19: 2},
-            scratch_shapes=[
-                pltpu.VMEM((kt, d), BF16),
-                pltpu.VMEM((kt, d), F32),
-                pltpu.VMEM((SLOTS, 8, d), F32),
-                dma,
-            ],
-            compiler_params=pltpu.CompilerParams(vmem_limit_bytes=36 << 20),
+            out_shape=(u_shape, dw_shape, de_shape),
+            in_specs=[SMEM] + [VMEM] * 14 + [ANY, ANY],
+            out_specs=(ANY, ANY, ANY),
+            input_output_aliases={15: 0, 16: 2},
+            scratch_shapes=[pltpu.VMEM((kt, d), F32), pltpu.VMEM((SLOTS + 1, 8, d), F32)] + group
+                           + [pltpu.VMEM((d, f), F32), dma, dma, dma],
+            compiler_params=pltpu.CompilerParams(vmem_limit_bytes=28 << 20),
             name="finish",
-        )(at, row, slot, block, count, blocks, y, yl, yr, xo, do, py, pyl, pyr, pxo, pdo, w, du, g, de)
+        )(plan, y, yl, yr, py, xo, do, pyl, pyr, pxo, pdo, w, du, g, dwa, u, de)
         return u, x, de.reshape(vl, d), dw, dgf
 
     return jax.shard_map(

time: 111 us -> 103 us (0.928)
  Pallas kernels: 83.4 us -> 74.8 us
    pallas_call x4, Pallas kernels: 47.6 us -> 38.9 us  [the longest x1 13.5 us: step(): pl.pallas_call(functools.partial(clear_and_list, n, split), out_shape=(de...]
  transfers between devices with their start and end apart: 9 -> 9, of which waited for: 3 -> 3; matrix products, arithmetic and copies ran while one was open for 0% -> 0% of each run, Pallas kernels for 23% -> 24%
where the time goes in v4:
time: 103 us; the launch traced here: 102 us
  Pallas kernels  74.8 us (73%)
  waiting for transfers between devices  19.7 us (19%)
  starting transfers between devices  5.75 us (6%)
    pallas_call x1, Pallas kernels, step(): pl.pallas_call(functools.partial(exchange, n), out_shape=(jax.ShapeDtypeS...  36 us
    ppermute x9, waiting for transfers between devices, move(): return lax.ppermute(v, 'tp', perm)  19.7 us
    pallas_call x1, Pallas kernels, step(): pl.pallas_call(functools.partial(clear_and_list, n, split), out_shape=(de...  13.5 us
    pallas_call x1, Pallas kernels, step(): pl.pallas_call(functools.partial(clear_rest, n, split, vl - split), out_s...  10.5 us
    pallas_call x1, Pallas kernels, step(): pl.pallas_call(functools.partial(lookup, n), out_shape=jax.ShapeDtypeStru...  7.94 us
    pallas_call x1, Pallas kernels, step(): pl.pallas_call(functools.partial(finish, n), out_shape=(u_shape, dw_shape...  6.9 us
    ppermute x9, starting transfers between devices, move(): return lax.ppermute(v, 'tp', perm)  5.75 us
  transfers between devices with their start and end apart: 9, of which 3 were waited for; matrix products, arithmetic and copies ran while one was open for 0% of the time, Pallas kernels for 24%

profile of v4, /device:TPU:112, one launch (start us, length us, event | category | flops | bytes accessed | tf_op | source)
XLA Modules:
  0.0 102.0 jit_solution(1818353397686940544)
XLA Ops:
  0.6 0.0 copy-start.1
  0.6 0.0 copy-start
  0.7 0.0 copy-start.3
  0.7 0.0 copy-start.2
  0.7 0.0 copy-start.4
  0.7 0.8 copy-done.4
  1.5 7.9 %lookup.1 = bf16[512,2048]{1,0:T(8,128)(2,1)S(1)} custom-call(s32[2,256]{1,0:T(2,128)S(1)} %copy-done.4, bf16[1024,8,2048]{2,1,0:T(8,128)(2,1)} %bitcast.8), custom_call_target="tpu_custom_call" | custom-call | bytes 4194304 | tf_op jit(solution)/shard_map/lookup/pallas_call | solution.py:432
  9.5 0.0 copy-done.1
  9.5 0.0 copy-done
  9.5 0.0 copy-done.3
  9.5 36.0 %exchange.1 = (bf16[2,2,32,2048]{3,2,1,0:T(8,128)(2,1)S(1)}, f32[1,2048]{1,0:T(1,128)S(1)}) custom-call(bf16[8,64,2048]{2,1,0:T(8,128)(2,1)S(1)} %bitcast.7, bf16[2,256,384]{2,1,0:T(8,128)(2,1)S(1)} %copy-done.1, bf16[2048,384]{1,0:T(8,128)(2,1)S(1)} %copy-done, bf16[2048]{0:T(1024)(128)(2,1)S(1)} %copy-done.3, bf16[2,32,2048]{2,1,0:T(8,128)(2,1)S(1)} %copy-done.2), custom_call_target="tpu_custom_call" | custom-call | tf_op jit(solution)/shard_map/exchange/pallas_call | solution.py:446
  45.5 1.8 %collective-permute-start.1 = (bf16[2,2,32,2048]{3,2,1,0:T(8,128)(2,1)S(1)}, bf16[2,2,32,2048]{3,2,1,0:T(8,128)(2,1)S(1)}, u32[]{:S(2)}, u32[]{:S(2)}) collective-permute-start(bf16[2,2,32,2048]{3,2,1,0:T(8,128)(2,1)S(1)} %get-tuple-element.17.y_ref.y0), channel_id=1, source_target_pairs={{0,6},{1,7},{2,0},{3,1},{4,2},{5,3},{6,4},{7,5},{8,14},{9,15},{10,... | collective-permute-start | bytes 1572872 | tf_op jit(solution)/shard_map/ppermute | solution.py:471
  47.2 0.3 collective-permute-start
  47.6 0.0 collective-permute-start.2
  47.6 11.9 %collective-permute-done.1.yr = bf16[2,2,32,2048]{3,2,1,0:T(8,128)(2,1)S(1)} collective-permute-done((bf16[2,2,32,2048]{3,2,1,0:T(8,128)(2,1)S(1)}, bf16[2,2,32,2048]{3,2,1,0:T(8,128)(2,1)S(1)}, u32[]{:S(2)}, u32[]{:S(2)}) %collective-permute-start.1) | collective-permute-done | bytes 524320 | tf_op jit(solution)/shard_map/ppermute | solution.py:471
  59.5 3.0 %collective-permute-start.4 = (bf16[2,32,2048]{2,1,0:T(8,128)(2,1)S(1)}, bf16[2,32,2048]{2,1,0:T(8,128)(2,1)S(1)}, u32[]{:S(2)}, u32[]{:S(2)}) collective-permute-start(bf16[2,32,2048]{2,1,0:T(8,128)(2,1)S(1)} %slice_bitcast_fusion), channel_id=1, source_target_pairs={{0,6},{1,7},{2,0},{3,1},{4,2},{5,3},{6,4},{7,5},{8,14},{9,15},{10,... | collective-permute-start | bytes 786440 | tf_op jit(solution)/shard_map/ppermute | solution.py:471
  62.5 0.0 collective-permute-done.yl
  62.5 0.1 collective-permute-start.3
  62.6 0.1 collective-permute-start.6
  62.7 0.5 collective-permute-start.5
  63.2 4.3 %collective-permute-done.4.do = bf16[2,32,2048]{2,1,0:T(8,128)(2,1)S(1)} collective-permute-done((bf16[2,32,2048]{2,1,0:T(8,128)(2,1)S(1)}, bf16[2,32,2048]{2,1,0:T(8,128)(2,1)S(1)}, u32[]{:S(2)}, u32[]{:S(2)}) %collective-permute-start.4) | collective-permute-done | bytes 262176 | tf_op jit(solution)/shard_map/ppermute | solution.py:471
  67.5 0.0 collective-permute-start.8
  67.5 3.5 %collective-permute-done.3.xo = bf16[2,32,2048]{2,1,0:T(8,128)(2,1)S(1)} collective-permute-done((bf16[2,32,2048]{2,1,0:T(8,128)(2,1)S(1)}, bf16[2,32,2048]{2,1,0:T(8,128)(2,1)S(1)}, u32[]{:S(2)}, u32[]{:S(2)}) %collective-permute-start.3) | collective-permute-done | bytes 262176 | tf_op jit(solution)/shard_map/ppermute | solution.py:471
  71.0 0.0 collective-permute-start.7
  71.0 13.5 %clear0.1 = (f32[1024,8,2048]{2,1,0:T(8,128)}, bf16[2,32,2048]{2,1,0:T(8,128)(2,1)}, s32[1664]{0:T(1024)S(1)}) custom-call(bf16[2,2,32,2048]{3,2,1,0:T(8,128)(2,1)S(1)} %get-tuple-element.17.y_ref.y0, s32[2,256]{1,0:T(2,128)S(1)} %copy-done.4), custom_call_target="tpu_custom_call" | custom-call | bytes 41943040 | tf_op jit(solution)/shard_map/clear0/pallas_call | solution.py:492
  84.5 0.0 collective-permute-done.2.p0
  84.5 10.5 %clear1.1 = (f32[1024,8,2048]{2,1,0:T(8,128)}, f32[2048]{0:T(1024)}, bf16[2,256,384]{2,1,0:T(8,128)(2,1)}, f32[2048,384]{1,0:T(8,128)S(1)}) custom-call(bf16[2,2,32,2048]{3,2,1,0:T(8,128)(2,1)S(1)} %get-tuple-element.17.y_ref.y0, bf16[2,2,32,2048]{3,2,1,0:T(8,128)(2,1)S(1)} %collective-permute-done.yl, ...), custom_call_target="tpu_custom_call", output_to_operand_aliasing={{0}: (8, {})} | custom-call | bytes 25165824 | tf_op jit(solution)/shard_map/clear1/pallas_call | solution.py:503
  95.1 0.0 collective-permute-done.8.pdo
  95.1 0.0 collective-permute-done.6.pr
  95.1 0.0 collective-permute-done.7.pxo
  95.1 0.0 collective-permute-done.5.pl_
  95.1 6.9 %finish.1 = (bf16[2,256,384]{2,1,0:T(8,128)(2,1)}, f32[2048,384]{1,0:T(8,128)}, f32[1024,8,2048]{2,1,0:T(8,128)}) custom-call(s32[1664]{0:T(1024)S(1)} %get-tuple-element.18.plan, bf16[2,2,32,2048]{3,2,1,0:T(8,128)(2,1)S(1)} %get-tuple-element.17.y_ref.y0, ...), custom_call_target="tpu_custom_call", output_to_operand_aliasing={{0}: (15, {}), {2}: (16, {})} | custom-call | tf_op jit(solution)/shard_map/finish/pallas_call | solution.py:514
  (3 shorter events, 0.0 us)
Async XLA Ops:
  0.6 8.8 %copy-start.1 = (bf16[2,256,384]{2,1,0:T(8,128)(2,1)S(1)}, bf16[2,256,384]{2,1,0:T(8,128)(2,1)}, u32[]{:S(2)}) copy-start(bf16[2,256,384]{2,1,0:T(8,128)(2,1)} %du_ref.5) | copy-start | bytes 1179652
  0.6 8.8 %copy-start = (bf16[2048,384]{1,0:T(8,128)(2,1)S(1)}, bf16[2048,384]{1,0:T(8,128)(2,1)}, u32[]{:S(2)}) copy-start(bf16[2048,384]{1,0:T(8,128)(2,1)} %w_ref.5) | copy-start | bytes 4718596
  0.7 8.8 %copy-start.3 = (bf16[2048]{0:T(1024)(128)(2,1)S(1)}, bf16[2048]{0:T(1024)(128)(2,1)}, u32[]{:S(2)}) copy-start(bf16[2048]{0:T(1024)(128)(2,1)} %g_ref.5) | copy-start | bytes 12292
  0.7 8.8 %copy-start.2 = (bf16[2,32,2048]{2,1,0:T(8,128)(2,1)S(1)}, bf16[2,32,2048]{2,1,0:T(8,128)(2,1)}, u32[]{:S(2)}) copy-start(bf16[2,32,2048]{2,1,0:T(8,128)(2,1)} %dres_ref.1) | copy-start | bytes 786436
  0.7 0.8 copy-start.4
  45.5 14.0 %collective-permute-start.1 = (bf16[2,2,32,2048]{3,2,1,0:T(8,128)(2,1)S(1)}, bf16[2,2,32,2048]{3,2,1,0:T(8,128)(2,1)S(1)}, u32[]{:S(2)}, u32[]{:S(2)}) collective-permute-start(bf16[2,2,32,2048]{3,2,1,0:T(8,128)(2,1)S(1)} %get-tuple-element.17.y_ref.y0), channel_id=1, source_target_pairs={{0,6},{1,7},{2,0},{3,1},{4,2},{5,3},{6,4},{7,5},{8,14},{9,15},{10,... | collective-permute-start | bytes 1572872 | tf_op jit(solution)/shard_map/ppermute | solution.py:471
  47.2 15.3 %collective-permute-start = (bf16[2,2,32,2048]{3,2,1,0:T(8,128)(2,1)S(1)}, bf16[2,2,32,2048]{3,2,1,0:T(8,128)(2,1)S(1)}, u32[]{:S(2)}, u32[]{:S(2)}) collective-permute-start(bf16[2,2,32,2048]{3,2,1,0:T(8,128)(2,1)S(1)} %get-tuple-element.17.y_ref.y0), channel_id=1, source_target_pairs={{0,2},{1,3},{2,4},{3,5},{4,6},{5,7},{6,0},{7,1},{8,10},{9,11},{10,... | collective-permute-start | bytes 1572872 | tf_op jit(solution)/shard_map/ppermute | solution.py:471
  47.6 36.9 %collective-permute-start.2 = (bf16[2,2,32,2048]{3,2,1,0:T(8,128)(2,1)S(1)}, bf16[2,2,32,2048]{3,2,1,0:T(8,128)(2,1)S(1)}, u32[]{:S(2)}, u32[]{:S(2)}) collective-permute-start(bf16[2,2,32,2048]{3,2,1,0:T(8,128)(2,1)S(1)} %get-tuple-element.17.y_ref.y0), channel_id=1, source_target_pairs={{0,1},{1,0},{2,3},{3,2},{4,5},{5,4},{6,7},{7,6},{8,9},{9,8},{10,11... | collective-permute-start | bytes 1572872 | tf_op jit(solution)/shard_map/ppermute | solution.py:471
  59.5 8.0 %collective-permute-start.4 = (bf16[2,32,2048]{2,1,0:T(8,128)(2,1)S(1)}, bf16[2,32,2048]{2,1,0:T(8,128)(2,1)S(1)}, u32[]{:S(2)}, u32[]{:S(2)}) collective-permute-start(bf16[2,32,2048]{2,1,0:T(8,128)(2,1)S(1)} %slice_bitcast_fusion), channel_id=1, source_target_pairs={{0,6},{1,7},{2,0},{3,1},{4,2},{5,3},{6,4},{7,5},{8,14},{9,15},{10,... | collective-permute-start | bytes 786440 | tf_op jit(solution)/shard_map/ppermute | solution.py:471
  62.5 8.5 %collective-permute-start.3 = (bf16[2,32,2048]{2,1,0:T(8,128)(2,1)S(1)}, bf16[2,32,2048]{2,1,0:T(8,128)(2,1)S(1)}, u32[]{:S(2)}, u32[]{:S(2)}) collective-permute-start(bf16[2,32,2048]{2,1,0:T(8,128)(2,1)S(1)} %slice_bitcast_fusion.1), channel_id=1, source_target_pairs={{0,2},{1,3},{2,4},{3,5},{4,6},{5,7},{6,0},{7,1},{8,10},{9,11},{10,... | collective-permute-start | bytes 786440 | tf_op jit(solution)/shard_map/ppermute | solution.py:471
  62.6 32.4 %collective-permute-start.6 = (bf16[2,2,32,2048]{3,2,1,0:T(8,128)(2,1)S(1)}, bf16[2,2,32,2048]{3,2,1,0:T(8,128)(2,1)S(1)}, u32[]{:S(2)}, u32[]{:S(2)}) collective-permute-start(bf16[2,2,32,2048]{3,2,1,0:T(8,128)(2,1)S(1)} %collective-permute-done.1.yr), channel_id=1, source_target_pairs={{0,1},{1,0},{2,3},{3,2},{4,5},{5,4},{6,7},{7,6},{8,9},{9,8},{10,11... | collective-permute-start | bytes 1572872 | tf_op jit(solution)/shard_map/ppermute | solution.py:471
  62.7 32.4 %collective-permute-start.5 = (bf16[2,2,32,2048]{3,2,1,0:T(8,128)(2,1)S(1)}, bf16[2,2,32,2048]{3,2,1,0:T(8,128)(2,1)S(1)}, u32[]{:S(2)}, u32[]{:S(2)}) collective-permute-start(bf16[2,2,32,2048]{3,2,1,0:T(8,128)(2,1)S(1)} %collective-permute-done.yl), channel_id=1, source_target_pairs={{0,1},{1,0},{2,3},{3,2},{4,5},{5,4},{6,7},{7,6},{8,9},{9,8},{10,11... | collective-permute-start | bytes 1572872 | tf_op jit(solution)/shard_map/ppermute | solution.py:471
  67.5 27.6 %collective-permute-start.8 = (bf16[2,32,2048]{2,1,0:T(8,128)(2,1)S(1)}, bf16[2,32,2048]{2,1,0:T(8,128)(2,1)S(1)}, u32[]{:S(2)}, u32[]{:S(2)}) collective-permute-start(bf16[2,32,2048]{2,1,0:T(8,128)(2,1)S(1)} %collective-permute-done.4.do), channel_id=1, source_target_pairs={{0,1},{1,0},{2,3},{3,2},{4,5},{5,4},{6,7},{7,6},{8,9},{9,8},{10,11... | collective-permute-start | bytes 786440 | tf_op jit(solution)/shard_map/ppermute | solution.py:471
  71.0 24.1 %collective-permute-start.7 = (bf16[2,32,2048]{2,1,0:T(8,128)(2,1)S(1)}, bf16[2,32,2048]{2,1,0:T(8,128)(2,1)S(1)}, u32[]{:S(2)}, u32[]{:S(2)}) collective-permute-start(bf16[2,32,2048]{2,1,0:T(8,128)(2,1)S(1)} %collective-permute-done.3.xo), channel_id=1, source_target_pairs={{0,1},{1,0},{2,3},{3,2},{4,5},{5,4},{6,7},{7,6},{8,9},{9,8},{10,11... | collective-permute-start | bytes 786440 | tf_op jit(solution)/shard_map/ppermute | solution.py:471

commit v5 on v0

v5 whole, which is shorter than its diff:
```python
import functools

import jax
import jax.numpy as jnp
from jax import lax
from jax.experimental import pallas as pl
from jax.experimental.pallas import tpu as pltpu
from jax.sharding import PartitionSpec as P


EPS = 1e-6
MESH = pl.DeviceIdType.MESH
VMEM = pl.BlockSpec(memory_space=pltpu.VMEM)
SMEM = pl.BlockSpec(memory_space=pltpu.SMEM)
ANY = pl.BlockSpec(memory_space=pl.ANY)
HBM = pl.BlockSpec(memory_space=pltpu.HBM)
F32 = jnp.float32
BF16 = jnp.bfloat16
ROWS = 16
SLOTS = 128


def slab(i, m, k, h):
    return lax.div(i, h) * (k * h) + m * h + lax.rem(i, h)


def ring_places(n):
    me = lax.axis_index("tp")
    chips = n // 2
    return me, me // 2, me % 2, chips


def parts(n, du_ref, w_ref, mine_ref, other_ref, du_g):
    _, chip, core, chips = ring_places(n)
    k, t, _ = du_ref.shape
    h = t // n
    half = chips * k * h
    for side in range(2):
        for j in range(chips):
            owner = ((chip + j) % chips) * 2 + (core if side == 0 else 1 - core)
            for m in range(k):
                base = side * half + j * (k * h) + m * h
                du_g[base:base + h] = du_ref[m, pl.ds(pl.multiple_of(owner * h, h), h)]
    cw = 256

    def cols(i, _):
        c0 = pl.multiple_of(i * cw, cw)
        v = lax.dot_general(du_g[...], w_ref[pl.ds(c0, cw), :], (((1,), (1,)), ((), ())), preferred_element_type=F32)
        v = v.astype(BF16)
        mine_ref[:, :, pl.ds(c0, cw)] = v[:half].reshape(chips, k * h, cw)
        other_ref[:, :, pl.ds(c0, cw)] = v[half:].reshape(chips, k * h, cw)
        return 0

    lax.fori_loop(0, w_ref.shape[0] // cw, cols, 0)


def lookup(n, ids_ref, emb_ref, mine_ref, other_ref, buf, pf, found, at_s, row_s, sem):
    me, chip, core, chips = ring_places(n)
    k, t = ids_ref.shape
    h = t // n
    d = emb_ref.shape[2]
    vl = emb_ref.shape[0] * 8
    lo = me * vl
    half = chips * k * h

    cnt = jnp.int32(0)
    for m in range(k):
        def find(i, cnt):
            v = ids_ref[m, i]
            found[cnt] = i
            return cnt + ((v >= lo) & (v < lo + vl)).astype(jnp.int32)

        first = cnt
        cnt = lax.fori_loop(0, t, find, first, unroll=16)

        def fetch(c, _):
            i = found[c]
            v = ids_ref[m, i] - lo
            pltpu.make_async_copy(emb_ref.at[lax.div(v, 8)], buf.at[c], sem).start()
            owner = lax.div(i, h)
            side = jnp.where(lax.rem(owner, 2) == core, 0, half)
            j = lax.rem(lax.div(owner, 2) - chip + chips, chips)
            at_s[c] = side + j * (k * h) + m * h + lax.rem(i, h)
            row_s[c] = lax.rem(v, 8)
            return 0

        lax.fori_loop(first, cnt, fetch, 0)

    pf[...] = jnp.zeros_like(pf)
    sub = lax.broadcasted_iota(jnp.int32, (8, d), 0)

    def wait(i, _):
        pltpu.make_async_copy(emb_ref.at[0], buf.at[0], sem).wait()
        return 0

    lax.fori_loop(0, cnt, wait, 0)
    step = 4

    def place(q, _):
        rows = []
        for u in range(step):
            i = jnp.minimum(q * step + u, cnt - 1)
            x8 = buf[i].astype(F32)
            rows.append((at_s[i], jnp.sum(jnp.where(sub == row_s[i], x8, 0.0), axis=0, keepdims=True)))
        for at, x in rows:
            pf[pl.ds(at, 1)] = x
        return 0

    lax.fori_loop(0, lax.div(cnt + step - 1, step), place, 0)

    def pack(i, _):
        r0 = pl.multiple_of(i * ROWS, ROWS)
        mine_ref[pl.ds(r0, ROWS)] = pf[pl.ds(r0, ROWS)].astype(BF16)
        other_ref[pl.ds(r0, ROWS)] = pf[pl.ds(half + r0, ROWS)].astype(BF16)
        return 0

    lax.fori_loop(0, half // ROWS, pack, 0)


def fold(h, a_ref, b_ref, right_ref, left_ref, next_ref, prev_ref, own_ref):
    def put(dst, j, m):
        rows = pl.ds(m * h, h)
        dst[...] = a_ref[j, rows].astype(dst.dtype) + b_ref[j, rows].astype(dst.dtype)

    put(right_ref.at[0], 2, 0)
    put(left_ref.at[0], 2, 1)
    put(right_ref.at[1], 1, 1)
    put(left_ref.at[1], 3, 0)
    put(next_ref, 1, 0)
    put(prev_ref, 3, 1)
    put(own_ref.at[0], 0, 0)
    put(own_ref.at[1], 0, 1)


def relay(xn, xp, xl, xr, dn, dp, dl, dr, xn_ref, xp_ref, dn_ref, dp_ref):
    xn_ref[...] = xn[...] + xl[0]
    xp_ref[...] = xp[...] + xr[0]
    dn_ref[...] = dn[...] + dl[0]
    dp_ref[...] = dp[...] + dr[0]


def zeros(z, de_ref, first, rows, sem):
    zr = z.shape[0]
    z[...] = jnp.zeros_like(z)
    cs = [pltpu.make_async_copy(z, de_ref.at[pl.ds(first // 8 + i * zr, zr)], sem) for i in range(rows // (8 * zr))]
    for c in cs:
        c.start()
    return cs


def clear_and_list(n, rows, ids_hbm, de_ref, plan_ref, z, ids, found, table, plan, sem, s_sem):
    load = pltpu.make_async_copy(ids_hbm, ids, s_sem.at[0])
    load.start()
    cs = zeros(z, de_ref, 0, rows, sem)
    k, t = ids.shape
    h, kt = t // n, k * t
    vl = de_ref.shape[0] * 8
    lo = lax.axis_index("tp") * vl

    def reset(i, _):
        table[i] = -1
        return 0

    lax.fori_loop(0, table.shape[0], reset, 0, unroll=8)
    load.wait()
    cnt, used = jnp.int32(0), jnp.int32(0)
    for m in range(k):
        def find(i, cnt):
            v = ids[m, i]
            found[cnt] = i
            return cnt + ((v >= lo) & (v < lo + vl)).astype(jnp.int32)

        first = cnt
        cnt = lax.fori_loop(0, t, find, first, unroll=16)

        def one(c, used):
            i = found[c]
            v = ids[m, i] - lo
            b = lax.div(v, 8)
            s = table[b]
            fresh = (s < 0).astype(jnp.int32)
            s = jnp.where(s < 0, used, s)
            table[b] = s
            plan[c] = slab(i, m, k, h)
            plan[kt + c] = s * 16 + lax.rem(v, 8) * 2 + fresh
            plan[2 * kt + s] = b
            return used + fresh

        used = lax.fori_loop(first, cnt, one, used)
    plan[3 * kt] = cnt
    plan[3 * kt + 1] = used
    store = pltpu.make_async_copy(plan, plan_ref, s_sem.at[1])
    store.start()
    store.wait()
    for c in cs:
        c.wait()


def clear_rest(first, rows, de_in, de_ref, z, sem):
    del de_in
    for c in zeros(z, de_ref, first, rows, sem):
        c.wait()


def spread(n, x0, xl1, xr1, xl2, xr2, d0, dl1, dr1, dl2, dr2, g_ref, dres_ref, w_ref, du_ref,
           dx_all, x_ref, u_ref, dw_ref, dg_ref, x_all, nh_s, rs_s, dgs, n_g, du_g, s_sem, r_sem, gs_sem, gr_sem):
    me, chip, core, chips = ring_places(n)
    k, h, d = dres_ref.shape
    at = lambda off, c: ((chip + off) % chips) * 2 + c
    left, right, far = at(chips - 1, core), at(1, core), at(2, core)
    partner, p_left, p_right, p_far = at(0, 1 - core), at(chips - 1, 1 - core), at(1, 1 - core), at(2, 1 - core)
    near = (me, left, right, partner)
    rest = (far, p_left, p_right, p_far)

    barrier = pltpu.get_barrier_semaphore()
    for o in range(1, n):
        pl.semaphore_signal(barrier, inc=1, device_id={"tp": (me + o) % n}, device_id_type=MESH)

    gf = g_ref[...].astype(F32).reshape(1, d)
    pieces = h // ROWS
    sides = ((xr1, xl2, dr1, dl2), (xl1, xr2, dl1, dr2))
    for m in range(k):
        xa, xb, _, _ = sides[m]
        for i in range(pieces):
            rows = pl.ds(i * ROWS, ROWS)
            x = x0[m, rows] + xa[1, rows] + xb[rows]
            x_ref[m, rows] = x
            x_all[me, m, rows] = x
            xf = x.astype(F32)
            rs = lax.rsqrt(jnp.mean(xf * xf, axis=-1, keepdims=True) + EPS)
            nh_s[m, rows] = xf * rs
            rs_s[m, rows] = jnp.broadcast_to(rs, (ROWS, rs_s.shape[-1]))
    pl.semaphore_wait(barrier, n - 1)

    copies = []

    def send(src, dst, ss, rs, to):
        c = pltpu.make_async_remote_copy(src_ref=src, dst_ref=dst, send_sem=ss, recv_sem=rs,
                                         device_id={"tp": to}, device_id_type=MESH)
        c.start()
        copies.append(c)

    def arrived(dst, ss, rs):
        pltpu.make_async_remote_copy(src_ref=dst, dst_ref=dst, send_sem=ss, recv_sem=rs,
                                     device_id={"tp": partner}, device_id_type=MESH).wait_recv()

    def own(kind, ref):
        for slot, (to, rel) in enumerate(((right, 1), (left, 2), (partner, 0))):
            send(ref.at[me], ref.at[me], s_sem.at[kind, slot], r_sem.at[kind, rel], to)

    def got(kind, rel, view):
        arrived(view, s_sem.at[kind, rel], r_sem.at[kind, rel])

    def onward(kind, ref):
        got(kind, 1, ref.at[left])
        send(ref.at[left, 0], ref.at[left, 0], s_sem.at[kind, 3], r_sem.at[kind, 5], right)
        got(kind, 2, ref.at[right])
        send(ref.at[right, 1], ref.at[right, 1], s_sem.at[kind, 4], r_sem.at[kind, 6], left)
        send(ref.at[left], ref.at[left], s_sem.at[kind, 5], r_sem.at[kind, 3], partner)
        send(ref.at[right], ref.at[right], s_sem.at[kind, 6], r_sem.at[kind, 4], partner)
        got(kind, 0, ref.at[partner])

    def across(kind, ref):
        for m in range(2):
            got(kind, 5 + m, ref.at[far, m])
            send(ref.at[far, m], ref.at[far, m], s_sem.at[kind, 7 + m], r_sem.at[kind, 7 + m], partner)
        got(kind, 3, ref.at[p_left])
        got(kind, 4, ref.at[p_right])

    def last(kind, ref):
        for m in range(2):
            got(kind, 7 + m, ref.at[p_far, m])

    own(0, x_all)

    dg = jnp.zeros((1, d), F32)
    for m in range(k):
        _, _, da, db = sides[m]
        for i in range(pieces):
            rows = pl.ds(i * ROWS, ROWS)
            dn = d0[m, rows] + da[1, rows] + db[rows]
            nh = nh_s[m, rows]
            dg = dg + jnp.sum(dn * nh, axis=0, keepdims=True)
            gdn = gf * dn
            dxn = rs_s[m, rows, :1] * (gdn - nh * jnp.mean(nh * gdn, axis=-1, keepdims=True))
            dx_all[me, m, rows] = (dres_ref[m, rows].astype(F32) + dxn).astype(BF16)
    dgs[me] = dg
    own(1, dx_all)
    for o in range(1, n):
        send(dgs.at[me], dgs.at[me], gs_sem.at[o], gr_sem.at[me], (me + o) % n)

    def project(owners, add):
        for p, owner in enumerate(owners):
            for m in range(k):
                base = p * (k * h) + m * h
                du_g[base:base + h] = du_ref[m, pl.ds(pl.multiple_of(owner * h, h), h)]
                for i in range(pieces):
                    xf = x_all[owner, m, pl.ds(i * ROWS, ROWS)].astype(F32)
                    rs = lax.rsqrt(jnp.mean(xf * xf, axis=-1, keepdims=True) + EPS)
                    n_g[base + i * ROWS:base + (i + 1) * ROWS] = ((xf * rs) * gf).astype(BF16)
        u = jnp.dot(n_g[...], w_ref[...], preferred_element_type=F32).astype(BF16)
        for p, owner in enumerate(owners):
            for m in range(k):
                base = p * (k * h) + m * h
                u_ref[m, pl.ds(pl.multiple_of(owner * h, h), h)] = u[base:base + h]
        cw = 512
        for i in range(d // cw):
            v = lax.dot_general(n_g[:, i * cw:(i + 1) * cw], du_g[...], (((0,), (0,)), ((), ())),
                                preferred_element_type=F32)
            rows = slice(i * cw, (i + 1) * cw)
            dw_ref[rows] = dw_ref[rows] + v if add else v

    onward(0, x_all)
    project(near, False)
    onward(1, dx_all)
    across(0, x_all)
    last(0, x_all)
    project(rest, True)
    across(1, dx_all)
    last(1, dx_all)

    for o in range(1, n):
        src = (me + o) % n
        arrived(dgs.at[src], gs_sem.at[o], gr_sem.at[src])
    total_dg = dgs[0]
    for i in range(1, n):
        total_dg = total_dg + dgs[i]
    dg_ref[...] = total_dg
    for c in copies:
        c.wait_send()


def finish(plan, dx_all, x_in, u_in, dw_in, dg_in, de_in, x_ref, u_ref, dw_ref, dg_ref, de_ref, dxf, acc, sem, o_sem):
    del de_in
    outs = [pltpu.make_async_copy(src, dst, o_sem.at[i])
            for i, (src, dst) in enumerate(((dw_in, dw_ref), (u_in, u_ref), (x_in, x_ref)))]
    for c in outs:
        c.start()
    dg_ref[...] = dg_in[...].reshape(dg_ref.shape)
    n, k, h, d = dx_all.shape
    kt = k * h * n

    def widen(i, _):
        for m in range(k):
            for s in range(h // ROWS):
                dxf[pl.ds(pl.multiple_of(i * (k * h) + m * h + s * ROWS, ROWS), ROWS)] = dx_all[i, m, pl.ds(s * ROWS, ROWS)].astype(F32)
        return 0

    lax.fori_loop(0, n, widen, 0)

    sub = lax.broadcasted_iota(jnp.int32, (8, d), 0)
    cnt, used = plan[3 * kt], plan[3 * kt + 1]
    step = 4

    def drain(i, _):
        pltpu.make_async_copy(acc.at[0], de_ref.at[0], sem).wait()
        return 0

    def turn(q, _):
        @pl.when(q > 0)
        def _():
            lax.fori_loop(0, SLOTS, drain, 0)

        def some(b, _):
            todo = []
            for e in range(step):
                i = b * step + e
                c = jnp.minimum(i, cnt - 1)
                code = plan[kt + c]
                s = (code >> 4) - q * SLOTS
                s = jnp.where((i < cnt) & (s >= 0) & (s < SLOTS), s, SLOTS)
                todo.append((s, (code >> 1) & 7, (code & 1) == 1, dxf[pl.ds(plan[c], 1)]))
            for s, r, fresh, x in todo:
                old = jnp.where(fresh, jnp.zeros((8, d), F32), acc[s])
                acc[s] = old + jnp.where(sub == r, jnp.broadcast_to(x, (8, d)), 0.0)
            return 0

        lax.fori_loop(0, lax.div(cnt + step - 1, step), some, 0)

        def put(i, _):
            pltpu.make_async_copy(acc.at[i], de_ref.at[plan[2 * kt + q * SLOTS + i]], sem).start()
            return 0

        lax.fori_loop(0, jnp.minimum(used - q * SLOTS, SLOTS), put, 0)
        return 0

    turns = lax.div(used + SLOTS - 1, SLOTS)
    lax.fori_loop(0, turns, turn, 0)

    for c in outs:
        c.wait()
    lax.fori_loop(0, used - jnp.maximum(turns - 1, 0) * SLOTS, drain, 0)


def solution(mesh):
    n = mesh.shape["tp"]
    chips = n // 2
    to_right = [(r, (r + 2) % n) for r in range(n)]
    to_left = [(r, (r + n - 2) % n) for r in range(n)]
    to_partner = [(r, r ^ 1) for r in range(n)]
    dma = pltpu.SemaphoreType.DMA

    def step(ids, emb, g, w, du, dres):
        k, t = ids.shape
        vl, d = emb.shape
        f = w.shape[1]
        h = t // n
        kt = k * t
        shape = jax.ShapeDtypeStruct
        i32 = lambda *s: shape(s, jnp.int32)
        smem = lambda *s: pltpu.SMEM(s, jnp.int32)
        cost = lambda b: pl.CostEstimate(flops=0, bytes_accessed=b, transcendentals=0)
        limit = lambda mib, **kw: pltpu.CompilerParams(vmem_limit_bytes=mib << 20, **kw)

        def move(v, perm):
            return lax.ppermute(v, "tp", perm)

        side = shape((chips, k * h, d), BF16)
        dm, do = pl.pallas_call(
            functools.partial(parts, n),
            out_shape=(side, side), in_specs=[VMEM] * 2, out_specs=(VMEM, VMEM),
            scratch_shapes=[pltpu.VMEM((kt, f), BF16)],
            compiler_params=limit(8), cost_estimate=cost(4 << 20), name="parts",
        )(du, w)
        dp = move(do, to_partner)

        flat = shape((kt // 2, d), BF16)
        xm, xo = pl.pallas_call(
            functools.partial(lookup, n),
            out_shape=(flat, flat), in_specs=[SMEM, HBM], out_specs=(VMEM, VMEM),
            scratch_shapes=[pltpu.VMEM((kt, 8, d), BF16), pltpu.VMEM((kt, d), F32), smem(kt + 1), smem(kt), smem(kt), dma],
            compiler_params=limit(32), cost_estimate=cost(16 << 20), name="lookup",
        )(ids, emb.reshape(vl // 8, 8, d))
        xp = move(xo.reshape(chips, k * h, d), to_partner)

        def fold_of(a, b, dtype):
            two, one = shape((2, h, d), dtype), shape((h, d), dtype)
            return pl.pallas_call(
                functools.partial(fold, h),
                out_shape=(two, two, one, one, two), in_specs=[VMEM] * 2, out_specs=(VMEM,) * 5,
                compiler_params=limit(8), cost_estimate=cost(2 << 20),
            )(a, b)

        d_r, d_l, d_n, d_p, d0 = fold_of(dm, dp, F32)
        x_r, x_l, x_n, x_p, x0 = fold_of(xm.reshape(chips, k * h, d), xp, BF16)
        dl1 = move(d_r, to_right)
        dr1 = move(d_l, to_left)
        xl1 = move(x_r, to_right)
        xr1 = move(x_l, to_left)

        zr = 16
        split = (vl * 10 // 16) // (8 * zr) * (8 * zr)
        de_shape = shape((vl // 8, 8, d), F32)
        size = 3 * kt + 128
        de, plan = pl.pallas_call(
            functools.partial(clear_and_list, n, split),
            out_shape=(de_shape, i32(size)), in_specs=[ANY], out_specs=(ANY, ANY),
            scratch_shapes=[pltpu.VMEM((zr, 8, d), F32), smem(k, t), smem(kt + 1), smem(vl // 8), smem(size),
                            dma, dma((2,))],
            compiler_params=limit(8), cost_estimate=cost(split * d * 4), name="clear0",
        )(ids)

        half_x, half_d = shape((h, d), BF16), shape((h, d), F32)
        x_n, x_p, d_n, d_p = pl.pallas_call(
            relay, out_shape=(half_x, half_x, half_d, half_d), in_specs=[VMEM] * 8, out_specs=(VMEM,) * 4,
            compiler_params=limit(8), cost_estimate=cost(2 << 20), name="relay",
        )(x_n, x_p, xl1, xr1, d_n, d_p, dl1, dr1)
        dl2 = move(d_n, to_right)
        dr2 = move(d_p, to_left)
        xl2 = move(x_n, to_right)
        xr2 = move(x_p, to_left)

        de = pl.pallas_call(
            functools.partial(clear_rest, split, vl - split),
            out_shape=de_shape, in_specs=[ANY], out_specs=ANY, input_output_aliases={0: 0},
            scratch_shapes=[pltpu.VMEM((zr, 8, d), F32), dma],
            compiler_params=limit(8), cost_estimate=cost((vl - split) * d * 4), name="clear1",
        )(de)

        tok, u_s, dw_s = shape((k, h, d), BF16), shape((k, t, f), BF16), shape((d, f), F32)
        some = kt // 2
        dx_all, x, u, dw, dg = pl.pallas_call(
            functools.partial(spread, n),
            out_shape=(shape((n, k, h, d), BF16), tok, u_s, dw_s, shape((1, d), F32)),
            in_specs=[VMEM] * 14, out_specs=(VMEM,) * 5,
            scratch_shapes=[pltpu.VMEM((n, k, h, d), BF16), pltpu.VMEM((k, h, d), F32), pltpu.VMEM((k, h, 128), F32),
                            pltpu.VMEM((n, 1, d), F32), pltpu.VMEM((some, d), BF16), pltpu.VMEM((some, f), BF16),
                            dma((2, 9)), dma((2, 9)), dma((n,)), dma((n,))],
            compiler_params=limit(24, collective_id=0, has_side_effects=True), name="spread",
        )(x0, xl1, xr1, xl2, xr2, d0, dl1, dr1, dl2, dr2, g, dres, w, du)

        x, u, dw, dg, de = pl.pallas_call(
            finish,
            out_shape=(tok, u_s, dw_s, shape((d,), F32), de_shape),
            in_specs=[SMEM] + [VMEM] * 5 + [ANY], out_specs=(ANY, ANY, ANY, VMEM, ANY),
            input_output_aliases={6: 4},
            scratch_shapes=[pltpu.VMEM((kt, d), F32), pltpu.VMEM((SLOTS + 1, 8, d), F32), dma, dma((3,))],
            compiler_params=limit(24), name="finish",
        )(plan, dx_all, x, u, dw, dg, de)
        return u, x, de.reshape(vl, d), dw, dg

    return jax.shard_map(
        step,
        mesh=mesh,
        in_specs=(P("dp", None), P("tp", None), P(None), P(None, "tp"), P("dp", None, "tp"), P("dp", "tp", None)),
        out_specs=(P("dp", None, "tp"), P("dp", "tp", None), P(("dp", "tp"), None), P(None, ("dp", "tp")), P("dp")),
        check_vma=False,
    )
```

time: 271 us -> 96.8 us (0.36)
  waiting for transfers between devices: 138 us -> 14.3 us
  matrix products: 72 us -> 0 us
  Pallas kernels: 0 us -> 63.8 us
  other arithmetic: 18.2 us -> 0 us
  blocking collectives: 14.2 us -> 0 us
  between operations: 13.8 us -> 0.81 us
  starting transfers between devices: 9.2 us -> 13.6 us
    psum x2 -> x0, waiting for transfers between devices: 108 us -> none  [micro(): x = lax.psum(xp, 'tp')]
    dot_general x8 -> x0, matrix products: 72 us -> none  [the longest x2 30.9 us: micro(): jnp.dot(oh, emb, preferred_element_type=jnp.float32).astype(jnp.bfloat16)]
    pallas_call x0 -> x9, Pallas kernels: none -> 63.8 us  [the longest x1 24.3 us: step(): pl.pallas_call(functools.partial(spread, n), out_shape=(shape((n, k, h, d...]
    all_gather x2 -> x0, waiting for transfers between devices: 29.9 us -> none  [micro(): dxa = lax.all_gather(dx, 'tp', axis=0, tiled=True)]
    ppermute x0 -> x10, waiting for transfers between devices: none -> 14.3 us  [move(): return lax.ppermute(v, 'tp', perm)]
    psum x1 -> x0, blocking collectives: 14.2 us -> none  [local(): dg = lax.psum(dg, 'tp')]
    ppermute x0 -> x10, starting transfers between devices: none -> 13.6 us  [move(): return lax.ppermute(v, 'tp', perm)]
    all_to_all x2 -> x0, starting transfers between devices: 9.07 us -> none  [micro(): recv = lax.all_to_all(pdn, 'tp', 0, 0, tiled=True).reshape(groups, tl, d)]
  transfers between devices with their start and end apart: 6 -> 10, of which waited for: 4 -> 1; matrix products, arithmetic and copies ran while one was open for 7% -> 0% of each run, Pallas kernels for 0% -> 32%
where the time goes in v5:
time: 96.8 us; the launch traced here: 95.5 us
  Pallas kernels  63.8 us (66%)
  waiting for transfers between devices  14.3 us (15%)
  starting transfers between devices  13.6 us (14%)
  local copies, waits for them, and re-layouts  3.1 us (3%)
    pallas_call x1, Pallas kernels, step(): pl.pallas_call(functools.partial(spread, n), out_shape=(shape((n, k, h, d...  24.3 us
    ppermute x10, waiting for transfers between devices, move(): return lax.ppermute(v, 'tp', perm)  14.3 us
    ppermute x10, starting transfers between devices, move(): return lax.ppermute(v, 'tp', perm)  13.6 us
    pallas_call x1, Pallas kernels, step(): pl.pallas_call(functools.partial(clear_and_list, n, split), out_shape=(de...  13.5 us
    pallas_call x1, Pallas kernels, step(): pl.pallas_call(functools.partial(lookup, n), out_shape=(flat, flat), in_s...  8.5 us
    pallas_call x1, Pallas kernels, step(): pl.pallas_call(functools.partial(clear_rest, split, vl - split), out_shap...  8.46 us
    pallas_call x1, Pallas kernels, step(): pl.pallas_call(finish, out_shape=(tok, u_s, dw_s, shape((d,), F32), de_sh...  5.94 us
    unnamed x14, local copies, waits for them, and re-layouts  3.1 us
  transfers between devices with their start and end apart: 10, of which 1 were waited for; matrix products, arithmetic and copies ran while one was open for 0% of the time, Pallas kernels for 32%

profile of v5, /device:TPU:112, one launch (start us, length us, event | category | flops | bytes accessed | tf_op | source)
XLA Modules:
  0.0 95.5 jit_solution(15322478532780052798)
XLA Ops:
  0.6 0.0 copy-start
  0.6 1.4 %copy-done = bf16[2048,384]{1,0:T(8,128)(2,1)S(1)} copy-done((bf16[2048,384]{1,0:T(8,128)(2,1)S(1)}, bf16[2048,384]{1,0:T(8,128)(2,1)}, u32[]{:S(2)}) %copy-start) | copy-done | bytes 1572888
  2.0 1.0 %copy-done.2 = bf16[2,256,384]{2,1,0:T(8,128)(2,1)S(1)} copy-done((bf16[2,256,384]{2,1,0:T(8,128)(2,1)S(1)}, bf16[2,256,384]{2,1,0:T(8,128)(2,1)}, u32[]{:S(2)}) %copy-start.2) | copy-done | bytes 393240
  3.0 2.7 %parts.1 = (bf16[4,64,2048]{2,1,0:T(8,128)(2,1)S(1)}, bf16[4,64,2048]{2,1,0:T(8,128)(2,1)S(1)}) custom-call(bf16[2,256,384]{2,1,0:T(8,128)(2,1)S(1)} %copy-done.2, bf16[2048,384]{1,0:T(8,128)(2,1)S(1)} %copy-done), custom_call_target="tpu_custom_call" | custom-call | bytes 4194304 | tf_op jit(solution)/shard_map/parts/pallas_call | solution.py:419
  5.7 0.1 collective-permute-start.3
  5.8 0.0 copy-start.5
  5.8 0.7 copy-done.5
  6.5 8.5 %lookup.1 = (bf16[256,2048]{1,0:T(8,128)(2,1)S(1)}, bf16[256,2048]{1,0:T(8,128)(2,1)S(1)}) custom-call(s32[2,256]{1,0:T(2,128)S(1)} %copy-done.5, bf16[1024,8,2048]{2,1,0:T(8,128)(2,1)} %bitcast.6), custom_call_target="tpu_custom_call" | custom-call | bytes 16777216 | tf_op jit(solution)/shard_map/lookup/pallas_call | solution.py:428
  15.0 0.3 collective-permute-start
  15.3 0.0 collective-permute-done.3.b_ref
  15.3 0.2 shard_map.102
  15.5 1.3 %collective-permute-start.4 = (f32[2,32,2048]{2,1,0:T(8,128)S(1)}, f32[2,32,2048]{2,1,0:T(8,128)S(1)}, u32[]{:S(2)}, u32[]{:S(2)}) collective-permute-start(f32[2,32,2048]{2,1,0:T(8,128)S(1)} %get-tuple-element.47), channel_id=1, source_target_pairs={{0,2},{1,3},{2,4},{3,5},{4,6},{5,7},{6,0},{7,1},{8,10},{9,11},{10,... | collective-permute-start | bytes 1572872 | tf_op jit(solution)/shard_map/ppermute | solution.py:416
  16.8 2.1 %collective-permute-start.5 = (f32[2,32,2048]{2,1,0:T(8,128)S(1)}, f32[2,32,2048]{2,1,0:T(8,128)S(1)}, u32[]{:S(2)}, u32[]{:S(2)}) collective-permute-start(f32[2,32,2048]{2,1,0:T(8,128)S(1)} %get-tuple-element.48), channel_id=1, source_target_pairs={{0,6},{1,7},{2,0},{3,1},{4,2},{5,3},{6,4},{7,5},{8,14},{9,15},{10,... | collective-permute-start | bytes 1572872 | tf_op jit(solution)/shard_map/ppermute | solution.py:416
  18.8 0.0 collective-permute-done.b_ref
  18.8 0.1 shard_map.101
  18.9 0.3 collective-permute-start.1
  19.3 3.0 %collective-permute-start.2 = (bf16[2,32,2048]{2,1,0:T(8,128)(2,1)S(1)}, bf16[2,32,2048]{2,1,0:T(8,128)(2,1)S(1)}, u32[]{:S(2)}, u32[]{:S(2)}) collective-permute-start(bf16[2,32,2048]{2,1,0:T(8,128)(2,1)S(1)} %get-tuple-element.40), channel_id=1, source_target_pairs={{0,6},{1,7},{2,0},{3,1},{4,2},{5,3},{6,4},{7,5},{8,14},{9,15},{10,... | collective-permute-start | bytes 786440 | tf_op jit(solution)/shard_map/ppermute | solution.py:416
  22.3 14.3 %collective-permute-done.1.xl.xl1 = bf16[2,32,2048]{2,1,0:T(8,128)(2,1)S(1)} collective-permute-done((bf16[2,32,2048]{2,1,0:T(8,128)(2,1)S(1)}, bf16[2,32,2048]{2,1,0:T(8,128)(2,1)S(1)}, u32[]{:S(2)}, u32[]{:S(2)}) %collective-permute-start.1) | collective-permute-done | bytes 262176 | tf_op jit(solution)/shard_map/ppermute | solution.py:416
  36.5 0.1 relay.1
  36.6 0.7 collective-permute-start.8
  37.3 2.6 %collective-permute-start.9 = (f32[32,2048]{1,0:T(8,128)S(1)}, f32[32,2048]{1,0:T(8,128)S(1)}, u32[]{:S(2)}, u32[]{:S(2)}) collective-permute-start(f32[32,2048]{1,0:T(8,128)S(1)} %get-tuple-element.53), channel_id=1, source_target_pairs={{0,6},{1,7},{2,0},{3,1},{4,2},{5,3},{6,4},{7,5},{8,14},{9,15},{10,... | collective-permute-start | bytes 786440 | tf_op jit(solution)/shard_map/ppermute | solution.py:416
  40.0 3.2 %collective-permute-start.7 = (bf16[32,2048]{1,0:T(8,128)(2,1)S(1)}, bf16[32,2048]{1,0:T(8,128)(2,1)S(1)}, u32[]{:S(2)}, u32[]{:S(2)}) collective-permute-start(bf16[32,2048]{1,0:T(8,128)(2,1)S(1)} %get-tuple-element.50), channel_id=1, source_target_pairs={{0,6},{1,7},{2,0},{3,1},{4,2},{5,3},{6,4},{7,5},{8,14},{9,15},{10,... | collective-permute-start | bytes 393224 | tf_op jit(solution)/shard_map/ppermute | solution.py:416
  43.2 13.5 %clear0.1 = (f32[1024,8,2048]{2,1,0:T(8,128)}, s32[1664]{0:T(1024)S(1)}) custom-call(s32[2,256]{1,0:T(2,128)S(1)} %copy-done.5), custom_call_target="tpu_custom_call" | custom-call | bytes 41943040 | tf_op jit(solution)/shard_map/clear0/pallas_call | solution.py:455
  56.7 0.0 copy-start.1
  56.7 0.0 copy-start.3
  56.7 0.0 copy-start.4
  56.7 0.0 copy-start.6
  56.7 8.5 %clear1.1.de_in = f32[1024,8,2048]{2,1,0:T(8,128)} custom-call(f32[1024,8,2048]{2,1,0:T(8,128)} %get-tuple-element.59.de_in), custom_call_target="tpu_custom_call", output_to_operand_aliasing={{}: (0, {})} | custom-call | bytes 25165824 | tf_op jit(solution)/shard_map/clear1/pallas_call | solution.py:473
  65.2 0.0 collective-permute-done.6.xl2
  65.2 0.0 collective-permute-done.8.dl2
  65.3 24.3 %spread.1 = (bf16[8,2,32,2048]{3,2,1,0:T(8,128)(2,1)S(1)}, bf16[2,32,2048]{2,1,0:T(8,128)(2,1)S(1)}, bf16[2,256,384]{2,1,0:T(8,128)(2,1)S(1)}, f32[2048,384]{1,0:T(8,128)S(1)}, f32[1,2048]{1,0:T(1,128)S(1)}) custom-call(bf16[2,32,2048]{2,1,0:T(8,128)(2,1)S(1)} %get-tuple-element.38.x0, bf16[2,32,2048]{2,1,0:T(8,128)(2,1)S(1)} %collective-permute-done.1.xl.xl1, ...), custom_call_target="tpu_custom_call" | custom-call | tf_op jit(solution)/shard_map/spread/pallas_call | solution.py:482
  89.6 5.9 %finish.1 = (bf16[2,32,2048]{2,1,0:T(8,128)(2,1)}, bf16[2,256,384]{2,1,0:T(8,128)(2,1)}, f32[2048,384]{1,0:T(8,128)}, f32[2048]{0:T(1024)}, f32[1024,8,2048]{2,1,0:T(8,128)}) custom-call(s32[1664]{0:T(1024)S(1)} %get-tuple-element.35.plan, bf16[8,2,32,2048]{3,2,1,0:T(8,128)(2,1)S(1)} %get-tuple-element.54.dx_all, ...), custom_call_target="tpu_custom_call", output_to_operand_aliasing={{4}: (6, {})} | custom-call | tf_op jit(solution)/shard_map/finish/pallas_call | solution.py:492
  (11 shorter events, 0.0 us)
Async XLA Ops:
  0.6 1.4 %copy-start = (bf16[2048,384]{1,0:T(8,128)(2,1)S(1)}, bf16[2048,384]{1,0:T(8,128)(2,1)}, u32[]{:S(2)}) copy-start(bf16[2048,384]{1,0:T(8,128)(2,1)} %w_ref.3) | copy-start | bytes 4718596
  2.0 1.0 %copy-start.2 = (bf16[2,256,384]{2,1,0:T(8,128)(2,1)S(1)}, bf16[2,256,384]{2,1,0:T(8,128)(2,1)}, u32[]{:S(2)}) copy-start(bf16[2,256,384]{2,1,0:T(8,128)(2,1)} %du_ref.3) | copy-start | bytes 1179652
  5.7 9.6 %collective-permute-start.3 = (bf16[4,64,2048]{2,1,0:T(8,128)(2,1)S(1)}, bf16[4,64,2048]{2,1,0:T(8,128)(2,1)S(1)}, u32[]{:S(2)}, u32[]{:S(2)}) collective-permute-start(bf16[4,64,2048]{2,1,0:T(8,128)(2,1)S(1)} %get-tuple-element.44), channel_id=1, source_target_pairs={{0,1},{1,0},{2,3},{3,2},{4,5},{5,4},{6,7},{7,6},{8,9},{9,8},{10,11... | collective-permute-start | bytes 3145736 | tf_op jit(solution)/shard_map/ppermute | solution.py:416
  5.8 0.7 copy-start.5
  15.0 3.8 %collective-permute-start = (bf16[4,64,2048]{2,1,0:T(8,128)(2,1)S(1)}, bf16[4,64,2048]{2,1,0:T(8,128)(2,1)S(1)}, u32[]{:S(2)}, u32[]{:S(2)}) collective-permute-start(bf16[4,64,2048]{2,1,0:T(8,128)(2,1)S(1)} %bitcast.5), channel_id=1, source_target_pairs={{0,1},{1,0},{2,3},{3,2},{4,5},{5,4},{6,7},{7,6},{8,9},{9,8},{10,11... | collective-permute-start | bytes 3145736 | tf_op jit(solution)/shard_map/ppermute | solution.py:416
  15.5 21.0 %collective-permute-start.4 = (f32[2,32,2048]{2,1,0:T(8,128)S(1)}, f32[2,32,2048]{2,1,0:T(8,128)S(1)}, u32[]{:S(2)}, u32[]{:S(2)}) collective-permute-start(f32[2,32,2048]{2,1,0:T(8,128)S(1)} %get-tuple-element.47), channel_id=1, source_target_pairs={{0,2},{1,3},{2,4},{3,5},{4,6},{5,7},{6,0},{7,1},{8,10},{9,11},{10,... | collective-permute-start | bytes 1572872 | tf_op jit(solution)/shard_map/ppermute | solution.py:416
  16.8 19.8 %collective-permute-start.5 = (f32[2,32,2048]{2,1,0:T(8,128)S(1)}, f32[2,32,2048]{2,1,0:T(8,128)S(1)}, u32[]{:S(2)}, u32[]{:S(2)}) collective-permute-start(f32[2,32,2048]{2,1,0:T(8,128)S(1)} %get-tuple-element.48), channel_id=1, source_target_pairs={{0,6},{1,7},{2,0},{3,1},{4,2},{5,3},{6,4},{7,5},{8,14},{9,15},{10,... | collective-permute-start | bytes 1572872 | tf_op jit(solution)/shard_map/ppermute | solution.py:416
  18.9 17.6 %collective-permute-start.1 = (bf16[2,32,2048]{2,1,0:T(8,128)(2,1)S(1)}, bf16[2,32,2048]{2,1,0:T(8,128)(2,1)S(1)}, u32[]{:S(2)}, u32[]{:S(2)}) collective-permute-start(bf16[2,32,2048]{2,1,0:T(8,128)(2,1)S(1)} %get-tuple-element.39), channel_id=1, source_target_pairs={{0,2},{1,3},{2,4},{3,5},{4,6},{5,7},{6,0},{7,1},{8,10},{9,11},{10,... | collective-permute-start | bytes 786440 | tf_op jit(solution)/shard_map/ppermute | solution.py:416
  19.3 17.2 %collective-permute-start.2 = (bf16[2,32,2048]{2,1,0:T(8,128)(2,1)S(1)}, bf16[2,32,2048]{2,1,0:T(8,128)(2,1)S(1)}, u32[]{:S(2)}, u32[]{:S(2)}) collective-permute-start(bf16[2,32,2048]{2,1,0:T(8,128)(2,1)S(1)} %get-tuple-element.40), channel_id=1, source_target_pairs={{0,6},{1,7},{2,0},{3,1},{4,2},{5,3},{6,4},{7,5},{8,14},{9,15},{10,... | collective-permute-start | bytes 786440 | tf_op jit(solution)/shard_map/ppermute | solution.py:416
  36.6 28.6 %collective-permute-start.8 = (f32[32,2048]{1,0:T(8,128)S(1)}, f32[32,2048]{1,0:T(8,128)S(1)}, u32[]{:S(2)}, u32[]{:S(2)}) collective-permute-start(f32[32,2048]{1,0:T(8,128)S(1)} %get-tuple-element.52), channel_id=1, source_target_pairs={{0,2},{1,3},{2,4},{3,5},{4,6},{5,7},{6,0},{7,1},{8,10},{9,11},{10,... | collective-permute-start | bytes 786440 | tf_op jit(solution)/shard_map/ppermute | solution.py:416
  37.3 27.9 %collective-permute-start.9 = (f32[32,2048]{1,0:T(8,128)S(1)}, f32[32,2048]{1,0:T(8,128)S(1)}, u32[]{:S(2)}, u32[]{:S(2)}) collective-permute-start(f32[32,2048]{1,0:T(8,128)S(1)} %get-tuple-element.53), channel_id=1, source_target_pairs={{0,6},{1,7},{2,0},{3,1},{4,2},{5,3},{6,4},{7,5},{8,14},{9,15},{10,... | collective-permute-start | bytes 786440 | tf_op jit(solution)/shard_map/ppermute | solution.py:416
  40.0 25.2 %collective-permute-start.6 = (bf16[32,2048]{1,0:T(8,128)(2,1)S(1)}, bf16[32,2048]{1,0:T(8,128)(2,1)S(1)}, u32[]{:S(2)}, u32[]{:S(2)}) collective-permute-start(bf16[32,2048]{1,0:T(8,128)(2,1)S(1)} %get-tuple-element.49), channel_id=1, source_target_pairs={{0,2},{1,3},{2,4},{3,5},{4,6},{5,7},{6,0},{7,1},{8,10},{9,11},{10,... | collective-permute-start | bytes 393224 | tf_op jit(solution)/shard_map/ppermute | solution.py:416
  40.0 25.2 %collective-permute-start.7 = (bf16[32,2048]{1,0:T(8,128)(2,1)S(1)}, bf16[32,2048]{1,0:T(8,128)(2,1)S(1)}, u32[]{:S(2)}, u32[]{:S(2)}) collective-permute-start(bf16[32,2048]{1,0:T(8,128)(2,1)S(1)} %get-tuple-element.50), channel_id=1, source_target_pairs={{0,6},{1,7},{2,0},{3,1},{4,2},{5,3},{6,4},{7,5},{8,14},{9,15},{10,... | collective-permute-start | bytes 393224 | tf_op jit(solution)/shard_map/ppermute | solution.py:416
  56.7 8.6 %copy-start.1 = (bf16[2048,384]{1,0:T(8,128)(2,1)S(1)}, bf16[2048,384]{1,0:T(8,128)(2,1)}, u32[]{:S(2)}) copy-start(bf16[2048,384]{1,0:T(8,128)(2,1)} %w_ref.3) | copy-start | bytes 4718596
  56.7 8.6 %copy-start.3 = (bf16[2,256,384]{2,1,0:T(8,128)(2,1)S(1)}, bf16[2,256,384]{2,1,0:T(8,128)(2,1)}, u32[]{:S(2)}) copy-start(bf16[2,256,384]{2,1,0:T(8,128)(2,1)} %du_ref.3) | copy-start | bytes 1179652
  56.7 8.6 %copy-start.4 = (bf16[2,32,2048]{2,1,0:T(8,128)(2,1)S(1)}, bf16[2,32,2048]{2,1,0:T(8,128)(2,1)}, u32[]{:S(2)}) copy-start(bf16[2,32,2048]{2,1,0:T(8,128)(2,1)} %dres_ref.1) | copy-start | bytes 786436
  56.7 8.6 %copy-start.6 = (bf16[2048]{0:T(1024)(128)(2,1)S(1)}, bf16[2048]{0:T(1024)(128)(2,1)}, u32[]{:S(2)}) copy-start(bf16[2048]{0:T(1024)(128)(2,1)} %g_ref.1) | copy-start | bytes 12292

commit v6 on v5

--- a/solution.py
+++ b/solution.py
@@ -30,7 +30,8 @@
     return me, me // 2, me % 2, chips
 
 
-def parts(n, du_ref, w_ref, mine_ref, other_ref, du_g):
+def parts(n, du_ref, w_ref, after_ref, mine_ref, other_ref, du_g):
+    del after_ref
     _, chip, core, chips = ring_places(n)
     k, t, _ = du_ref.shape
     h = t // n
@@ -100,18 +101,20 @@
         rows = []
         for u in range(step):
             i = jnp.minimum(q * step + u, cnt - 1)
-            x8 = buf[i].astype(F32)
-            rows.append((at_s[i], jnp.sum(jnp.where(sub == row_s[i], x8, 0.0), axis=0, keepdims=True)))
-        for at, x in rows:
-            pf[pl.ds(at, 1)] = x
+            at = at_s[i]
+            to = at & 7
+            rows.append((at >> 3, to, pltpu.roll(buf[i].astype(F32), (to - row_s[i]) & 7, 0)))
+        for block, to, x in rows:
+            pf[block] = jnp.where(sub == to, x, pf[block])
         return 0
 
     lax.fori_loop(0, lax.div(cnt + step - 1, step), place, 0)
 
     def pack(i, _):
         r0 = pl.multiple_of(i * ROWS, ROWS)
-        mine_ref[pl.ds(r0, ROWS)] = pf[pl.ds(r0, ROWS)].astype(BF16)
-        other_ref[pl.ds(r0, ROWS)] = pf[pl.ds(half + r0, ROWS)].astype(BF16)
+        b0 = pl.multiple_of(i * (ROWS // 8), ROWS // 8)
+        for dst, first in ((mine_ref, 0), (other_ref, half // 8)):
+            dst[pl.ds(r0, ROWS)] = pf[pl.ds(first + b0, ROWS // 8)].reshape(ROWS, d).astype(BF16)
         return 0
 
     lax.fori_loop(0, half // ROWS, pack, 0)
@@ -132,11 +135,9 @@
     put(own_ref.at[1], 0, 1)
 
 
-def relay(xn, xp, xl, xr, dn, dp, dl, dr, xn_ref, xp_ref, dn_ref, dp_ref):
-    xn_ref[...] = xn[...] + xl[0]
-    xp_ref[...] = xp[...] + xr[0]
-    dn_ref[...] = dn[...] + dl[0]
-    dp_ref[...] = dp[...] + dr[0]
+def relay(nxt, prv, from_left, from_right, nxt_ref, prv_ref):
+    nxt_ref[...] = nxt[...] + from_left[0]
+    prv_ref[...] = prv[...] + from_right[0]
 
 
 def zeros(z, de_ref, first, rows, sem):
@@ -415,23 +416,23 @@
         def move(v, perm):
             return lax.ppermute(v, "tp", perm)
 
-        side = shape((chips, k * h, d), BF16)
-        dm, do = pl.pallas_call(
-            functools.partial(parts, n),
-            out_shape=(side, side), in_specs=[VMEM] * 2, out_specs=(VMEM, VMEM),
-            scratch_shapes=[pltpu.VMEM((kt, f), BF16)],
-            compiler_params=limit(8), cost_estimate=cost(4 << 20), name="parts",
-        )(du, w)
-        dp = move(do, to_partner)
-
         flat = shape((kt // 2, d), BF16)
         xm, xo = pl.pallas_call(
             functools.partial(lookup, n),
             out_shape=(flat, flat), in_specs=[SMEM, HBM], out_specs=(VMEM, VMEM),
-            scratch_shapes=[pltpu.VMEM((kt, 8, d), BF16), pltpu.VMEM((kt, d), F32), smem(kt + 1), smem(kt), smem(kt), dma],
+            scratch_shapes=[pltpu.VMEM((kt, 8, d), BF16), pltpu.VMEM((kt // 8, 8, d), F32), smem(kt + 1), smem(kt), smem(kt), dma],
             compiler_params=limit(32), cost_estimate=cost(16 << 20), name="lookup",
         )(ids, emb.reshape(vl // 8, 8, d))
         xp = move(xo.reshape(chips, k * h, d), to_partner)
+
+        side = shape((chips, k * h, d), BF16)
+        dm, do = pl.pallas_call(
+            functools.partial(parts, n),
+            out_shape=(side, side), in_specs=[VMEM] * 2 + [ANY], out_specs=(VMEM, VMEM),
+            scratch_shapes=[pltpu.VMEM((kt, f), BF16)],
+            compiler_params=limit(8), cost_estimate=cost(4 << 20), name="parts",
+        )(du, w, xm)
+        dp = move(do, to_partner)
 
         def fold_of(a, b, dtype):
             two, one = shape((2, h, d), dtype), shape((h, d), dtype)
@@ -441,41 +442,48 @@
                 compiler_params=limit(8), cost_estimate=cost(2 << 20),
             )(a, b)
 
+        def relay_of(a, b, c, e):
+            one = shape(a.shape, a.dtype)
+            return pl.pallas_call(
+                relay, out_shape=(one, one), in_specs=[VMEM] * 4, out_specs=(VMEM,) * 2,
+                compiler_params=limit(8), cost_estimate=cost(2 << 20),
+            )(a, b, c, e)
+
+        zr = 16
+        unit = vl // 16
+        ends = (4 * unit, 10 * unit)
+        de_shape = shape((vl // 8, 8, d), F32)
+        size = 3 * kt + 128
+
+        def clear_more(de, first, last):
+            return pl.pallas_call(
+                functools.partial(clear_rest, first, last - first),
+                out_shape=de_shape, in_specs=[ANY], out_specs=ANY, input_output_aliases={0: 0},
+                scratch_shapes=[pltpu.VMEM((zr, 8, d), F32), dma],
+                compiler_params=limit(8), cost_estimate=cost((last - first) * d * 4),
+            )(de)
+
+        x_r, x_l, x_n, x_p, x0 = fold_of(xm.reshape(chips, k * h, d), xp, BF16)
+        xl1 = move(x_r, to_right)
+        xr1 = move(x_l, to_left)
         d_r, d_l, d_n, d_p, d0 = fold_of(dm, dp, F32)
-        x_r, x_l, x_n, x_p, x0 = fold_of(xm.reshape(chips, k * h, d), xp, BF16)
         dl1 = move(d_r, to_right)
         dr1 = move(d_l, to_left)
-        xl1 = move(x_r, to_right)
-        xr1 = move(x_l, to_left)
-
-        zr = 16
-        split = (vl * 10 // 16) // (8 * zr) * (8 * zr)
-        de_shape = shape((vl // 8, 8, d), F32)
-        size = 3 * kt + 128
         de, plan = pl.pallas_call(
-            functools.partial(clear_and_list, n, split),
+            functools.partial(clear_and_list, n, ends[0]),
             out_shape=(de_shape, i32(size)), in_specs=[ANY], out_specs=(ANY, ANY),
             scratch_shapes=[pltpu.VMEM((zr, 8, d), F32), smem(k, t), smem(kt + 1), smem(vl // 8), smem(size),
                             dma, dma((2,))],
-            compiler_params=limit(8), cost_estimate=cost(split * d * 4), name="clear0",
+            compiler_params=limit(8), cost_estimate=cost(ends[0] * d * 4), name="clear0",
         )(ids)
-
-        half_x, half_d = shape((h, d), BF16), shape((h, d), F32)
-        x_n, x_p, d_n, d_p = pl.pallas_call(
-            relay, out_shape=(half_x, half_x, half_d, half_d), in_specs=[VMEM] * 8, out_specs=(VMEM,) * 4,
-            compiler_params=limit(8), cost_estimate=cost(2 << 20), name="relay",
-        )(x_n, x_p, xl1, xr1, d_n, d_p, dl1, dr1)
+        x_n, x_p = relay_of(x_n, x_p, xl1, xr1)
+        xl2 = move(x_n, to_right)
+        xr2 = move(x_p, to_left)
+        de = clear_more(de, ends[0], ends[1])
+        d_n, d_p = relay_of(d_n, d_p, dl1, dr1)
         dl2 = move(d_n, to_right)
         dr2 = move(d_p, to_left)
-        xl2 = move(x_n, to_right)
-        xr2 = move(x_p, to_left)
-
-        de = pl.pallas_call(
-            functools.partial(clear_rest, split, vl - split),
-            out_shape=de_shape, in_specs=[ANY], out_specs=ANY, input_output_aliases={0: 0},
-            scratch_shapes=[pltpu.VMEM((zr, 8, d), F32), dma],
-            compiler_params=limit(8), cost_estimate=cost((vl - split) * d * 4), name="clear1",
-        )(de)
+        de = clear_more(de, ends[1], vl)
 
         tok, u_s, dw_s = shape((k, h, d), BF16), shape((k, t, f), BF16), shape((d, f), F32)
         some = kt // 2

time: 96.8 us -> 94.2 us (0.973)
  local copies, waits for them, and re-layouts: 3.1 us -> 0.83 us
    unnamed x14 -> x10, local copies, waits for them, and re-layouts: 3.1 us -> 0.83 us
    pallas_call x1, Pallas kernels: 8.5 us -> 7.11 us  [step(): pl.pallas_call(functools.partial(lookup, n), out_shape=(flat, flat), in_s...]
    pallas_call x3 -> x5, Pallas kernels: 22 us -> 23.1 us  [the longest x2 16.8 us: clear_more(): pl.pallas_call(functools.partial(clear_rest, first, last - first), out_sh...]
  transfers between devices with their start and end apart: 10 -> 10, of which waited for: 1 -> 5; matrix products, arithmetic and copies ran while one was open for 0% -> 0% of each run, Pallas kernels for 32% -> 25%
where the time goes in v6:
time: 94.2 us; the launch traced here: 93.2 us
  Pallas kernels  63.6 us (68%)
  waiting for transfers between devices  14.2 us (15%)
  starting transfers between devices  13.8 us (15%)
    pallas_call x1, Pallas kernels, step(): pl.pallas_call(functools.partial(spread, n), out_shape=(shape((n, k, h, d...  24.4 us
    pallas_call x2, Pallas kernels, clear_more(): pl.pallas_call(functools.partial(clear_rest, first, last - first), out_sh...  16.8 us
    ppermute x10, waiting for transfers between devices, move(): return lax.ppermute(v, 'tp', perm)  14.2 us
    ppermute x10, starting transfers between devices, move(): return lax.ppermute(v, 'tp', perm)  13.8 us
    pallas_call x1, Pallas kernels, step(): pl.pallas_call(functools.partial(lookup, n), out_shape=(flat, flat), in_s...  7.11 us
    pallas_call x1, Pallas kernels, step(): pl.pallas_call(functools.partial(clear_and_list, n, ends[0]), out_shape=(...  6.19 us
    pallas_call x1, Pallas kernels, step(): pl.pallas_call(finish, out_shape=(tok, u_s, dw_s, shape((d,), F32), de_sh...  5.94 us
    pallas_call x1, Pallas kernels, step(): pl.pallas_call(functools.partial(parts, n), out_shape=(side, side), in_sp...  2.69 us
  transfers between devices with their start and end apart: 10, of which 5 were waited for; matrix products, arithmetic and copies ran while one was open for 0% of the time, Pallas kernels for 25%

profile of v6, /device:TPU:112, one launch (start us, length us, event | category | flops | bytes accessed | tf_op | source)
XLA Modules:
  0.0 93.2 jit_solution(8544259564016250909)
XLA Ops:
  0.7 0.8 copy-done.3
  1.5 7.1 %lookup.1 = (bf16[256,2048]{1,0:T(8,128)(2,1)S(1)}, bf16[256,2048]{1,0:T(8,128)(2,1)S(1)}) custom-call(s32[2,256]{1,0:T(2,128)S(1)} %copy-done.3, bf16[1024,8,2048]{2,1,0:T(8,128)(2,1)} %bitcast.6), custom_call_target="tpu_custom_call" | custom-call | bytes 16777216 | tf_op jit(solution)/shard_map/lookup/pallas_call | solution.py:420
  8.6 2.7 %parts.1 = (bf16[4,64,2048]{2,1,0:T(8,128)(2,1)S(1)}, bf16[4,64,2048]{2,1,0:T(8,128)(2,1)S(1)}) custom-call(bf16[2,256,384]{2,1,0:T(8,128)(2,1)S(1)} %copy-done.1, bf16[2048,384]{1,0:T(8,128)(2,1)S(1)} %copy-done, bf16[256,2048]{1,0:T(8,128)(2,1)S(1)} %get-tuple-element.36.after_ref), custom_call_target="tpu_custom_call" | custom-call | bytes 4194304 | tf_op jit(solution)/shard_map/parts/pallas_call | solution.py:429
  11.3 0.1 collective-permute-start.5
  11.4 0.5 collective-permute-start
  11.9 2.1 %collective-permute-done.5.b_ref = bf16[4,64,2048]{2,1,0:T(8,128)(2,1)S(1)} collective-permute-done((bf16[4,64,2048]{2,1,0:T(8,128)(2,1)S(1)}, bf16[4,64,2048]{2,1,0:T(8,128)(2,1)S(1)}, u32[]{:S(2)}, u32[]{:S(2)}) %collective-permute-start.5) | collective-permute-done | bytes 1048608 | tf_op jit(solution)/shard_map/ppermute | solution.py:417
  14.0 0.3 shard_map.103
  14.3 1.7 %collective-permute-start.6 = (f32[2,32,2048]{2,1,0:T(8,128)S(1)}, f32[2,32,2048]{2,1,0:T(8,128)S(1)}, u32[]{:S(2)}, u32[]{:S(2)}) collective-permute-start(f32[2,32,2048]{2,1,0:T(8,128)S(1)} %get-tuple-element.48), channel_id=1, source_target_pairs={{0,2},{1,3},{2,4},{3,5},{4,6},{5,7},{6,0},{7,1},{8,10},{9,11},{10,... | collective-permute-start | bytes 1572872 | tf_op jit(solution)/shard_map/ppermute | solution.py:417
  16.0 1.6 %collective-permute-start.7 = (f32[2,32,2048]{2,1,0:T(8,128)S(1)}, f32[2,32,2048]{2,1,0:T(8,128)S(1)}, u32[]{:S(2)}, u32[]{:S(2)}) collective-permute-start(f32[2,32,2048]{2,1,0:T(8,128)S(1)} %get-tuple-element.49), channel_id=1, source_target_pairs={{0,6},{1,7},{2,0},{3,1},{4,2},{5,3},{6,4},{7,5},{8,14},{9,15},{10,... | collective-permute-start | bytes 1572872 | tf_op jit(solution)/shard_map/ppermute | solution.py:417
  17.6 0.0 collective-permute-done.b_ref
  17.6 0.1 shard_map.101
  17.7 0.5 collective-permute-start.1
  18.2 2.8 %collective-permute-start.2 = (bf16[2,32,2048]{2,1,0:T(8,128)(2,1)S(1)}, bf16[2,32,2048]{2,1,0:T(8,128)(2,1)S(1)}, u32[]{:S(2)}, u32[]{:S(2)}) collective-permute-start(bf16[2,32,2048]{2,1,0:T(8,128)(2,1)S(1)} %get-tuple-element.40), channel_id=1, source_target_pairs={{0,6},{1,7},{2,0},{3,1},{4,2},{5,3},{6,4},{7,5},{8,14},{9,15},{10,... | collective-permute-start | bytes 786440 | tf_op jit(solution)/shard_map/ppermute | solution.py:417
  21.0 9.3 %collective-permute-done.6.from_left.dl1 = f32[2,32,2048]{2,1,0:T(8,128)S(1)} collective-permute-done((f32[2,32,2048]{2,1,0:T(8,128)S(1)}, f32[2,32,2048]{2,1,0:T(8,128)S(1)}, u32[]{:S(2)}, u32[]{:S(2)}) %collective-permute-start.6) | collective-permute-done | bytes 524320 | tf_op jit(solution)/shard_map/ppermute | solution.py:417
  30.4 0.4 collective-permute-done.7.from_right.dr1
  30.8 0.1 shard_map.104
  30.9 1.1 %collective-permute-start.8 = (f32[32,2048]{1,0:T(8,128)S(1)}, f32[32,2048]{1,0:T(8,128)S(1)}, u32[]{:S(2)}, u32[]{:S(2)}) collective-permute-start(f32[32,2048]{1,0:T(8,128)S(1)} %get-tuple-element.52), channel_id=1, source_target_pairs={{0,2},{1,3},{2,4},{3,5},{4,6},{5,7},{6,0},{7,1},{8,10},{9,11},{10,... | collective-permute-start | bytes 786440 | tf_op jit(solution)/shard_map/ppermute | solution.py:417
  31.9 2.2 %collective-permute-start.9 = (f32[32,2048]{1,0:T(8,128)S(1)}, f32[32,2048]{1,0:T(8,128)S(1)}, u32[]{:S(2)}, u32[]{:S(2)}) collective-permute-start(f32[32,2048]{1,0:T(8,128)S(1)} %get-tuple-element.53), channel_id=1, source_target_pairs={{0,6},{1,7},{2,0},{3,1},{4,2},{5,3},{6,4},{7,5},{8,14},{9,15},{10,... | collective-permute-start | bytes 786440 | tf_op jit(solution)/shard_map/ppermute | solution.py:417
  34.2 1.8 %collective-permute-done.1.from_left.xl1 = bf16[2,32,2048]{2,1,0:T(8,128)(2,1)S(1)} collective-permute-done((bf16[2,32,2048]{2,1,0:T(8,128)(2,1)S(1)}, bf16[2,32,2048]{2,1,0:T(8,128)(2,1)S(1)}, u32[]{:S(2)}, u32[]{:S(2)}) %collective-permute-start.1) | collective-permute-done | bytes 262176 | tf_op jit(solution)/shard_map/ppermute | solution.py:417
  36.0 0.4 collective-permute-done.2.from_right.xr1
  36.5 1.1 %collective-permute-start.3 = (bf16[32,2048]{1,0:T(8,128)(2,1)S(1)}, bf16[32,2048]{1,0:T(8,128)(2,1)S(1)}, u32[]{:S(2)}, u32[]{:S(2)}) collective-permute-start(bf16[32,2048]{1,0:T(8,128)(2,1)S(1)} %get-tuple-element.43), channel_id=1, source_target_pairs={{0,2},{1,3},{2,4},{3,5},{4,6},{5,7},{6,0},{7,1},{8,10},{9,11},{10,... | collective-permute-start | bytes 393224 | tf_op jit(solution)/shard_map/ppermute | solution.py:417
  37.5 2.2 %collective-permute-start.4 = (bf16[32,2048]{1,0:T(8,128)(2,1)S(1)}, bf16[32,2048]{1,0:T(8,128)(2,1)S(1)}, u32[]{:S(2)}, u32[]{:S(2)}) collective-permute-start(bf16[32,2048]{1,0:T(8,128)(2,1)S(1)} %get-tuple-element.44), channel_id=1, source_target_pairs={{0,6},{1,7},{2,0},{3,1},{4,2},{5,3},{6,4},{7,5},{8,14},{9,15},{10,... | collective-permute-start | bytes 393224 | tf_op jit(solution)/shard_map/ppermute | solution.py:417
  39.8 6.2 %clear0.1 = (f32[1024,8,2048]{2,1,0:T(8,128)}, s32[1664]{0:T(1024)S(1)}) custom-call(s32[2,256]{1,0:T(2,128)S(1)} %copy-done.3), custom_call_target="tpu_custom_call" | custom-call | bytes 16777216 | tf_op jit(solution)/shard_map/clear0/pallas_call | solution.py:472
  46.0 8.4 %shard_map.105.de_in = f32[1024,8,2048]{2,1,0:T(8,128)} custom-call(f32[1024,8,2048]{2,1,0:T(8,128)} %get-tuple-element.59.de_in), custom_call_target="tpu_custom_call", output_to_operand_aliasing={{}: (0, {})} | custom-call | bytes 25165824 | tf_op jit(solution)/shard_map/pallas_call | solution.py:459
  54.4 0.0 copy-start.2
  54.4 0.0 copy-start.4
  54.4 8.4 %shard_map.106.de_in = f32[1024,8,2048]{2,1,0:T(8,128)} custom-call(f32[1024,8,2048]{2,1,0:T(8,128)} %shard_map.105.de_in), custom_call_target="tpu_custom_call", output_to_operand_aliasing={{}: (0, {})} | custom-call | bytes 25165824 | tf_op jit(solution)/shard_map/pallas_call | solution.py:459
  62.9 0.0 collective-permute-done.3.xl2
  62.9 0.0 collective-permute-done.8.dl2
  62.9 0.0 collective-permute-done.9.dr2
  62.9 24.4 %spread.1 = (bf16[8,2,32,2048]{3,2,1,0:T(8,128)(2,1)S(1)}, bf16[2,32,2048]{2,1,0:T(8,128)(2,1)S(1)}, bf16[2,256,384]{2,1,0:T(8,128)(2,1)S(1)}, f32[2048,384]{1,0:T(8,128)S(1)}, f32[1,2048]{1,0:T(1,128)S(1)}) custom-call(bf16[2,32,2048]{2,1,0:T(8,128)(2,1)S(1)} %get-tuple-element.38.x0, bf16[2,32,2048]{2,1,0:T(8,128)(2,1)S(1)} %collective-permute-done.1.from_left.xl1, ...), custom_call_target="tpu_custom_call" | custom-call | tf_op jit(solution)/shard_map/spread/pallas_call | solution.py:490
  87.3 5.9 %finish.1 = (bf16[2,32,2048]{2,1,0:T(8,128)(2,1)}, bf16[2,256,384]{2,1,0:T(8,128)(2,1)}, f32[2048,384]{1,0:T(8,128)}, f32[2048]{0:T(1024)}, f32[1024,8,2048]{2,1,0:T(8,128)}) custom-call(s32[1664]{0:T(1024)S(1)} %get-tuple-element.35.plan, bf16[8,2,32,2048]{3,2,1,0:T(8,128)(2,1)S(1)} %get-tuple-element.54.dx_all, ...), custom_call_target="tpu_custom_call", output_to_operand_aliasing={{4}: (6, {})} | custom-call | tf_op jit(solution)/shard_map/finish/pallas_call | solution.py:500
  (9 shorter events, 0.0 us)
Async XLA Ops:
  0.6 8.0 %copy-start.1 = (bf16[2,256,384]{2,1,0:T(8,128)(2,1)S(1)}, bf16[2,256,384]{2,1,0:T(8,128)(2,1)}, u32[]{:S(2)}) copy-start(bf16[2,256,384]{2,1,0:T(8,128)(2,1)} %du_ref.3) | copy-start | bytes 1179652
  0.6 8.0 %copy-start = (bf16[2048,384]{1,0:T(8,128)(2,1)S(1)}, bf16[2048,384]{1,0:T(8,128)(2,1)}, u32[]{:S(2)}) copy-start(bf16[2048,384]{1,0:T(8,128)(2,1)} %w_ref.3) | copy-start | bytes 4718596
  0.7 0.8 copy-start.3
  11.3 2.7 %collective-permute-start.5 = (bf16[4,64,2048]{2,1,0:T(8,128)(2,1)S(1)}, bf16[4,64,2048]{2,1,0:T(8,128)(2,1)S(1)}, u32[]{:S(2)}, u32[]{:S(2)}) collective-permute-start(bf16[4,64,2048]{2,1,0:T(8,128)(2,1)S(1)} %get-tuple-element.46), channel_id=1, source_target_pairs={{0,1},{1,0},{2,3},{3,2},{4,5},{5,4},{6,7},{7,6},{8,9},{9,8},{10,11... | collective-permute-start | bytes 3145736 | tf_op jit(solution)/shard_map/ppermute | solution.py:417
  11.4 6.2 %collective-permute-start = (bf16[4,64,2048]{2,1,0:T(8,128)(2,1)S(1)}, bf16[4,64,2048]{2,1,0:T(8,128)(2,1)S(1)}, u32[]{:S(2)}, u32[]{:S(2)}) collective-permute-start(bf16[4,64,2048]{2,1,0:T(8,128)(2,1)S(1)} %bitcast.5), channel_id=1, source_target_pairs={{0,1},{1,0},{2,3},{3,2},{4,5},{5,4},{6,7},{7,6},{8,9},{9,8},{10,11... | collective-permute-start | bytes 3145736 | tf_op jit(solution)/shard_map/ppermute | solution.py:417
  14.3 16.1 %collective-permute-start.6 = (f32[2,32,2048]{2,1,0:T(8,128)S(1)}, f32[2,32,2048]{2,1,0:T(8,128)S(1)}, u32[]{:S(2)}, u32[]{:S(2)}) collective-permute-start(f32[2,32,2048]{2,1,0:T(8,128)S(1)} %get-tuple-element.48), channel_id=1, source_target_pairs={{0,2},{1,3},{2,4},{3,5},{4,6},{5,7},{6,0},{7,1},{8,10},{9,11},{10,... | collective-permute-start | bytes 1572872 | tf_op jit(solution)/shard_map/ppermute | solution.py:417
  16.0 14.8 %collective-permute-start.7 = (f32[2,32,2048]{2,1,0:T(8,128)S(1)}, f32[2,32,2048]{2,1,0:T(8,128)S(1)}, u32[]{:S(2)}, u32[]{:S(2)}) collective-permute-start(f32[2,32,2048]{2,1,0:T(8,128)S(1)} %get-tuple-element.49), channel_id=1, source_target_pairs={{0,6},{1,7},{2,0},{3,1},{4,2},{5,3},{6,4},{7,5},{8,14},{9,15},{10,... | collective-permute-start | bytes 1572872 | tf_op jit(solution)/shard_map/ppermute | solution.py:417
  17.7 18.3 %collective-permute-start.1 = (bf16[2,32,2048]{2,1,0:T(8,128)(2,1)S(1)}, bf16[2,32,2048]{2,1,0:T(8,128)(2,1)S(1)}, u32[]{:S(2)}, u32[]{:S(2)}) collective-permute-start(bf16[2,32,2048]{2,1,0:T(8,128)(2,1)S(1)} %get-tuple-element.39), channel_id=1, source_target_pairs={{0,2},{1,3},{2,4},{3,5},{4,6},{5,7},{6,0},{7,1},{8,10},{9,11},{10,... | collective-permute-start | bytes 786440 | tf_op jit(solution)/shard_map/ppermute | solution.py:417
  18.2 18.2 %collective-permute-start.2 = (bf16[2,32,2048]{2,1,0:T(8,128)(2,1)S(1)}, bf16[2,32,2048]{2,1,0:T(8,128)(2,1)S(1)}, u32[]{:S(2)}, u32[]{:S(2)}) collective-permute-start(bf16[2,32,2048]{2,1,0:T(8,128)(2,1)S(1)} %get-tuple-element.40), channel_id=1, source_target_pairs={{0,6},{1,7},{2,0},{3,1},{4,2},{5,3},{6,4},{7,5},{8,14},{9,15},{10,... | collective-permute-start | bytes 786440 | tf_op jit(solution)/shard_map/ppermute | solution.py:417
  30.9 32.0 %collective-permute-start.8 = (f32[32,2048]{1,0:T(8,128)S(1)}, f32[32,2048]{1,0:T(8,128)S(1)}, u32[]{:S(2)}, u32[]{:S(2)}) collective-permute-start(f32[32,2048]{1,0:T(8,128)S(1)} %get-tuple-element.52), channel_id=1, source_target_pairs={{0,2},{1,3},{2,4},{3,5},{4,6},{5,7},{6,0},{7,1},{8,10},{9,11},{10,... | collective-permute-start | bytes 786440 | tf_op jit(solution)/shard_map/ppermute | solution.py:417
  31.9 30.9 %collective-permute-start.9 = (f32[32,2048]{1,0:T(8,128)S(1)}, f32[32,2048]{1,0:T(8,128)S(1)}, u32[]{:S(2)}, u32[]{:S(2)}) collective-permute-start(f32[32,2048]{1,0:T(8,128)S(1)} %get-tuple-element.53), channel_id=1, source_target_pairs={{0,6},{1,7},{2,0},{3,1},{4,2},{5,3},{6,4},{7,5},{8,14},{9,15},{10,... | collective-permute-start | bytes 786440 | tf_op jit(solution)/shard_map/ppermute | solution.py:417
  36.5 26.4 %collective-permute-start.3 = (bf16[32,2048]{1,0:T(8,128)(2,1)S(1)}, bf16[32,2048]{1,0:T(8,128)(2,1)S(1)}, u32[]{:S(2)}, u32[]{:S(2)}) collective-permute-start(bf16[32,2048]{1,0:T(8,128)(2,1)S(1)} %get-tuple-element.43), channel_id=1, source_target_pairs={{0,2},{1,3},{2,4},{3,5},{4,6},{5,7},{6,0},{7,1},{8,10},{9,11},{10,... | collective-permute-start | bytes 393224 | tf_op jit(solution)/shard_map/ppermute | solution.py:417
  37.5 25.3 %collective-permute-start.4 = (bf16[32,2048]{1,0:T(8,128)(2,1)S(1)}, bf16[32,2048]{1,0:T(8,128)(2,1)S(1)}, u32[]{:S(2)}, u32[]{:S(2)}) collective-permute-start(bf16[32,2048]{1,0:T(8,128)(2,1)S(1)} %get-tuple-element.44), channel_id=1, source_target_pairs={{0,6},{1,7},{2,0},{3,1},{4,2},{5,3},{6,4},{7,5},{8,14},{9,15},{10,... | collective-permute-start | bytes 393224 | tf_op jit(solution)/shard_map/ppermute | solution.py:417
  54.4 8.5 %copy-start.2 = (bf16[2,32,2048]{2,1,0:T(8,128)(2,1)S(1)}, bf16[2,32,2048]{2,1,0:T(8,128)(2,1)}, u32[]{:S(2)}) copy-start(bf16[2,32,2048]{2,1,0:T(8,128)(2,1)} %dres_ref.1) | copy-start | bytes 786436
  54.4 8.5 %copy-start.4 = (bf16[2048]{0:T(1024)(128)(2,1)S(1)}, bf16[2048]{0:T(1024)(128)(2,1)}, u32[]{:S(2)}) copy-start(bf16[2048]{0:T(1024)(128)(2,1)} %g_ref.1) | copy-start | bytes 12292

commit v7 on v6

--- a/solution.py
+++ b/solution.py
@@ -120,24 +120,33 @@
     lax.fori_loop(0, half // ROWS, pack, 0)
 
 
-def fold(h, a_ref, b_ref, right_ref, left_ref, next_ref, prev_ref, own_ref):
-    def put(dst, j, m):
-        rows = pl.ds(m * h, h)
-        dst[...] = a_ref[j, rows].astype(dst.dtype) + b_ref[j, rows].astype(dst.dtype)
-
-    put(right_ref.at[0], 2, 0)
-    put(left_ref.at[0], 2, 1)
-    put(right_ref.at[1], 1, 1)
-    put(left_ref.at[1], 3, 0)
-    put(next_ref, 1, 0)
-    put(prev_ref, 3, 1)
-    put(own_ref.at[0], 0, 0)
-    put(own_ref.at[1], 0, 1)
-
-
-def relay(nxt, prv, from_left, from_right, nxt_ref, prv_ref):
-    nxt_ref[...] = nxt[...] + from_left[0]
-    prv_ref[...] = prv[...] + from_right[0]
+def fold(h, xm, xp, dm, dp, right_ref, left_ref, xn_ref, xv_ref, x0_ref, dn_ref, dv_ref, d0_ref):
+    def x(j, m):
+        return xm[j, m * h:(m + 1) * h] + xp[j, m * h:(m + 1) * h]
+
+    def dn(j, m):
+        return dm[j, m * h:(m + 1) * h].astype(F32) + dp[j, m * h:(m + 1) * h].astype(F32)
+
+    for ref, far, near in ((right_ref, (2, 0), (1, 1)), (left_ref, (2, 1), (3, 0))):
+        for i, (j, m) in enumerate((far, near)):
+            rows = slice(m * h, (m + 1) * h)
+            ref[2 * i] = dm[j, rows]
+            ref[2 * i + 1] = dp[j, rows]
+            ref[4 + i] = x(j, m)
+    xn_ref[...] = x(1, 0)
+    xv_ref[...] = x(3, 1)
+    dn_ref[...] = dn(1, 0)
+    dv_ref[...] = dn(3, 1)
+    for m in range(2):
+        x0_ref[m] = x(0, m)
+        d0_ref[m] = dn(0, m)
+
+
+def relay(xn, xv, dn, dv, fl, fr, xn_ref, xv_ref, dn_ref, dv_ref):
+    dn_ref[...] = dn[...] + fl[0].astype(F32) + fl[1].astype(F32)
+    dv_ref[...] = dv[...] + fr[0].astype(F32) + fr[1].astype(F32)
+    xn_ref[...] = xn[...] + fl[4]
+    xv_ref[...] = xv[...] + fr[4]
 
 
 def zeros(z, de_ref, first, rows, sem):
@@ -203,15 +212,15 @@
         c.wait()
 
 
-def spread(n, x0, xl1, xr1, xl2, xr2, d0, dl1, dr1, dl2, dr2, g_ref, dres_ref, w_ref, du_ref,
+def spread(n, fl, fr, x0, xl2, xr2, d0, dl2, dr2, g_ref, dres_ref, w_ref, du_ref,
            dx_all, x_ref, u_ref, dw_ref, dg_ref, x_all, nh_s, rs_s, dgs, n_g, du_g, s_sem, r_sem, gs_sem, gr_sem):
     me, chip, core, chips = ring_places(n)
     k, h, d = dres_ref.shape
     at = lambda off, c: ((chip + off) % chips) * 2 + c
     left, right, far = at(chips - 1, core), at(1, core), at(2, core)
     partner, p_left, p_right, p_far = at(0, 1 - core), at(chips - 1, 1 - core), at(1, 1 - core), at(2, 1 - core)
-    near = (me, left, right, partner)
-    rest = (far, p_left, p_right, p_far)
+    early = (me, left, right, partner, p_left, p_right)
+    late = (far, p_far)
 
     barrier = pltpu.get_barrier_semaphore()
     for o in range(1, n):
@@ -219,12 +228,12 @@
 
     gf = g_ref[...].astype(F32).reshape(1, d)
     pieces = h // ROWS
-    sides = ((xr1, xl2, dr1, dl2), (xl1, xr2, dl1, dr2))
+    sides = ((fr, xl2, dl2), (fl, xr2, dr2))
     for m in range(k):
-        xa, xb, _, _ = sides[m]
+        one, xb, _ = sides[m]
         for i in range(pieces):
             rows = pl.ds(i * ROWS, ROWS)
-            x = x0[m, rows] + xa[1, rows] + xb[rows]
+            x = x0[m, rows] + one[5, rows] + xb[rows]
             x_ref[m, rows] = x
             x_all[me, m, rows] = x
             xf = x.astype(F32)
@@ -260,13 +269,13 @@
         send(ref.at[left], ref.at[left], s_sem.at[kind, 5], r_sem.at[kind, 3], partner)
         send(ref.at[right], ref.at[right], s_sem.at[kind, 6], r_sem.at[kind, 4], partner)
         got(kind, 0, ref.at[partner])
+        got(kind, 3, ref.at[p_left])
+        got(kind, 4, ref.at[p_right])
 
     def across(kind, ref):
         for m in range(2):
             got(kind, 5 + m, ref.at[far, m])
             send(ref.at[far, m], ref.at[far, m], s_sem.at[kind, 7 + m], r_sem.at[kind, 7 + m], partner)
-        got(kind, 3, ref.at[p_left])
-        got(kind, 4, ref.at[p_right])
 
     def last(kind, ref):
         for m in range(2):
@@ -276,10 +285,10 @@
 
     dg = jnp.zeros((1, d), F32)
     for m in range(k):
-        _, _, da, db = sides[m]
+        one, _, db = sides[m]
         for i in range(pieces):
             rows = pl.ds(i * ROWS, ROWS)
-            dn = d0[m, rows] + da[1, rows] + db[rows]
+            dn = d0[m, rows] + one[2, rows].astype(F32) + one[3, rows].astype(F32) + db[rows]
             nh = nh_s[m, rows]
             dg = dg + jnp.sum(dn * nh, axis=0, keepdims=True)
             gdn = gf * dn
@@ -299,24 +308,25 @@
                     xf = x_all[owner, m, pl.ds(i * ROWS, ROWS)].astype(F32)
                     rs = lax.rsqrt(jnp.mean(xf * xf, axis=-1, keepdims=True) + EPS)
                     n_g[base + i * ROWS:base + (i + 1) * ROWS] = ((xf * rs) * gf).astype(BF16)
-        u = jnp.dot(n_g[...], w_ref[...], preferred_element_type=F32).astype(BF16)
+        size = len(owners) * k * h
+        u = jnp.dot(n_g[:size], w_ref[...], preferred_element_type=F32).astype(BF16)
         for p, owner in enumerate(owners):
             for m in range(k):
                 base = p * (k * h) + m * h
                 u_ref[m, pl.ds(pl.multiple_of(owner * h, h), h)] = u[base:base + h]
         cw = 512
         for i in range(d // cw):
-            v = lax.dot_general(n_g[:, i * cw:(i + 1) * cw], du_g[...], (((0,), (0,)), ((), ())),
+            v = lax.dot_general(n_g[:size, i * cw:(i + 1) * cw], du_g[:size], (((0,), (0,)), ((), ())),
                                 preferred_element_type=F32)
             rows = slice(i * cw, (i + 1) * cw)
             dw_ref[rows] = dw_ref[rows] + v if add else v
 
     onward(0, x_all)
-    project(near, False)
+    project(early, False)
     onward(1, dx_all)
     across(0, x_all)
     last(0, x_all)
-    project(rest, True)
+    project(late, True)
     across(1, dx_all)
     last(1, dx_all)
 
@@ -434,68 +444,54 @@
         )(du, w, xm)
         dp = move(do, to_partner)
 
-        def fold_of(a, b, dtype):
-            two, one = shape((2, h, d), dtype), shape((h, d), dtype)
-            return pl.pallas_call(
-                functools.partial(fold, h),
-                out_shape=(two, two, one, one, two), in_specs=[VMEM] * 2, out_specs=(VMEM,) * 5,
-                compiler_params=limit(8), cost_estimate=cost(2 << 20),
-            )(a, b)
-
-        def relay_of(a, b, c, e):
-            one = shape(a.shape, a.dtype)
-            return pl.pallas_call(
-                relay, out_shape=(one, one), in_specs=[VMEM] * 4, out_specs=(VMEM,) * 2,
-                compiler_params=limit(8), cost_estimate=cost(2 << 20),
-            )(a, b, c, e)
-
         zr = 16
         unit = vl // 16
-        ends = (4 * unit, 10 * unit)
+        split = 13 * unit
         de_shape = shape((vl // 8, 8, d), F32)
         size = 3 * kt + 128
 
-        def clear_more(de, first, last):
-            return pl.pallas_call(
-                functools.partial(clear_rest, first, last - first),
-                out_shape=de_shape, in_specs=[ANY], out_specs=ANY, input_output_aliases={0: 0},
-                scratch_shapes=[pltpu.VMEM((zr, 8, d), F32), dma],
-                compiler_params=limit(8), cost_estimate=cost((last - first) * d * 4),
-            )(de)
-
-        x_r, x_l, x_n, x_p, x0 = fold_of(xm.reshape(chips, k * h, d), xp, BF16)
-        xl1 = move(x_r, to_right)
-        xr1 = move(x_l, to_left)
-        d_r, d_l, d_n, d_p, d0 = fold_of(dm, dp, F32)
-        dl1 = move(d_r, to_right)
-        dr1 = move(d_l, to_left)
+        chunk, half_x, half_d = shape((6, h, d), BF16), shape((h, d), BF16), shape((h, d), F32)
+        to_r, to_l, x_n, x_v, x0, d_n, d_v, d0 = pl.pallas_call(
+            functools.partial(fold, h),
+            out_shape=(chunk, chunk, half_x, half_x, shape((2, h, d), BF16), half_d, half_d, shape((2, h, d), F32)),
+            in_specs=[VMEM] * 4, out_specs=(VMEM,) * 8,
+            compiler_params=limit(8), cost_estimate=cost(4 << 20), name="fold",
+        )(xm.reshape(chips, k * h, d), xp, dm, dp)
+        fl = move(to_r, to_right)
+        fr = move(to_l, to_left)
         de, plan = pl.pallas_call(
-            functools.partial(clear_and_list, n, ends[0]),
+            functools.partial(clear_and_list, n, split),
             out_shape=(de_shape, i32(size)), in_specs=[ANY], out_specs=(ANY, ANY),
             scratch_shapes=[pltpu.VMEM((zr, 8, d), F32), smem(k, t), smem(kt + 1), smem(vl // 8), smem(size),
                             dma, dma((2,))],
-            compiler_params=limit(8), cost_estimate=cost(ends[0] * d * 4), name="clear0",
+            compiler_params=limit(8), cost_estimate=cost(split * d * 4), name="clear0",
         )(ids)
-        x_n, x_p = relay_of(x_n, x_p, xl1, xr1)
+        x_n, x_v, d_n, d_v = pl.pallas_call(
+            relay, out_shape=(half_x, half_x, half_d, half_d), in_specs=[VMEM] * 6, out_specs=(VMEM,) * 4,
+            compiler_params=limit(8), cost_estimate=cost(2 << 20), name="relay",
+        )(x_n, x_v, d_n, d_v, fl, fr)
+        dl2 = move(d_n, to_right)
+        dr2 = move(d_v, to_left)
         xl2 = move(x_n, to_right)
-        xr2 = move(x_p, to_left)
-        de = clear_more(de, ends[0], ends[1])
-        d_n, d_p = relay_of(d_n, d_p, dl1, dr1)
-        dl2 = move(d_n, to_right)
-        dr2 = move(d_p, to_left)
-        de = clear_more(de, ends[1], vl)
+        xr2 = move(x_v, to_left)
+        de = pl.pallas_call(
+            functools.partial(clear_rest, split, vl - split),
+            out_shape=de_shape, in_specs=[ANY], out_specs=ANY, input_output_aliases={0: 0},
+            scratch_shapes=[pltpu.VMEM((zr, 8, d), F32), dma],
+            compiler_params=limit(8), cost_estimate=cost((vl - split) * d * 4), name="clear1",
+        )(de)
 
         tok, u_s, dw_s = shape((k, h, d), BF16), shape((k, t, f), BF16), shape((d, f), F32)
-        some = kt // 2
+        some = 6 * k * h
         dx_all, x, u, dw, dg = pl.pallas_call(
             functools.partial(spread, n),
             out_shape=(shape((n, k, h, d), BF16), tok, u_s, dw_s, shape((1, d), F32)),
-            in_specs=[VMEM] * 14, out_specs=(VMEM,) * 5,
+            in_specs=[VMEM] * 12, out_specs=(VMEM,) * 5,
             scratch_shapes=[pltpu.VMEM((n, k, h, d), BF16), pltpu.VMEM((k, h, d), F32), pltpu.VMEM((k, h, 128), F32),
                             pltpu.VMEM((n, 1, d), F32), pltpu.VMEM((some, d), BF16), pltpu.VMEM((some, f), BF16),
                             dma((2, 9)), dma((2, 9)), dma((n,)), dma((n,))],
             compiler_params=limit(24, collective_id=0, has_side_effects=True), name="spread",
-        )(x0, xl1, xr1, xl2, xr2, d0, dl1, dr1, dl2, dr2, g, dres, w, du)
+        )(fl, fr, x0, xl2, xr2, d0, dl2, dr2, g, dres, w, du)
 
         x, u, dw, dg, de = pl.pallas_call(
             finish,

time: 94.2 us -> 95 us (level)
  waiting for transfers between devices: 14.2 us -> 20.2 us
  starting transfers between devices: 13.8 us -> 10.5 us
  Pallas kernels: 63.6 us -> 61.8 us
    ppermute x10 -> x8, waiting for transfers between devices: 14.2 us -> 20.2 us  [move(): return lax.ppermute(v, 'tp', perm)]
    ppermute x10 -> x8, starting transfers between devices: 13.8 us -> 10.5 us  [move(): return lax.ppermute(v, 'tp', perm)]
    pallas_call x7 -> x4, Pallas kernels: 23.5 us -> 22.3 us  [the longest x1 17.3 us: step(): pl.pallas_call(functools.partial(clear_and_list, n, split), out_shape=(de...]
  transfers between devices with their start and end apart: 10 -> 8, of which waited for: 5 -> 3; matrix products, arithmetic and copies ran while one was open for 0% -> 0% of each run, Pallas kernels for 25% -> 26%
where the time goes in v7:
time: 95 us; the launch traced here: 94.1 us
  Pallas kernels  61.8 us (65%)
  waiting for transfers between devices  20.2 us (21%)
  starting transfers between devices  10.5 us (11%)
    pallas_call x1, Pallas kernels, step(): pl.pallas_call(functools.partial(spread, n), out_shape=(shape((n, k, h, d...  23.8 us
    ppermute x8, waiting for transfers between devices, move(): return lax.ppermute(v, 'tp', perm)  20.2 us
    pallas_call x1, Pallas kernels, step(): pl.pallas_call(functools.partial(clear_and_list, n, split), out_shape=(de...  17.3 us
    ppermute x8, starting transfers between devices, move(): return lax.ppermute(v, 'tp', perm)  10.5 us
    pallas_call x1, Pallas kernels, step(): pl.pallas_call(functools.partial(lookup, n), out_shape=(flat, flat), in_s...  7.11 us
    pallas_call x1, Pallas kernels, step(): pl.pallas_call(finish, out_shape=(tok, u_s, dw_s, shape((d,), F32), de_sh...  5.94 us
    pallas_call x1, Pallas kernels, step(): pl.pallas_call(functools.partial(clear_rest, split, vl - split), out_shap...  4.63 us
    pallas_call x1, Pallas kernels, step(): pl.pallas_call(functools.partial(parts, n), out_shape=(side, side), in_sp...  2.69 us
  transfers between devices with their start and end apart: 8, of which 3 were waited for; matrix products, arithmetic and copies ran while one was open for 0% of the time, Pallas kernels for 26%

profile of v7, /device:TPU:112, one launch (start us, length us, event | category | flops | bytes accessed | tf_op | source)
XLA Modules:
  0.0 94.1 jit_solution(13023178476021027120)
XLA Ops:
  0.6 0.0 copy-start.1
  0.6 0.0 copy-start
  0.7 0.0 copy-start.3
  0.7 0.8 copy-done.3
  1.5 7.1 %lookup.1 = (bf16[256,2048]{1,0:T(8,128)(2,1)S(1)}, bf16[256,2048]{1,0:T(8,128)(2,1)S(1)}) custom-call(s32[2,256]{1,0:T(2,128)S(1)} %copy-done.3, bf16[1024,8,2048]{2,1,0:T(8,128)(2,1)} %bitcast.6), custom_call_target="tpu_custom_call" | custom-call | bytes 16777216 | tf_op jit(solution)/shard_map/lookup/pallas_call | solution.py:430
  8.6 0.1 collective-permute-start
  8.7 0.0 copy-done.1
  8.7 0.0 copy-done
  8.7 2.7 %parts.1 = (bf16[4,64,2048]{2,1,0:T(8,128)(2,1)S(1)}, bf16[4,64,2048]{2,1,0:T(8,128)(2,1)S(1)}) custom-call(bf16[2,256,384]{2,1,0:T(8,128)(2,1)S(1)} %copy-done.1, bf16[2048,384]{1,0:T(8,128)(2,1)S(1)} %copy-done, bf16[256,2048]{1,0:T(8,128)(2,1)S(1)} %get-tuple-element.34.after_ref), custom_call_target="tpu_custom_call" | custom-call | bytes 4194304 | tf_op jit(solution)/shard_map/parts/pallas_call | solution.py:439
  11.4 0.5 collective-permute-start.1
  11.9 0.0 collective-permute-done.xp
  11.9 2.3 %collective-permute-done.1.dp = bf16[4,64,2048]{2,1,0:T(8,128)(2,1)S(1)} collective-permute-done((bf16[4,64,2048]{2,1,0:T(8,128)(2,1)S(1)}, bf16[4,64,2048]{2,1,0:T(8,128)(2,1)S(1)}, u32[]{:S(2)}, u32[]{:S(2)}) %collective-permute-start.1) | collective-permute-done | bytes 1048608 | tf_op jit(solution)/shard_map/ppermute | solution.py:427
  14.2 0.3 fold.1
  14.5 1.7 %collective-permute-start.2 = (bf16[6,32,2048]{2,1,0:T(8,128)(2,1)S(1)}, bf16[6,32,2048]{2,1,0:T(8,128)(2,1)S(1)}, u32[]{:S(2)}, u32[]{:S(2)}) collective-permute-start(bf16[6,32,2048]{2,1,0:T(8,128)(2,1)S(1)} %get-tuple-element.38), channel_id=1, source_target_pairs={{0,2},{1,3},{2,4},{3,5},{4,6},{5,7},{6,0},{7,1},{8,10},{9,11},{10,... | collective-permute-start | bytes 2359304 | tf_op jit(solution)/shard_map/ppermute | solution.py:427
  16.2 1.6 %collective-permute-start.3 = (bf16[6,32,2048]{2,1,0:T(8,128)(2,1)S(1)}, bf16[6,32,2048]{2,1,0:T(8,128)(2,1)S(1)}, u32[]{:S(2)}, u32[]{:S(2)}) collective-permute-start(bf16[6,32,2048]{2,1,0:T(8,128)(2,1)S(1)} %get-tuple-element.39), channel_id=1, source_target_pairs={{0,6},{1,7},{2,0},{3,1},{4,2},{5,3},{6,4},{7,5},{8,14},{9,15},{10,... | collective-permute-start | bytes 2359304 | tf_op jit(solution)/shard_map/ppermute | solution.py:427
  17.8 17.8 %collective-permute-done.2.fl = bf16[6,32,2048]{2,1,0:T(8,128)(2,1)S(1)} collective-permute-done((bf16[6,32,2048]{2,1,0:T(8,128)(2,1)S(1)}, bf16[6,32,2048]{2,1,0:T(8,128)(2,1)S(1)}, u32[]{:S(2)}, u32[]{:S(2)}) %collective-permute-start.2) | collective-permute-done | bytes 786464 | tf_op jit(solution)/shard_map/ppermute | solution.py:427
  35.6 0.1 collective-permute-done.3.fr
  35.7 0.1 relay.1
  35.8 1.1 %collective-permute-start.6 = (f32[32,2048]{1,0:T(8,128)S(1)}, f32[32,2048]{1,0:T(8,128)S(1)}, u32[]{:S(2)}, u32[]{:S(2)}) collective-permute-start(f32[32,2048]{1,0:T(8,128)S(1)} %get-tuple-element.48), channel_id=1, source_target_pairs={{0,2},{1,3},{2,4},{3,5},{4,6},{5,7},{6,0},{7,1},{8,10},{9,11},{10,... | collective-permute-start | bytes 786440 | tf_op jit(solution)/shard_map/ppermute | solution.py:427
  36.9 2.2 %collective-permute-start.7 = (f32[32,2048]{1,0:T(8,128)S(1)}, f32[32,2048]{1,0:T(8,128)S(1)}, u32[]{:S(2)}, u32[]{:S(2)}) collective-permute-start(f32[32,2048]{1,0:T(8,128)S(1)} %get-tuple-element.49), channel_id=1, source_target_pairs={{0,6},{1,7},{2,0},{3,1},{4,2},{5,3},{6,4},{7,5},{8,14},{9,15},{10,... | collective-permute-start | bytes 786440 | tf_op jit(solution)/shard_map/ppermute | solution.py:427
  39.1 0.0 collective-permute-start.4
  39.1 3.2 %collective-permute-start.5 = (bf16[32,2048]{1,0:T(8,128)(2,1)S(1)}, bf16[32,2048]{1,0:T(8,128)(2,1)S(1)}, u32[]{:S(2)}, u32[]{:S(2)}) collective-permute-start(bf16[32,2048]{1,0:T(8,128)(2,1)S(1)} %get-tuple-element.46), channel_id=1, source_target_pairs={{0,6},{1,7},{2,0},{3,1},{4,2},{5,3},{6,4},{7,5},{8,14},{9,15},{10,... | collective-permute-start | bytes 393224 | tf_op jit(solution)/shard_map/ppermute | solution.py:427
  42.4 17.3 %clear0.1 = (f32[1024,8,2048]{2,1,0:T(8,128)}, s32[1664]{0:T(1024)S(1)}) custom-call(s32[2,256]{1,0:T(2,128)S(1)} %copy-done.3), custom_call_target="tpu_custom_call" | custom-call | bytes 54525952 | tf_op jit(solution)/shard_map/clear0/pallas_call | solution.py:462
  59.6 0.0 copy-start.2
  59.7 0.0 copy-start.4
  59.7 4.6 %clear1.1.de_in = f32[1024,8,2048]{2,1,0:T(8,128)} custom-call(f32[1024,8,2048]{2,1,0:T(8,128)} %get-tuple-element.55.de_in), custom_call_target="tpu_custom_call", output_to_operand_aliasing={{}: (0, {})} | custom-call | bytes 12582912 | tf_op jit(solution)/shard_map/clear1/pallas_call | solution.py:477
  64.3 0.0 collective-permute-done.4.xl2
  64.3 0.0 collective-permute-done.5.xr2
  64.3 0.0 collective-permute-done.6.dl2
  64.3 0.0 collective-permute-done.7.dr2
  64.4 23.8 %spread.1 = (bf16[8,2,32,2048]{3,2,1,0:T(8,128)(2,1)S(1)}, bf16[2,32,2048]{2,1,0:T(8,128)(2,1)S(1)}, bf16[2,256,384]{2,1,0:T(8,128)(2,1)S(1)}, f32[2048,384]{1,0:T(8,128)S(1)}, f32[1,2048]{1,0:T(1,128)S(1)}) custom-call(bf16[6,32,2048]{2,1,0:T(8,128)(2,1)S(1)} %collective-permute-done.2.fl, bf16[6,32,2048]{2,1,0:T(8,128)(2,1)S(1)} %collective-permute-done.3.fr, ...), custom_call_target="tpu_custom_call" | custom-call | tf_op jit(solution)/shard_map/spread/pallas_call | solution.py:486
  88.2 5.9 %finish.1 = (bf16[2,32,2048]{2,1,0:T(8,128)(2,1)}, bf16[2,256,384]{2,1,0:T(8,128)(2,1)}, f32[2048,384]{1,0:T(8,128)}, f32[2048]{0:T(1024)}, f32[1024,8,2048]{2,1,0:T(8,128)}) custom-call(s32[1664]{0:T(1024)S(1)} %get-tuple-element.33.plan, bf16[8,2,32,2048]{3,2,1,0:T(8,128)(2,1)S(1)} %get-tuple-element.50.dx_all, ...), custom_call_target="tpu_custom_call", output_to_operand_aliasing={{4}: (6, {})} | custom-call | tf_op jit(solution)/shard_map/finish/pallas_call | solution.py:496
  (2 shorter events, 0.0 us)
Async XLA Ops:
  0.6 8.1 %copy-start.1 = (bf16[2,256,384]{2,1,0:T(8,128)(2,1)S(1)}, bf16[2,256,384]{2,1,0:T(8,128)(2,1)}, u32[]{:S(2)}) copy-start(bf16[2,256,384]{2,1,0:T(8,128)(2,1)} %du_ref.3) | copy-start | bytes 1179652
  0.6 8.1 %copy-start = (bf16[2048,384]{1,0:T(8,128)(2,1)S(1)}, bf16[2048,384]{1,0:T(8,128)(2,1)}, u32[]{:S(2)}) copy-start(bf16[2048,384]{1,0:T(8,128)(2,1)} %w_ref.3) | copy-start | bytes 4718596
  0.7 0.8 copy-start.3
  8.6 3.3 %collective-permute-start = (bf16[4,64,2048]{2,1,0:T(8,128)(2,1)S(1)}, bf16[4,64,2048]{2,1,0:T(8,128)(2,1)S(1)}, u32[]{:S(2)}, u32[]{:S(2)}) collective-permute-start(bf16[4,64,2048]{2,1,0:T(8,128)(2,1)S(1)} %bitcast.5), channel_id=1, source_target_pairs={{0,1},{1,0},{2,3},{3,2},{4,5},{5,4},{6,7},{7,6},{8,9},{9,8},{10,11... | collective-permute-start | bytes 3145736 | tf_op jit(solution)/shard_map/ppermute | solution.py:427
  11.4 2.8 %collective-permute-start.1 = (bf16[4,64,2048]{2,1,0:T(8,128)(2,1)S(1)}, bf16[4,64,2048]{2,1,0:T(8,128)(2,1)S(1)}, u32[]{:S(2)}, u32[]{:S(2)}) collective-permute-start(bf16[4,64,2048]{2,1,0:T(8,128)(2,1)S(1)} %get-tuple-element.37), channel_id=1, source_target_pairs={{0,1},{1,0},{2,3},{3,2},{4,5},{5,4},{6,7},{7,6},{8,9},{9,8},{10,11... | collective-permute-start | bytes 3145736 | tf_op jit(solution)/shard_map/ppermute | solution.py:427
  14.5 21.1 %collective-permute-start.2 = (bf16[6,32,2048]{2,1,0:T(8,128)(2,1)S(1)}, bf16[6,32,2048]{2,1,0:T(8,128)(2,1)S(1)}, u32[]{:S(2)}, u32[]{:S(2)}) collective-permute-start(bf16[6,32,2048]{2,1,0:T(8,128)(2,1)S(1)} %get-tuple-element.38), channel_id=1, source_target_pairs={{0,2},{1,3},{2,4},{3,5},{4,6},{5,7},{6,0},{7,1},{8,10},{9,11},{10,... | collective-permute-start | bytes 2359304 | tf_op jit(solution)/shard_map/ppermute | solution.py:427
  16.2 19.5 %collective-permute-start.3 = (bf16[6,32,2048]{2,1,0:T(8,128)(2,1)S(1)}, bf16[6,32,2048]{2,1,0:T(8,128)(2,1)S(1)}, u32[]{:S(2)}, u32[]{:S(2)}) collective-permute-start(bf16[6,32,2048]{2,1,0:T(8,128)(2,1)S(1)} %get-tuple-element.39), channel_id=1, source_target_pairs={{0,6},{1,7},{2,0},{3,1},{4,2},{5,3},{6,4},{7,5},{8,14},{9,15},{10,... | collective-permute-start | bytes 2359304 | tf_op jit(solution)/shard_map/ppermute | solution.py:427
  35.8 28.5 %collective-permute-start.6 = (f32[32,2048]{1,0:T(8,128)S(1)}, f32[32,2048]{1,0:T(8,128)S(1)}, u32[]{:S(2)}, u32[]{:S(2)}) collective-permute-start(f32[32,2048]{1,0:T(8,128)S(1)} %get-tuple-element.48), channel_id=1, source_target_pairs={{0,2},{1,3},{2,4},{3,5},{4,6},{5,7},{6,0},{7,1},{8,10},{9,11},{10,... | collective-permute-start | bytes 786440 | tf_op jit(solution)/shard_map/ppermute | solution.py:427
  36.9 27.4 %collective-permute-start.7 = (f32[32,2048]{1,0:T(8,128)S(1)}, f32[32,2048]{1,0:T(8,128)S(1)}, u32[]{:S(2)}, u32[]{:S(2)}) collective-permute-start(f32[32,2048]{1,0:T(8,128)S(1)} %get-tuple-element.49), channel_id=1, source_target_pairs={{0,6},{1,7},{2,0},{3,1},{4,2},{5,3},{6,4},{7,5},{8,14},{9,15},{10,... | collective-permute-start | bytes 786440 | tf_op jit(solution)/shard_map/ppermute | solution.py:427
  39.1 25.2 %collective-permute-start.4 = (bf16[32,2048]{1,0:T(8,128)(2,1)S(1)}, bf16[32,2048]{1,0:T(8,128)(2,1)S(1)}, u32[]{:S(2)}, u32[]{:S(2)}) collective-permute-start(bf16[32,2048]{1,0:T(8,128)(2,1)S(1)} %get-tuple-element.45), channel_id=1, source_target_pairs={{0,2},{1,3},{2,4},{3,5},{4,6},{5,7},{6,0},{7,1},{8,10},{9,11},{10,... | collective-permute-start | bytes 393224 | tf_op jit(solution)/shard_map/ppermute | solution.py:427
  39.1 25.2 %collective-permute-start.5 = (bf16[32,2048]{1,0:T(8,128)(2,1)S(1)}, bf16[32,2048]{1,0:T(8,128)(2,1)S(1)}, u32[]{:S(2)}, u32[]{:S(2)}) collective-permute-start(bf16[32,2048]{1,0:T(8,128)(2,1)S(1)} %get-tuple-element.46), channel_id=1, source_target_pairs={{0,6},{1,7},{2,0},{3,1},{4,2},{5,3},{6,4},{7,5},{8,14},{9,15},{10,... | collective-permute-start | bytes 393224 | tf_op jit(solution)/shard_map/ppermute | solution.py:427
  59.6 4.7 %copy-start.2 = (bf16[2,32,2048]{2,1,0:T(8,128)(2,1)S(1)}, bf16[2,32,2048]{2,1,0:T(8,128)(2,1)}, u32[]{:S(2)}) copy-start(bf16[2,32,2048]{2,1,0:T(8,128)(2,1)} %dres_ref.1) | copy-start | bytes 786436
  59.7 4.7 %copy-start.4 = (bf16[2048]{0:T(1024)(128)(2,1)S(1)}, bf16[2048]{0:T(1024)(128)(2,1)}, u32[]{:S(2)}) copy-start(bf16[2048]{0:T(1024)(128)(2,1)} %g_ref.1) | copy-start | bytes 12292
